TPU v7x, 1024 devices: a whole 4x4x32 slice. The times are simulated.
1024 devices in a mesh: gx: 8 (over z_lo), gy: 16 (over y, z_hi), gz: 8 (over x, core).
Axes of the slice: x: 4, y: 4, z: 32 (z_hi: 4, z_lo: 8; z = z_hi * 8 + z_lo), core: 2. Of those that a mesh axis runs over, the one named last changes fastest.
Arguments:
- cell_index: int32 [8, 16, 8, 8192], P('gx', 'gy', 'gz'), may hold values from 2471 to 301728, as said below
- offsets: float32 [8, 16, 8, 3, 8192], P('gx', 'gy', 'gz'), may hold values from -0.5 to 0.5
- mass: float32 [8, 16, 8, 8192], P('gx', 'gy', 'gz'), may hold values from 0.5 to 2
- counts: int32 [8, 16, 8], P('gx', 'gy', 'gz'), may hold values from 2048 to 8192, as said below
Outputs:
- density: float32 [1024, 8, 32, 1024], P(None, 'gx', 'gy', 'gz')
- spectrum: float32 [2, 512, 8, 32, 1024], P(None, None, 'gx', 'gy', 'gz')
Inputs may be any that keep to these rules, and one draw needn't show every extreme that they name: `cell_index`: each entry is (i + 1) * 18 * 130 + (j + 1) * 130 + k + 1 for a cell (i, j, k) with 0 <= i < 128, 0 <= j < 16, 0 <= k < 128; slots past a block's count hold such indices too. `counts`: some block is full in every draw.
All inputs are finite; a program needn't handle non-finite values.
Results may differ from a plain program's by a relative error of at most 0.0003.
Values sent between devices are 32-bit elements; how exact they have to be, the bound alone decides.
No kernel may reach another device: no remote copies, remote signals or barrier semaphores. Data moves between devices by JAX's collectives and lax.ppermute only.
A program may use at most 32 MiB of HBM per device.

v0:
```python
import math

import jax
import jax.numpy as jnp
from jax import lax
from jax.sharding import PartitionSpec as P

CX = 128
YP = 2
CZ = 128


def with_halo(cells, sides, width):
    for axis, dim in sides:
        count = lax.axis_size(axis)
        head = lax.slice_in_dim(cells, 0, width, axis=dim)
        tail = lax.slice_in_dim(cells, cells.shape[dim] - width, cells.shape[dim], axis=dim)
        cells = jnp.concatenate(
            [
                lax.ppermute(tail, axis, [(i, (i + 1) % count) for i in range(count)]),
                cells,
                lax.ppermute(head, axis, [((i + 1) % count, i) for i in range(count)]),
            ],
            axis=dim,
        )
    return cells


def collapse(extended, axis_dim):
    inner_len = extended.shape[axis_dim] - 4
    core_part = lax.slice_in_dim(extended, 2, inner_len + 2, axis=axis_dim)
    low_ghost = lax.slice_in_dim(extended, 0, 1, axis=axis_dim)
    high_ghost = lax.slice_in_dim(extended, inner_len + 3, inner_len + 4, axis=axis_dim)
    first_row = lax.slice_in_dim(core_part, 0, 1, axis=axis_dim) + low_ghost
    middle = lax.slice_in_dim(core_part, 1, inner_len - 1, axis=axis_dim)
    last_row = lax.slice_in_dim(core_part, inner_len - 1, inner_len, axis=axis_dim) + high_ghost
    return jnp.concatenate([first_row, middle, last_row], axis=axis_dim)


def dft_tables(count_out, count_in, period):
    rows_out = lax.iota(jnp.int32, count_out)
    rows_in = lax.iota(jnp.int32, count_in)
    phase = (rows_out[:, None] * rows_in[None, :] % period).astype(jnp.float32)
    angle = phase * jnp.float32(2.0 * math.pi / period)
    return (jnp.cos(angle), jnp.sin(angle))


def body(cell_index, offsets, mass, counts):
    groups = lax.axis_size("gx")
    width_y = YP * groups
    depth_z = CZ
    stride_y = depth_z + 2
    stride_x = (width_y + 2) * stride_y
    strides = (stride_x, stride_y, 1)
    cell_flat = cell_index.reshape(-1)
    offset_rows = offsets.reshape(3, -1)
    mass_flat = mass.reshape(-1)
    live_count = counts.reshape(())
    slot_total = cell_flat.shape[0]
    tile_rows = min(8192, slot_total)

    def paint(turn, painted):
        start = turn * tile_rows
        slot_ids = start + lax.iota(jnp.int32, tile_rows)
        loaded = jnp.where(slot_ids < live_count, mass_flat, jnp.float32(0.0))
        step_sizes = [
            jnp.where(offset_rows[axis_pos] >= 0.0, strides[axis_pos], -strides[axis_pos])
            for axis_pos in range(3)
        ]
        targets = []
        weights = []
        for corner in range(8):
            target = cell_flat
            factor = None
            for axis_pos in range(3):
                upper_bit = corner >> 2 - axis_pos & 1
                magnitude = jnp.abs(offset_rows[axis_pos])
                if upper_bit:
                    target = target + step_sizes[axis_pos]
                    factor_one = magnitude
                else:
                    factor_one = 1.0 - magnitude
                factor = factor_one if factor is None else factor * factor_one
            targets.append(target)
            weights.append(factor * loaded)
        return painted.at[jnp.stack(targets)].add(jnp.stack(weights))

    turn_count = slot_total // tile_rows
    painted = lax.fori_loop(0, turn_count, paint, jnp.zeros(((CX + 2) * stride_x,), jnp.float32))
    block = painted.reshape(CX + 2, width_y + 2, depth_z + 2)
    extended = with_halo(block, (("gy", 1), ("gz", 2)), 1)
    folded = collapse(collapse(extended, 1), 2)
    pencil = lax.all_to_all(folded, "gx", split_axis=1, concat_axis=0, tiled=True)
    stacked = pencil.reshape(groups, CX + 2, YP, depth_z)
    core_part = stacked[:, 1 : CX + 1]
    low_ghost = jnp.roll(stacked[:, 0], -1, axis=0)
    high_ghost = jnp.roll(stacked[:, CX + 1], 1, axis=0)
    core_part = core_part.at[:, 0].add(high_ghost).at[:, CX - 1].add(low_ghost)
    density = core_part.reshape(groups * CX, YP, depth_z)
    length = groups * CX
    power = length.bit_length() - 1
    split_b = 2 ** (power // 2)
    split_a = length // split_b
    highest = lax.Precision.HIGHEST
    cos_b, sin_b = dft_tables(split_b, split_b, split_b)
    columns = density.reshape(split_b, split_a, YP * depth_z)
    first_real = jnp.einsum("kb,bar->kar", cos_b, columns, precision=highest)
    first_imag = -jnp.einsum("kb,bar->kar", sin_b, columns, precision=highest)
    twist_cos, twist_sin = dft_tables(split_b, split_a, length)
    twist_cos = twist_cos[:, :, None]
    twist_sin = twist_sin[:, :, None]
    turned_real = first_real * twist_cos + first_imag * twist_sin
    turned_imag = first_imag * twist_cos - first_real * twist_sin
    cos_a, sin_a = dft_tables(split_a // 2, split_a, split_a)
    final_real = jnp.einsum("ja,kar->jkr", cos_a, turned_real, precision=highest) + jnp.einsum(
        "ja,kar->jkr", sin_a, turned_imag, precision=highest
    )
    final_imag = jnp.einsum("ja,kar->jkr", cos_a, turned_imag, precision=highest) - jnp.einsum(
        "ja,kar->jkr", sin_a, turned_real, precision=highest
    )
    scale = 1.0 / math.sqrt(length)
    spectrum = jnp.stack([final_real, final_imag]) * scale
    spectrum = spectrum.reshape(2, length // 2, 1, YP, depth_z)
    return (density.reshape(length, 1, YP, depth_z), spectrum)


def solution(mesh):
    placed = (
        P("gx", "gy", "gz", None),
        P("gx", "gy", "gz", None, None),
        P("gx", "gy", "gz", None),
        P("gx", "gy", "gz"),
    )
    return jax.shard_map(
        body,
        mesh=mesh,
        in_specs=placed,
        out_specs=(P(None, "gx", "gy", "gz"), P(None, None, "gx", "gy", "gz")),
        check_vma=False,
    )
```

profile of v0, /device:TPU:1, one launch (start us, length us, event | category | flops | bytes accessed | tf_op | source)
XLA Modules:
  0.0 504.7 jit_solution(13105103944264208127)
XLA Ops:
  1.3 1.0 fusion.18
  2.3 1.0 fusion.19
  3.3 0.4 stack.72
  4.3 0.3 compare_select_fusion
  4.6 342.4 %scatter_custom_fusion = f32[304200]{0:T(1024)} fusion(s32[65536]{0:T(1024)S(1)} %bitcast.195, f32[65536]{0:T(1024)S(1)} %bitcast.194, f32[]{:T(128)} %constant.112.clone.1), kind=kCustom, calls=%fused_computation.24 | custom fusion | flops 65536 | bytes 1216804 | tf_op jit(solution)/shard_map/while/body/eval_jaxpr/scatter-add | solution.py:86
  347.0 2.8 reshape.966
  349.9 0.2 fusion.84
  350.1 16.3 %collective-permute-start = (f32[130,1,130]{2,1,0:T(1,128)S(1)}, f32[130,1,130]{2,1,0:T(1,128)S(1)}, u32[]{:S(2)}, u32[]{:S(2)}) collective-permute-start(f32[130,1,130]{2,1,0:T(1,128)S(1)} %get-tuple-element.60), channel_id=1, source_target_pairs={{0,8},{8,16},{16,24},{24,32},{32,40},{40,48},{48,56},{56,64},{64,7... | collective-permute-start | bytes 202808 | tf_op jit(solution)/shard_map/ppermute | solution.py:20
  366.3 11.8 %collective-permute-start.1 = (f32[130,1,130]{2,1,0:T(1,128)S(1)}, f32[130,1,130]{2,1,0:T(1,128)S(1)}, u32[]{:S(2)}, u32[]{:S(2)}) collective-permute-start(f32[130,1,130]{2,1,0:T(1,128)S(1)} %get-tuple-element.61), channel_id=1, source_target_pairs={{8,0},{16,8},{24,16},{32,24},{40,32},{48,40},{56,48},{64,56},{72,6... | collective-permute-start | bytes 202808 | tf_op jit(solution)/shard_map/ppermute | solution.py:22
  378.2 1.0 collective-permute-done
  379.2 24.9 %collective-permute-done.1 = f32[130,1,130]{2,1,0:T(1,128)S(1)} collective-permute-done((f32[130,1,130]{2,1,0:T(1,128)S(1)}, f32[130,1,130]{2,1,0:T(1,128)S(1)}, u32[]{:S(2)}, u32[]{:S(2)}) %collective-permute-start.1) | collective-permute-done | bytes 67632 | tf_op jit(solution)/shard_map/ppermute | solution.py:22
  404.1 0.6 pad_maximum_fusion
  404.8 2.2 fusion.83
  406.9 2.2 copy.42
  409.1 3.3 collective-permute-start.2
  412.4 2.2 copy.43
  414.6 2.1 copy.44
  416.7 1.1 collective-permute-done.3
  417.9 2.1 copy.45
  420.0 3.8 pad_maximum_fusion.1
  423.8 0.3 slice.213
  424.1 1.1 copy-done
  425.2 0.5 copy-done.1
  425.7 1.4 maximum_add_fusion.1
  427.1 1.5 maximum_add_fusion
  428.6 0.5 pad_maximum_fusion.2
  429.1 0.3 slice.216
  429.4 0.9 slice_add_fusion.1
  430.3 0.6 pad_maximum_fusion.3
  430.9 1.3 copy.46
  432.3 4.6 all-to-all-start
  437.2 52.8 %all-to-all-done = f32[130,16,128]{2,0,1:T(8,128)S(1)} async-done(((f32[130,16,128]{2,0,1:T(8,128)}), f32[130,16,128]{2,0,1:T(8,128)S(1)}, u32[]{:S(2)}, u32[]{:S(2)}) %all-to-all-start) | async-done | bytes 1064992 | tf_op jit(solution)/shard_map/all_to_all | solution.py:93
  490.0 0.2 copy.47
  490.3 0.4 copy.50
  490.7 0.3 copy.49
  491.0 0.8 reshape_reshape.7
  491.9 1.8 copy.61
  493.7 1.6 fusion.8
  495.3 1.8 multiply_add_fusion
  497.1 1.2 fusion.5
  498.3 1.2 fusion.1
  499.5 1.2 convolution_add_fusion
  500.8 1.2 convolution_subtract_fusion
  502.0 0.3 copy.60
  502.3 0.3 stack.74
  502.6 0.3 copy.57
  502.9 0.3 stack.73
  503.2 1.5 fusion
  (26 shorter events, 1.0 us)
Async XLA Ops:
  0.6 3.2 copy-start.2
  0.6 3.2 copy-start.3
  350.1 29.1 %collective-permute-start = (f32[130,1,130]{2,1,0:T(1,128)S(1)}, f32[130,1,130]{2,1,0:T(1,128)S(1)}, u32[]{:S(2)}, u32[]{:S(2)}) collective-permute-start(f32[130,1,130]{2,1,0:T(1,128)S(1)} %get-tuple-element.60), channel_id=1, source_target_pairs={{0,8},{8,16},{16,24},{24,32},{32,40},{40,48},{48,56},{56,64},{64,7... | collective-permute-start | bytes 202808 | tf_op jit(solution)/shard_map/ppermute | solution.py:20
  366.3 37.8 %collective-permute-start.1 = (f32[130,1,130]{2,1,0:T(1,128)S(1)}, f32[130,1,130]{2,1,0:T(1,128)S(1)}, u32[]{:S(2)}, u32[]{:S(2)}) collective-permute-start(f32[130,1,130]{2,1,0:T(1,128)S(1)} %get-tuple-element.61), channel_id=1, source_target_pairs={{8,0},{16,8},{24,16},{32,24},{40,32},{48,40},{56,48},{64,56},{72,6... | collective-permute-start | bytes 202808 | tf_op jit(solution)/shard_map/ppermute | solution.py:22
  409.1 5.5 %collective-permute-start.2 = (f32[130,20,1]{0,2,1:T(1,128)S(1)}, f32[130,20,1]{0,2,1:T(1,128)S(1)}, u32[]{:S(2)}, u32[]{:S(2)}) collective-permute-start(f32[130,20,1]{0,2,1:T(1,128)S(1)} %copy.42), channel_id=1, source_target_pairs={{0,1},{1,2},{2,3},{3,4},{4,5},{5,6},{6,7},{7,0},{8,9},{9,10},{10,1... | collective-permute-start | bytes 31208 | tf_op jit(solution)/shard_map/ppermute | solution.py:20
  414.6 3.2 collective-permute-start.3
  423.8 1.4 copy-start
  423.8 1.9 copy-start.1
  432.3 57.7 %all-to-all-start = ((f32[130,16,128]{2,0,1:T(8,128)}), f32[130,16,128]{2,0,1:T(8,128)S(1)}, u32[]{:S(2)}, u32[]{:S(2)}) async-start(f32[130,16,128]{2,0,1:T(8,128)} %copy.46), calls=%async_computation | async-start | bytes 2228224 | tf_op jit(solution)/shard_map/all_to_all | solution.py:93
where the time goes:
time: 506 us; the launch traced here: 505 us
  other arithmetic  356 us (70%)
  waiting for transfers between devices  79.8 us (16%)
  starting transfers between devices  36 us (7%)
  local copies, waits for them, and re-layouts  22.8 us (5%)
  matrix products  8.25 us (2%)
    scatter-add x1, other arithmetic, paint(): return painted.at[jnp.stack(targets)].add(jnp.stack(weights))  342 us
    all_to_all x1, waiting for transfers between devices, body(): lax.all_to_all(folded, 'gx', split_axis=1, concat_axis=0, tiled=True)  52.8 us
    ppermute x2, waiting for transfers between devices, with_halo(): lax.ppermute(head, axis, [((i + 1) % count, i) for i in range(count)])  26.1 us
    ppermute x2, starting transfers between devices, with_halo(): lax.ppermute(tail, axis, [(i, (i + 1) % count) for i in range(count)])  19.5 us
    ppermute x2, starting transfers between devices, with_halo(): lax.ppermute(head, axis, [((i + 1) % count, i) for i in range(count)])  11.8 us
  transfers between devices with their start and end apart: 5, of which 4 were waited for; matrix products, arithmetic and copies ran while one was open for 1% of the time, Pallas kernels for 0%

commit v1 on v0

v1 whole, which is shorter than its diff:
```python
import functools
import math

import jax
import jax.numpy as jnp
from jax import lax
from jax.experimental import pallas as pl
from jax.experimental.pallas import tpu as pltpu
from jax.sharding import PartitionSpec as P

F32, I32, BF = jnp.float32, jnp.int32, jnp.bfloat16
GX = 8
ROWS = 18
FROWS = 8
NROW = 64
PAYROWS = 96
XR = 136
LANE = {6: 64, 7: 1, 8: 2, 9: 4, 10: 8, 11: 16, 12: 32}
SUB = {3: 1, 4: 2, 5: 4}
VM = pl.BlockSpec(memory_space=pltpu.VMEM)
SM = pl.BlockSpec(memory_space=pltpu.SMEM)


def cells_of(flat):
    row = jnp.floor((flat + 0.5) * (1.0 / 130.0))
    xp = jnp.floor((row + 0.5) * (1.0 / 18.0))
    return xp, row - 18.0 * xp, flat - 130.0 * row


def halves(value):
    high = value.astype(BF).astype(F32)
    return high, value - high


def index_bit(bit, lane, sub, reg):
    if bit < 3:
        return bool((reg >> bit) & 1)
    if bit in SUB:
        return (sub & SUB[bit]) != 0
    return (lane & LANE[bit]) != 0


def sort_network(ops, lane, sub):
    for size in range(1, 14):
        for bit in range(size - 1, -1, -1):
            new = [[None] * 8 for _ in ops]
            if bit < 3:
                for v in range(8):
                    w = v | (1 << bit)
                    if v == w:
                        continue
                    down = False if size == 13 else index_bit(size, lane, sub, v)
                    a, c = ops[0][v], ops[0][w]
                    if down is True:
                        move = a < c
                    elif down is False:
                        move = a > c
                    else:
                        move = ((a > c) ^ down) & (a != c)
                    for o in range(len(ops)):
                        a, c = ops[o][v], ops[o][w]
                        new[o][v] = jnp.where(move, c, a)
                        new[o][w] = jnp.where(move, a, c)
            else:
                axis, step, index = (0, SUB[bit], sub) if bit in SUB else (1, LANE[bit], lane)
                upper = (index & step) != 0
                other = index ^ step

                def partner(x):
                    if 2 * step == x.shape[axis]:
                        return pltpu.roll(x, step, axis)
                    return jnp.take_along_axis(x, other, axis=axis)

                for v in range(8):
                    down = False if size == 13 else index_bit(size, lane, sub, v)
                    mine, theirs = ops[0][v], partner(ops[0][v])
                    if down is True:
                        big = ~upper
                    elif down is False:
                        big = upper
                    else:
                        big = upper ^ down
                    move = ((theirs > mine) & big) | ((theirs < mine) & ~big)
                    new[0][v] = jnp.where(move, theirs, mine)
                    for o in range(1, len(ops)):
                        new[o][v] = jnp.where(move, partner(ops[o][v]), ops[o][v])
            ops = new
    return ops


def sort_kernel(count_ref, cell_ref, off_ref, mass_ref, sorted_ref, pay_ref):
    lane = lax.broadcasted_iota(I32, (8, 128), 1)
    sub = lax.broadcasted_iota(I32, (8, 128), 0)
    count = count_ref[0]
    key, px, py, pz, pm = [], [], [], [], []
    below = [jnp.zeros((8, 128), F32) for _ in range(17)]
    for v in range(8):
        s = slice(8 * v, 8 * v + 8)
        cell = cell_ref[s, :]
        dy = off_ref[1, s, :]
        live = v * 1024 + sub * 128 + lane < count
        _, yp, _ = cells_of(cell.astype(F32))
        k = jnp.where(live, jnp.where(dy >= 0, yp, yp - 1.0), 20.0)
        for t in range(1, 17):
            below[t] = below[t] + jnp.where(k < t, 1.0, 0.0)
        key.append((k.astype(I32) << 19) | cell)
        px.append(off_ref[0, s, :])
        py.append(dy)
        pz.append(off_ref[2, s, :])
        pm.append(jnp.where(live, mass_ref[s, :], 0.0))
    below = [None] + [jnp.sum(b).astype(I32) for b in below[1:]]
    ops = sort_network([key, px, py, pz, pm], lane, sub)
    ops[0] = [(k & ((1 << 19) - 1)).astype(F32) for k in ops[0]]
    for o in range(5):
        t = jnp.concatenate(ops[o], axis=0).T
        sorted_ref[o] = jnp.concatenate([t[:64], t[64:]], axis=1)
    starts, over = [], below[1] > FROWS * 128
    for p in range(GX):
        if p < GX - 1:
            begin = below[2 * p] if p else jnp.int32(0)
            w = jnp.minimum(begin // 128, NROW - ROWS)
            over = over | (below[2 * p + 3] > 128 * (w + ROWS))
        else:
            w = jnp.clip((count + 127) // 128 - ROWS, 0, NROW - ROWS)
            over = over | (below[2 * p] < 128 * w) | (below[2 * p + 2] < 128 * (w + ROWS - FROWS))
        starts.append(w)
    flag = jnp.where(over, 1.0, 0.0)
    for p in range(GX):
        for o in range(5):
            pay_ref[p, o * ROWS : (o + 1) * ROWS, :] = sorted_ref[o, pl.ds(starts[p], ROWS), :]
        pay_ref[p, 5 * ROWS : PAYROWS, :] = jnp.full((PAYROWS - 5 * ROWS, 128), flag, F32)


def sort_and_pack(count, cell, off, mass):
    return pl.pallas_call(
        sort_kernel,
        out_shape=(
            jax.ShapeDtypeStruct((5, NROW, 128), F32),
            jax.ShapeDtypeStruct((GX, PAYROWS, 128), F32),
        ),
        in_specs=[SM, VM, VM, VM],
        out_specs=(VM, VM),
        name="sort_pack",
        cost_estimate=pl.CostEstimate(flops=30000000, bytes_accessed=800000, transcendentals=0),
    )(count, cell, off, mass)


def x_cells():
    i = lax.broadcasted_iota(I32, (XR, 128), 0)
    i = jnp.where(i == 128, 0, jnp.where(i == 129, 129, jnp.where(i > 129, 200, i + 1)))
    return i.astype(F32).astype(BF)


def spread(grid, first, second, one, two):
    zero = jnp.zeros((), BF)
    return jnp.where(first, one, jnp.where(second, two, zero))


def paint_kernel(rows, add, skip, where_ref, *refs):
    if add:
        recv_ref, acc_ref, out_ref, val_ref, a_ref, z_ref = refs
    else:
        recv_ref, out_ref, val_ref, a_ref, z_ref = refs
    ybase = where_ref[0].astype(F32)

    def source(i, carry):
        def op(k):
            return recv_ref[i, k * rows : (k + 1) * rows, :]

        dx, dy, dz, m = op(1), op(2), op(3), op(4)
        xp, yp, zp = cells_of(op(0))
        y = yp - 1.0 - ybase
        y1 = y + jnp.where(dy >= 0, 1.0, -1.0)
        ax, ay, az = jnp.abs(dx), jnp.abs(dy), jnp.abs(dz)
        coarse = jnp.floor(az * 256.0) * (1.0 / 256.0)
        fine = az - coarse
        vals = [xp, xp + jnp.where(dx >= 0, 1.0, -1.0), zp - 1.0, zp - 1.0 + jnp.where(dz >= 0, 1.0, -1.0)]
        vals += [1.0 - coarse, coarse, -fine, fine]
        for j in range(2):
            mj = m * (jnp.where(y == j, 1.0 - ay, 0.0) + jnp.where(y1 == j, ay, 0.0))
            for w in (1.0 - ax, ax):
                vals += list(halves(mj * w))
        for n, v in enumerate(vals):
            val_ref[n] = v
        xi = x_cells()
        zi = lax.broadcasted_iota(I32, (128, 128), 0).astype(F32).astype(BF)
        for r in range(rows):

            def row(n, height):
                return jnp.broadcast_to(val_ref[n, r : r + 1, :].astype(BF), (height, 128))

            cols = slice(r * 128, (r + 1) * 128)
            first, second = xi == row(0, XR), xi == row(1, XR)
            for j in range(2):
                for h in range(2):
                    n = 8 + 4 * j + h
                    a_ref[(2 * j + h) * XR : (2 * j + h + 1) * XR, cols] = spread(xi, first, second, row(n, XR), row(n + 2, XR))
            first, second = zi == row(2, 128), zi == row(3, 128)
            z_ref[0:128, cols] = spread(zi, first, second, row(4, 128), row(5, 128))
            z_ref[128:256, cols] = spread(zi, first, second, row(6, 128), row(7, 128))
        o = lax.dot_general(a_ref[...], z_ref[...], (((1,), (1,)), ((), ())), preferred_element_type=F32)
        for j in range(2):
            high, low = o[2 * j * XR : (2 * j + 1) * XR], o[(2 * j + 1) * XR : (2 * j + 2) * XR]
            total = high[:, :128] + high[:, 128:] + low[:, :128]
            if add:
                total = total + acc_ref[i, j]
            out_ref[i, j] = total
        return carry

    if skip:

        @pl.when((where_ref[1] == 0) | (where_ref[1] == GX - 1))
        def _():
            lax.fori_loop(0, GX, source, 0)
    else:
        lax.fori_loop(0, GX, source, 0)


def paint(where, recv, acc=None, rows=ROWS, skip=False):
    add = acc is not None
    shape = jax.ShapeDtypeStruct((GX, 2, XR, 128), F32)
    return pl.pallas_call(
        functools.partial(paint_kernel, rows, add, skip),
        out_shape=shape,
        in_specs=[SM, VM] + ([VM] if add else []),
        out_specs=VM,
        scratch_shapes=[
            pltpu.VMEM((16, rows, 128), F32),
            pltpu.VMEM((4 * XR, rows * 128), BF),
            pltpu.VMEM((256, rows * 128), BF),
        ],
        input_output_aliases={2: 0} if add else {},
        name="paint",
        cost_estimate=pl.CostEstimate(flops=rows * 3000000, bytes_accessed=2000000, transcendentals=0),
    )(where, recv, *([acc] if add else []))


def face_kernel(count_ref, cell_ref, off_ref, mass_ref, low_ref, high_ref, val_ref, x_ref, v_ref):
    count = count_ref[0]
    slot = lax.broadcasted_iota(I32, (NROW, 128), 0) * 128 + lax.broadcasted_iota(I32, (NROW, 128), 1)
    m = jnp.where(slot < count, mass_ref[...], 0.0)
    dx, dy, dz = off_ref[0], off_ref[1], off_ref[2]
    xp, yp, zp = cells_of(cell_ref[...].astype(F32))
    up = (zp == 128.0) & (dz >= 0)
    down = (zp == 1.0) & (dz < 0)
    ax, ay = jnp.abs(dx), jnp.abs(dy)
    w = jnp.where(up | down, m * jnp.abs(dz), 0.0)
    coarse = jnp.floor(ax * 256.0) * (1.0 / 256.0)
    fine = ax - coarse
    y = yp + jnp.where(up, 24.0, 0.0)
    vals = [xp, xp + jnp.where(dx >= 0, 1.0, -1.0), 1.0 - coarse, coarse, -fine, fine]
    vals += [y, y + jnp.where(dy >= 0, 1.0, -1.0)]
    vals += [*halves(w * (1.0 - ay)), *halves(w * ay)]
    for n, v in enumerate(vals):
        val_ref[n] = v
    xi = x_cells()
    yi = lax.broadcasted_iota(I32, (48, 128), 0).astype(F32).astype(BF)

    def chunk(b, total):
        for r in range(16):

            def row(n, height):
                return jnp.broadcast_to(val_ref[n, pl.ds(b * 16 + r, 1), :].astype(BF), (height, 128))

            cols = slice(r * 128, (r + 1) * 128)
            first, second = xi == row(0, XR), xi == row(1, XR)
            x_ref[0:XR, cols] = spread(xi, first, second, row(2, XR), row(3, XR))
            x_ref[XR : 2 * XR, cols] = spread(xi, first, second, row(4, XR), row(5, XR))
            first, second = yi == row(6, 48), yi == row(7, 48)
            v_ref[0:48, cols] = spread(yi, first, second, row(8, 48), row(10, 48))
            v_ref[64:112, cols] = spread(yi, first, second, row(9, 48), row(11, 48))
        return total + lax.dot_general(x_ref[...], v_ref[...], (((1,), (1,)), ((), ())), preferred_element_type=F32)

    v_ref[...] = jnp.zeros(v_ref.shape, BF)
    o = lax.fori_loop(0, 4, chunk, jnp.zeros((2 * XR, 128), F32))
    g = o[0:XR] + pltpu.roll(o[0:XR], 64, 1) + o[XR : 2 * XR]
    t = g.T
    low_ref[0:24] = t[0:24, 0:128]
    high_ref[0:24] = t[24:48, 0:128]
    low_ref[24:32] = g[128:136]
    high_ref[24:32] = g[128:136]


def faces(count, cell, off, mass):
    shape = jax.ShapeDtypeStruct((32, 128), F32)
    return pl.pallas_call(
        face_kernel,
        out_shape=(shape, shape),
        in_specs=[SM, VM, VM, VM],
        out_specs=(VM, VM),
        scratch_shapes=[
            pltpu.VMEM((12, NROW, 128), F32),
            pltpu.VMEM((2 * XR, 2048), BF),
            pltpu.VMEM((128, 2048), BF),
        ],
        name="faces",
        cost_estimate=pl.CostEstimate(flops=8000000, bytes_accessed=200000, transcendentals=0),
    )(count, cell, off, mass)


def face_pack_kernel(low_ref, high_ref, out_ref):
    for p in range(GX):
        out_ref[p, 0:4] = low_ref[2 * p : 2 * p + 4]
        out_ref[p, 4:8] = high_ref[2 * p : 2 * p + 4]
        out_ref[p, 8:10] = low_ref[24:26]
        out_ref[p, 10:12] = high_ref[24:26]
        out_ref[p, 12:16] = jnp.zeros((4, 128), F32)


def face_pack(low, high):
    return pl.pallas_call(
        face_pack_kernel,
        out_shape=jax.ShapeDtypeStruct((GX, 16, 128), F32),
        in_specs=[VM, VM],
        out_specs=VM,
        name="face_pack",
        cost_estimate=pl.CostEstimate(flops=500000, bytes_accessed=100000, transcendentals=0),
    )(low, high)


def forward_kernel(where_ref, recv_ref, face_ref, out_ref):
    first = jnp.where(where_ref[1] == GX - 1, ROWS - FROWS, 0)
    flag = jnp.zeros((1, 128), F32)
    for i in range(GX):
        for o in range(5):
            out_ref[i, o * FROWS : (o + 1) * FROWS, :] = recv_ref[i, pl.ds(o * ROWS + first, FROWS), :]
        flag = jnp.maximum(flag, recv_ref[i, 5 * ROWS : 5 * ROWS + 1, :])
    for i in range(GX):
        out_ref[i, 40:52, :] = face_ref[i, 0:12, :]
        out_ref[i, 52:56, :] = jnp.broadcast_to(flag, (4, 128))


def forward_pack(where, recv, face):
    return pl.pallas_call(
        forward_kernel,
        out_shape=jax.ShapeDtypeStruct((GX, 56, 128), F32),
        in_specs=[SM, VM, VM],
        out_specs=VM,
        name="forward_pack",
        cost_estimate=pl.CostEstimate(flops=500000, bytes_accessed=600000, transcendentals=0),
    )(where, recv, face)


def table_kernel(high_ref, low_ref, base_ref):
    step = 2.0 * math.pi / 1024.0
    x = lax.broadcasted_iota(I32, (64, 1024), 1)
    k = lax.broadcasted_iota(I32, (64, 1024), 0)
    angle = ((k * x) & 1023).astype(F32) * step
    base_ref[0] = jnp.cos(angle)
    base_ref[1] = jnp.sin(angle)
    x = lax.broadcasted_iota(I32, (8, 1024), 1)
    k = lax.broadcasted_iota(I32, (8, 1024), 0)
    angle = ((64 * k * x) & 1023).astype(F32) * step
    scale = 1.0 / 32.0
    turn_c, turn_s = jnp.cos(angle) * scale, jnp.sin(angle) * scale
    for b in range(8):
        c, s = turn_c[b : b + 1], turn_s[b : b + 1]
        real = base_ref[0] * c - base_ref[1] * s
        imag = -(base_ref[0] * s + base_ref[1] * c)
        for part, value in ((0, real), (512, imag)):
            high = value.astype(BF)
            high_ref[part + 64 * b : part + 64 * b + 64] = high
            low_ref[part + 64 * b : part + 64 * b + 64] = (value - high.astype(F32)).astype(BF)


def tables():
    shape = jax.ShapeDtypeStruct((1024, 1024), BF)
    return pl.pallas_call(
        table_kernel,
        out_shape=(shape, shape),
        out_specs=(VM, VM),
        scratch_shapes=[pltpu.VMEM((2, 64, 1024), F32)],
        name="tables",
        cost_estimate=pl.CostEstimate(flops=8000000, bytes_accessed=4000000, transcendentals=0),
    )()


def final_kernel(where_ref, acc_ref, face_ref, in_ref, th_ref, tl_ref, dens_ref, spec_ref, dh_ref, dl_ref):
    p = where_ref[1]
    first, last = p == 0, p == GX - 1
    lane = lax.broadcasted_iota(I32, (8, 128), 1)
    lane1 = lax.broadcasted_iota(I32, (1, 128), 1)

    def face_rows(i, j):
        got = []
        for side in range(2):
            v = face_ref[i, 4 * side + 1 + j : 4 * side + 2 + j, :]
            if j == 0:
                v = v + jnp.where(first, in_ref[i, 40 + 4 * side + 3 : 40 + 4 * side + 4, :], 0.0)
            else:
                v = v + jnp.where(last, in_ref[i, 40 + 4 * side : 40 + 4 * side + 1, :], 0.0)
            got.append(v)
        return got

    def ghost(i, j, side, end):
        n = 8 + 2 * side + end
        base = 24 if side == 0 else 0
        v = jnp.sum(jnp.where(lane1 == base + 2 * p + 1 + j, face_ref[i, n : n + 1, :], 0.0), axis=1, keepdims=True)
        pick, on = (17, first) if j == 0 else (0, last)
        u = jnp.sum(jnp.where(lane1 == base + pick, in_ref[i, 40 + n : 41 + n, :], 0.0), axis=1, keepdims=True)
        return v + jnp.where(on, u, 0.0)

    wide = lax.broadcasted_iota(I32, (128, 128), 1)
    tall = lax.broadcasted_iota(I32, (128, 128), 0)
    for i in range(GX):
        before, after = (i - 1) % GX, (i + 1) % GX
        rows = []
        for j in range(2):
            for side, v in enumerate(face_rows(i, j)):
                v = v + jnp.where(lane1 == 127, ghost(after, j, side, 0), 0.0)
                v = v + jnp.where(lane1 == 0, ghost(before, j, side, 1), 0.0)
                rows.append(v)
        cols = jnp.concatenate(rows + [jnp.zeros((124, 128), F32)], axis=0).T
        for j in range(2):
            v = acc_ref[i, j, 0:128, :]
            v = v + jnp.where(tall == 127, acc_ref[after, j, 128:129, :], 0.0)
            v = v + jnp.where(tall == 0, acc_ref[before, j, 129:130, :], 0.0)
            v = v + jnp.where(wide == 0, cols[:, 2 * j : 2 * j + 1], 0.0)
            v = v + jnp.where(wide == 127, cols[:, 2 * j + 1 : 2 * j + 2], 0.0)
            dens_ref[pl.ds(i * 256 + j, 128, stride=2), :] = v
            high = v.astype(BF)
            dh_ref[i * 128 : (i + 1) * 128, j * 128 : (j + 1) * 128] = high
            dl_ref[i * 128 : (i + 1) * 128, j * 128 : (j + 1) * 128] = (v - high.astype(F32)).astype(BF)
    for b in range(4):
        rows = slice(b * 256, (b + 1) * 256)
        o = jnp.dot(th_ref[rows], dh_ref[...], preferred_element_type=F32)
        o = o + jnp.dot(th_ref[rows], dl_ref[...], preferred_element_type=F32)
        o = o + jnp.dot(tl_ref[rows], dh_ref[...], preferred_element_type=F32)
        for j in range(2):
            spec_ref[pl.ds(b * 512 + j, 256, stride=2), :] = o[:, j * 128 : (j + 1) * 128]


def finish(where, acc, face, received, th, tl):
    shape = jax.ShapeDtypeStruct((2048, 128), F32)
    return pl.pallas_call(
        final_kernel,
        out_shape=(shape, shape),
        in_specs=[SM] + [VM] * 5,
        out_specs=(VM, VM),
        scratch_shapes=[pltpu.VMEM((1024, 256), BF), pltpu.VMEM((1024, 256), BF)],
        name="finish",
        cost_estimate=pl.CostEstimate(flops=1600000000, bytes_accessed=8000000, transcendentals=0),
    )(where, acc, face, received, th, tl)


def y_pairs(blocks):
    pairs = []
    for q in range(blocks):
        pairs.append(((GX - 1) * blocks + q, (q + 1) % blocks))
        pairs.append((q, (GX - 1) * blocks + (q - 1) % blocks))
    return pairs


def exchange(x):
    return lax.all_to_all(x, "gx", split_axis=0, concat_axis=0, tiled=False)


def hand_on(x):
    return lax.ppermute(x, ("gx", "gy"), y_pairs(lax.axis_size("gy")))


def later_window(ordered, count, turn):
    xp, yp, zp = cells_of(ordered[0])
    live = ordered[4] != 0.0
    key = jnp.where(live, jnp.where(ordered[2] >= 0, yp, yp - 1.0), 20.0)
    space = jnp.zeros((5, NROW + 3 * ROWS, 128), F32)
    padded = jnp.concatenate([space, ordered, space], axis=1)
    base = NROW + 3 * ROWS
    blocks = []
    for p in range(GX):
        if p < GX - 1:
            begin = jnp.sum(jnp.where(key < 2 * p, 1, 0))
            w = jnp.minimum(begin // 128, NROW - ROWS) + turn * ROWS
        else:
            w = jnp.clip((count + 127) // 128 - ROWS, 0, NROW - ROWS) - turn * ROWS
        part = lax.dynamic_slice_in_dim(padded, base + w, ROWS, axis=1).reshape(5 * ROWS, 128)
        blocks.append(jnp.concatenate([part, jnp.zeros((PAYROWS - 5 * ROWS, 128), F32)], axis=0))
    return jnp.stack(blocks)


def body(cell_index, offsets, mass, counts):
    p = lax.axis_index("gx")
    blocks = lax.axis_size("gz")
    cell, off, m, count = cell_index.reshape(NROW, 128), offsets.reshape(3, NROW, 128), mass.reshape(NROW, 128), counts.reshape(1)
    here = jnp.stack([2 * p, p]).astype(I32)
    there = jnp.stack([jnp.where(p == 0, 16, -2), p]).astype(I32)

    ordered, pay = sort_and_pack(count, cell, off, m)
    recv = exchange(pay)

    low, high = faces(count, cell, off, m)
    from_below = lax.ppermute(high, "gz", [(i, (i + 1) % blocks) for i in range(blocks)])
    from_above = lax.ppermute(low, "gz", [((i + 1) % blocks, i) for i in range(blocks)])
    face = exchange(face_pack(from_below, from_above))
    th, tl = tables()

    passed = hand_on(forward_pack(here, recv, face))
    acc = paint(here, recv)
    acc = paint(there, passed[:, :40], acc, rows=FROWS, skip=True)

    mine = jnp.max(recv[:, 5 * ROWS, 0]) > 0
    theirs = passed[0, 52, 0] > 0

    def slow(acc):
        later = lax.cond(
            mine,
            lambda: jnp.stack([exchange(later_window(ordered, count[0], t)) for t in (1, 2, 3)]),
            lambda: jnp.zeros((3,) + recv.shape, F32),
        )
        first = jnp.where(p == GX - 1, ROWS - FROWS, 0)
        row = lax.broadcasted_iota(I32, (PAYROWS, 128), 0) - 4 * ROWS
        sent = (row >= first) & (row < first + FROWS)
        rest = jnp.where(sent, 0.0, recv)
        for t in range(3):
            acc = paint(here, later[t], acc)
        for x in [rest] + [later[t] for t in range(3)]:
            acc = paint(there, hand_on(x), acc, skip=True)
        return acc

    acc = lax.cond(mine | theirs, slow, lambda a: a, acc)
    density, spectrum = finish(here, acc, face, passed, th, tl)
    return density.reshape(1024, 1, 2, 128), spectrum.reshape(2, 512, 1, 2, 128)


def solution(mesh):
    placed = (
        P("gx", "gy", "gz", None),
        P("gx", "gy", "gz", None, None),
        P("gx", "gy", "gz", None),
        P("gx", "gy", "gz"),
    )
    return jax.shard_map(
        body,
        mesh=mesh,
        in_specs=placed,
        out_specs=(P(None, "gx", "gy", "gz"), P(None, None, "gx", "gy", "gz")),
        check_vma=False,
    )
```

time: 506 us -> 106 us (0.21)
  other arithmetic: 356 us -> 0.76 us
  waiting for transfers between devices: 79.8 us -> 16.3 us
  Pallas kernels: 0 us -> 40.8 us
  local copies, waits for them, and re-layouts: 22.8 us -> 2.28 us
  matrix products: 8.25 us -> 0 us
  starting transfers between devices: 36 us -> 42.2 us
    scatter-add x3 -> x0, other arithmetic: 342 us -> none  [the longest x1 342 us: paint(): return painted.at[jnp.stack(targets)].add(jnp.stack(weights))]
    pallas_call x0 -> x8, Pallas kernels: none -> 40.8 us  [the longest x2 17.8 us: paint(): pl.pallas_call(functools.partial(paint_kernel, rows, add, skip), out_shap...]
    all_to_all x1 -> x2, waiting for transfers between devices: 52.8 us -> 15.2 us  [exchange(): return lax.all_to_all(x, 'gx', split_axis=0, concat_axis=0, tiled=False)]
    ppermute x4 -> x3, waiting for transfers between devices: 27.1 us -> 1.05 us  [the longest x1 0.88 us: body(): lax.ppermute(high, 'gz', [(i, (i + 1) % blocks) for i in range(blocks)])]
    dot_general x6 -> x0, matrix products: 8.25 us -> none  [the longest x1 1.84 us: body(): first_imag = -jnp.einsum('kb,bar->kar', sin_b, columns, precision=highest)]
    slice x9 -> x2, local copies, waits for them, and re-layouts: 7.48 us -> 1.23 us  [the longest x1 0.68 us: body(): acc = paint(there, passed[:, :40], acc, rows=FROWS, skip=True)]
    concatenate x4 -> x0, other arithmetic: 5.55 us -> none  [the longest x2 4.43 us: with_halo(): jnp.concatenate([lax.ppermute(tail, axis, [(i, (i + 1) % count) for i in...]
    ppermute x4 -> x3, starting transfers between devices: 31.4 us -> 34.5 us  [the longest x1 20.4 us: hand_on(): return lax.ppermute(x, ('gx', 'gy'), y_pairs(lax.axis_size('gy')))]
  transfers between devices with their start and end apart: 5 -> 5, of which waited for: 4 -> 4; matrix products, arithmetic and copies ran while one was open for 1% -> 1% of each run, Pallas kernels for 0% -> 19%
where the time goes in v1:
time: 106 us; the launch traced here: 105 us
  starting transfers between devices  42.2 us (40%)
  Pallas kernels  40.8 us (38%)
  waiting for transfers between devices  16.3 us (15%)
  between operations  2.66 us (3%)
  local copies, waits for them, and re-layouts  2.28 us (2%)
    ppermute x1, starting transfers between devices, hand_on(): return lax.ppermute(x, ('gx', 'gy'), y_pairs(lax.axis_size('gy')))  20.4 us
    pallas_call x2, Pallas kernels, paint(): pl.pallas_call(functools.partial(paint_kernel, rows, add, skip), out_shap...  17.8 us
    all_to_all x2, waiting for transfers between devices, exchange(): return lax.all_to_all(x, 'gx', split_axis=0, concat_axis=0, tiled=False)  15.2 us
    ppermute x1, starting transfers between devices, body(): lax.ppermute(low, 'gz', [((i + 1) % blocks, i) for i in range(blocks)])  11.5 us
    all_to_all x2, starting transfers between devices, exchange(): return lax.all_to_all(x, 'gx', split_axis=0, concat_axis=0, tiled=False)  7.65 us
    pallas_call x1, Pallas kernels, finish(): pl.pallas_call(final_kernel, out_shape=(shape, shape), in_specs=[SM] + [V...  6.69 us
    pallas_call x1, Pallas kernels, faces(): pl.pallas_call(face_kernel, out_shape=(shape, shape), in_specs=[SM, VM, V...  4.75 us
    pallas_call x1, Pallas kernels, sort_and_pack(): pl.pallas_call(sort_kernel, out_shape=(jax.ShapeDtypeStruct((5, NROW, 128...  4.71 us
  transfers between devices with their start and end apart: 5, of which 4 were waited for; matrix products, arithmetic and copies ran while one was open for 1% of the time, Pallas kernels for 19%

profile of v1, /device:TPU:1, one launch (start us, length us, event | category | flops | bytes accessed | tf_op | source)
XLA Modules:
  0.0 105.2 jit_solution(6493972766721914232)
XLA Ops:
  1.3 4.7 %faces.1 = (f32[32,128]{1,0:T(8,128)}, f32[32,128]{1,0:T(8,128)}) custom-call(s32[1]{0:T(128)} %bitcast.88.count_ref, s32[64,128]{1,0:T(8,128)} %bitcast.93, f32[3,64,128]{2,1,0:T(8,128)} %bitcast.91, f32[64,128]{1,0:T(8,128)} %bitcast.95), custom_call_target="tpu_custom_call" | custom-call | flops 8000000 | bytes 200000 | tf_op jit(solution)/shard_map/faces/pallas_call | solution.py:286
  6.0 2.6 %collective-permute-start.4 = (f32[32,128]{1,0:T(8,128)}, f32[32,128]{1,0:T(8,128)S(1)}, u32[]{:S(2)}, u32[]{:S(2)}) collective-permute-start(f32[32,128]{1,0:T(8,128)} %get-tuple-element.55), channel_id=1, source_target_pairs={{0,1},{1,2},{2,3},{3,4},{4,5},{5,6},{6,7},{7,0},{8,9},{9,10},{10,1... | collective-permute-start | bytes 49160 | tf_op jit(solution)/shard_map/ppermute | solution.py:492
  8.6 11.5 %collective-permute-start.5 = (f32[32,128]{1,0:T(8,128)}, f32[32,128]{1,0:T(8,128)S(1)}, u32[]{:S(2)}, u32[]{:S(2)}) collective-permute-start(f32[32,128]{1,0:T(8,128)} %get-tuple-element.56), channel_id=1, source_target_pairs={{1,0},{2,1},{3,2},{4,3},{5,4},{6,5},{7,6},{0,7},{9,8},{10,9},{11,1... | collective-permute-start | bytes 49160 | tf_op jit(solution)/shard_map/ppermute | solution.py:493
  20.1 0.9 collective-permute-done.4.low_ref
  21.0 0.0 copy-start.11
  21.0 0.2 collective-permute-done.5.high_ref
  21.2 0.4 copy-done.11
  21.6 0.0 copy-start.12
  21.6 0.6 copy-done.12
  22.2 1.4 %face_pack.1 = f32[8,16,128]{2,1,0:T(8,128)} custom-call(f32[32,128]{1,0:T(8,128)} %copy-done.11, f32[32,128]{1,0:T(8,128)} %copy-done.12), custom_call_target="tpu_custom_call" | custom-call | flops 500000 | bytes 100000 | tf_op jit(solution)/shard_map/face_pack/pallas_call | solution.py:311
  23.6 3.4 %all-to-all-start.4 = ((f32[8,16,128]{2,1,0:T(8,128)}), f32[8,16,128]{2,1,0:T(8,128)S(1)}, u32[]{:S(2)}, u32[]{:S(2)}) async-start(f32[8,16,128]{2,1,0:T(8,128)} %face_pack.1), calls=%async_computation.4 | async-start | bytes 131072 | tf_op jit(solution)/shard_map/all_to_all | solution.py:455
  27.0 4.7 %sort_pack.1 = (f32[5,64,128]{2,1,0:T(8,128)S(1)}, f32[8,96,128]{2,1,0:T(8,128)}) custom-call(s32[1]{0:T(128)} %bitcast.87.count_ref, s32[64,128]{1,0:T(8,128)} %bitcast.94, f32[3,64,128]{2,1,0:T(8,128)} %bitcast.92, f32[64,128]{1,0:T(8,128)} %bitcast.96), custom_call_target="tpu_custom_call" | custom-call | flops 30000000 | bytes 800000 | tf_op jit(solution)/shard_map/sort_pack/pallas_call | solution.py:135
  31.7 5.0 %all-to-all-done.4.face_ref = f32[8,16,128]{2,1,0:T(8,128)S(1)} async-done(((f32[8,16,128]{2,1,0:T(8,128)}), f32[8,16,128]{2,1,0:T(8,128)S(1)}, u32[]{:S(2)}, u32[]{:S(2)}) %all-to-all-start.4) | async-done | bytes 65568 | tf_op jit(solution)/shard_map/all_to_all | solution.py:455
  36.7 0.0 copy-start.3
  36.7 4.3 %all-to-all-start.3 = ((f32[8,96,128]{2,1,0:T(8,128)}), f32[8,96,128]{2,1,0:T(8,128)S(1)}, u32[]{:S(2)}, u32[]{:S(2)}) async-start(f32[8,96,128]{2,1,0:T(8,128)} %get-tuple-element.54), calls=%async_computation.3 | async-start | bytes 786432 | tf_op jit(solution)/shard_map/all_to_all | solution.py:455
  41.0 4.0 %tables.1 = (bf16[1024,1024]{1,0:T(8,128)(2,1)}, bf16[1024,1024]{1,0:T(8,128)(2,1)}) custom-call(), custom_call_target="tpu_custom_call" | custom-call | flops 8000000 | bytes 4000000 | tf_op jit(solution)/shard_map/tables/pallas_call | solution.py:368
  45.0 0.1 pad_add_fusion.where_ref
  45.0 10.2 %all-to-all-done.3.recv_ref.refs_0_ = f32[8,96,128]{2,1,0:T(8,128)S(1)} async-done(((f32[8,96,128]{2,1,0:T(8,128)}), f32[8,96,128]{2,1,0:T(8,128)S(1)}, u32[]{:S(2)}, u32[]{:S(2)}) %all-to-all-start.3) | async-done | bytes 393248 | tf_op jit(solution)/shard_map/all_to_all | solution.py:455
  55.3 0.0 copy-done.3
  55.3 1.6 %forward_pack.1 = f32[8,56,128]{2,1,0:T(8,128)} custom-call(s32[2]{0:T(128)S(1)} %pad_add_fusion.where_ref, f32[8,96,128]{2,1,0:T(8,128)S(1)} %all-to-all-done.3.recv_ref.refs_0_, f32[8,16,128]{2,1,0:T(8,128)} %copy-done.3), custom_call_target="tpu_custom_call" | custom-call | flops 500000 | bytes 600000 | tf_op jit(solution)/shard_map/forward_pack/pallas_call | solution.py:334
  56.8 20.4 %collective-permute-start.6 = (f32[8,56,128]{2,1,0:T(8,128)}, f32[8,56,128]{2,1,0:T(8,128)S(1)}, u32[]{:S(2)}, u32[]{:S(2)}) collective-permute-start(f32[8,56,128]{2,1,0:T(8,128)} %forward_pack.1), channel_id=1, source_target_pairs={{896,8},{0,1016},{904,16},{8,896},{912,24},{16,904},{920,32},{24,9... | collective-permute-start | bytes 688136 | tf_op jit(solution)/shard_map/ppermute | solution.py:459
  77.3 0.1 pad_add_fusion.1.where_ref
  77.3 0.6 slice_reduce_fusion
  78.6 10.9 %paint.16.refs_1_ = f32[8,2,136,128]{3,2,1,0:T(8,128)S(1)} custom-call(s32[2]{0:T(128)S(1)} %pad_add_fusion.where_ref, f32[8,96,128]{2,1,0:T(8,128)S(1)} %all-to-all-done.3.recv_ref.refs_0_), custom_call_target="tpu_custom_call" | custom-call | flops 54000000 | bytes 2000000 | tf_op jit(solution)/shard_map/paint/pallas_call | solution.py:222
  89.5 0.0 collective-permute-done.6.in_ref
  89.5 0.0 copy-start.10
  89.5 0.6 slice.42
  90.8 0.7 slice.43.refs_0_
  91.4 6.8 %paint.17 = f32[8,2,136,128]{3,2,1,0:T(8,128)S(1)} custom-call(s32[2]{0:T(128)S(1)} %pad_add_fusion.1.where_ref, f32[8,40,128]{2,1,0:T(8,128)} %slice.43.refs_0_, f32[8,2,136,128]{3,2,1,0:T(8,128)S(1)} %paint.16.refs_1_), custom_call_target="tpu_custom_call", output_to_operand_aliasing={{}: (2, {})} | custom-call | flops 24000000 | bytes 2000000 | tf_op jit(solution)/shard_map/paint/pallas_call | solution.py:222
  98.3 0.0 copy-done.10
  98.3 0.2 conditional.2
  98.5 6.7 %finish.1 = (f32[2048,128]{1,0:T(8,128)}, f32[2048,128]{1,0:T(8,128)}) custom-call(s32[2]{0:T(128)S(1)} %pad_add_fusion.where_ref, f32[8,2,136,128]{3,2,1,0:T(8,128)S(1)} %get-tuple-element.109.acc_ref, f32[8,16,128]{2,1,0:T(8,128)} %copy-done.3, f32[8,56,128]{2,1,0:T(8,128)} %copy-done.10, bf16[1024,1024]{1,0:T(8,128)(2,1)} %get-tuple-element.58.th_ref, ...), custom_call_target="tpu_custom_call" | custom-call | flops 1600000000 | bytes 8000000 | tf_op jit(solution)/shard_map/finish/pallas_call | solution.py:435
Async XLA Ops:
  6.0 15.0 %collective-permute-start.4 = (f32[32,128]{1,0:T(8,128)}, f32[32,128]{1,0:T(8,128)S(1)}, u32[]{:S(2)}, u32[]{:S(2)}) collective-permute-start(f32[32,128]{1,0:T(8,128)} %get-tuple-element.55), channel_id=1, source_target_pairs={{0,1},{1,2},{2,3},{3,4},{4,5},{5,6},{6,7},{7,0},{8,9},{9,10},{10,1... | collective-permute-start | bytes 49160 | tf_op jit(solution)/shard_map/ppermute | solution.py:492
  8.6 12.6 %collective-permute-start.5 = (f32[32,128]{1,0:T(8,128)}, f32[32,128]{1,0:T(8,128)S(1)}, u32[]{:S(2)}, u32[]{:S(2)}) collective-permute-start(f32[32,128]{1,0:T(8,128)} %get-tuple-element.56), channel_id=1, source_target_pairs={{1,0},{2,1},{3,2},{4,3},{5,4},{6,5},{7,6},{0,7},{9,8},{10,9},{11,1... | collective-permute-start | bytes 49160 | tf_op jit(solution)/shard_map/ppermute | solution.py:493
  21.0 0.6 copy-start.11
  21.6 0.6 copy-start.12
  23.6 13.0 %all-to-all-start.4 = ((f32[8,16,128]{2,1,0:T(8,128)}), f32[8,16,128]{2,1,0:T(8,128)S(1)}, u32[]{:S(2)}, u32[]{:S(2)}) async-start(f32[8,16,128]{2,1,0:T(8,128)} %face_pack.1), calls=%async_computation.4 | async-start | bytes 131072 | tf_op jit(solution)/shard_map/all_to_all | solution.py:455
  36.7 18.6 %copy-start.3 = (f32[8,16,128]{2,1,0:T(8,128)}, f32[8,16,128]{2,1,0:T(8,128)S(1)}, u32[]{:S(2)}) copy-start(f32[8,16,128]{2,1,0:T(8,128)S(1)} %all-to-all-done.4.face_ref) | copy-start | bytes 196612
  36.7 18.6 %all-to-all-start.3 = ((f32[8,96,128]{2,1,0:T(8,128)}), f32[8,96,128]{2,1,0:T(8,128)S(1)}, u32[]{:S(2)}, u32[]{:S(2)}) async-start(f32[8,96,128]{2,1,0:T(8,128)} %get-tuple-element.54), calls=%async_computation.3 | async-start | bytes 786432 | tf_op jit(solution)/shard_map/all_to_all | solution.py:455
  56.8 32.7 %collective-permute-start.6 = (f32[8,56,128]{2,1,0:T(8,128)}, f32[8,56,128]{2,1,0:T(8,128)S(1)}, u32[]{:S(2)}, u32[]{:S(2)}) collective-permute-start(f32[8,56,128]{2,1,0:T(8,128)} %forward_pack.1), channel_id=1, source_target_pairs={{896,8},{0,1016},{904,16},{8,896},{912,24},{16,904},{920,32},{24,9... | collective-permute-start | bytes 688136 | tf_op jit(solution)/shard_map/ppermute | solution.py:459
  89.5 8.8 %copy-start.10 = (f32[8,56,128]{2,1,0:T(8,128)}, f32[8,56,128]{2,1,0:T(8,128)S(1)}, u32[]{:S(2)}) copy-start(f32[8,56,128]{2,1,0:T(8,128)S(1)} %collective-permute-done.6.in_ref) | copy-start | bytes 688132

commit v2 on v1

v2 whole, which is shorter than its diff:
```python
import functools
import math

import jax
import jax.numpy as jnp
from jax import lax
from jax.experimental import pallas as pl
from jax.experimental.pallas import tpu as pltpu
from jax.sharding import PartitionSpec as P

F32, I32, BF = jnp.float32, jnp.int32, jnp.bfloat16
GX = 8
ROWS = 17
FROWS = 8
NROW = 64
PAYROWS = 96
FACE = 5 * ROWS
XR = 136
LANE = {6: 64, 7: 1, 8: 2, 9: 4, 10: 8, 11: 16, 12: 32}
SUB = {3: 1, 4: 2, 5: 4}
ROOM = pltpu.CompilerParams(vmem_limit_bytes=12 * 1024 * 1024)
VM = pl.BlockSpec(memory_space=pltpu.VMEM)
SM = pl.BlockSpec(memory_space=pltpu.SMEM)


def cells_of(flat):
    row = jnp.floor((flat + 0.5) * (1.0 / 130.0))
    xp = jnp.floor((row + 0.5) * (1.0 / 18.0))
    return xp, row - 18.0 * xp, flat - 130.0 * row


def halves(value):
    high = value.astype(BF).astype(F32)
    return high, value - high


def index_bit(bit, lane, sub, reg):
    if bit < 3:
        return bool((reg >> bit) & 1)
    if bit in SUB:
        return (sub & SUB[bit]) != 0
    return (lane & LANE[bit]) != 0


def sort_network(ops, lane, sub):
    for size in range(1, 14):
        for bit in range(size - 1, -1, -1):
            new = [[None] * 8 for _ in ops]
            if bit < 3:
                for v in range(8):
                    w = v | (1 << bit)
                    if v == w:
                        continue
                    down = False if size == 13 else index_bit(size, lane, sub, v)
                    a, c = ops[0][v], ops[0][w]
                    if down is True:
                        move = a < c
                    elif down is False:
                        move = a > c
                    else:
                        move = ((a > c) ^ down) & (a != c)
                    for o in range(len(ops)):
                        a, c = ops[o][v], ops[o][w]
                        new[o][v] = jnp.where(move, c, a)
                        new[o][w] = jnp.where(move, a, c)
            else:
                axis, step, index = (0, SUB[bit], sub) if bit in SUB else (1, LANE[bit], lane)
                upper = (index & step) != 0
                other = index ^ step

                def partner(x):
                    if 2 * step == x.shape[axis]:
                        return pltpu.roll(x, step, axis)
                    if axis == 0:
                        return jnp.where(upper, pltpu.roll(x, step, 0), pltpu.roll(x, 8 - step, 0))
                    return jnp.take_along_axis(x, other, axis=axis)

                for v in range(8):
                    down = False if size == 13 else index_bit(size, lane, sub, v)
                    mine, theirs = ops[0][v], partner(ops[0][v])
                    if down is True:
                        big = ~upper
                    elif down is False:
                        big = upper
                    else:
                        big = upper ^ down
                    move = ((theirs > mine) & big) | ((theirs < mine) & ~big)
                    new[0][v] = jnp.where(move, theirs, mine)
                    for o in range(1, len(ops)):
                        new[o][v] = jnp.where(move, partner(ops[o][v]), ops[o][v])
            ops = new
    return ops


def sort_kernel(count_ref, cell_ref, off_ref, mass_ref, sorted_ref, start_ref):
    lane = lax.broadcasted_iota(I32, (8, 128), 1)
    sub = lax.broadcasted_iota(I32, (8, 128), 0)
    count = count_ref[0]
    key, px, py, pz, pm = [], [], [], [], []
    below = [jnp.zeros((8, 128), F32) for _ in range(17)]
    for v in range(8):
        s = slice(8 * v, 8 * v + 8)
        cell = cell_ref[s, :]
        dy = off_ref[1, s, :]
        live = v * 1024 + sub * 128 + lane < count
        _, yp, _ = cells_of(cell.astype(F32))
        k = jnp.where(live, jnp.where(dy >= 0, yp, yp - 1.0), 20.0)
        for t in range(1, 17):
            below[t] = below[t] + jnp.where(k < t, 1.0, 0.0)
        key.append((k.astype(I32) << 19) | cell)
        px.append(off_ref[0, s, :])
        py.append(dy)
        pz.append(off_ref[2, s, :])
        pm.append(jnp.where(live, mass_ref[s, :], 0.0))
    below = [None] + [jnp.sum(b).astype(I32) for b in below[1:]]
    ops = sort_network([key, px, py, pz, pm], lane, sub)
    ops[0] = [(k & ((1 << 19) - 1)).astype(F32) for k in ops[0]]
    for o in range(5):
        t = jnp.concatenate(ops[o], axis=0).T
        sorted_ref[o] = jnp.concatenate([t[:64], t[64:]], axis=1)
    over = below[1] > FROWS * 128
    for p in range(GX):
        if p < GX - 1:
            begin = below[2 * p] if p else jnp.int32(0)
            w = jnp.minimum(begin >> 7, NROW - ROWS)
            over = over | (below[2 * p + 3] > 128 * (w + ROWS))
        else:
            w = jnp.clip(((count + 127) >> 7) - ROWS, 0, NROW - ROWS)
            over = over | (below[2 * p] < 128 * w) | (below[2 * p + 2] < 128 * (w + ROWS - FROWS))
        start_ref[p] = w
    start_ref[GX] = over.astype(I32)


def sort_particles(count, cell, off, mass):
    return pl.pallas_call(
        sort_kernel,
        out_shape=(jax.ShapeDtypeStruct((5, NROW, 128), F32), jax.ShapeDtypeStruct((GX + 1,), I32)),
        in_specs=[SM, VM, VM, VM],
        out_specs=(VM, SM),
        name="sort_particles",
        compiler_params=ROOM,
        cost_estimate=pl.CostEstimate(flops=30000000, bytes_accessed=800000, transcendentals=0),
    )(count, cell, off, mass)


def pack_kernel(start_ref, part_ref, below_ref, above_ref, pay_ref):
    lane = lax.broadcasted_iota(I32, (2, 128), 1)
    ghosts = jnp.where(lane < 24, above_ref[24:26], below_ref[24:26])
    ghosts = jnp.where(lane < 64, ghosts, start_ref[GX].astype(F32))
    for p in range(GX):
        for o in range(5):
            pay_ref[p, o * ROWS : (o + 1) * ROWS, :] = part_ref[o, pl.ds(start_ref[p], ROWS), :]
        past = 17 if p == GX - 1 else 0
        for n, ref in enumerate((below_ref, above_ref)):
            pay_ref[p, FACE + 3 * n : FACE + 3 * n + 2, :] = ref[2 * p + 1 : 2 * p + 3]
            pay_ref[p, FACE + 3 * n + 2 : FACE + 3 * n + 3, :] = ref[past : past + 1]
        pay_ref[p, FACE + 6 : FACE + 8, :] = ghosts


def pack(start, ordered, below, above):
    return pl.pallas_call(
        pack_kernel,
        out_shape=jax.ShapeDtypeStruct((GX, PAYROWS, 128), F32),
        in_specs=[SM, VM, VM, VM],
        out_specs=VM,
        name="pack",
        compiler_params=ROOM,
        cost_estimate=pl.CostEstimate(flops=3000000, bytes_accessed=600000, transcendentals=0),
    )(start, ordered, below, above)


def spread(first, second, one, two):
    return jnp.where(first, one, jnp.where(second, two, jnp.zeros((), BF)))


def counting(height, start=0):
    return (lax.broadcasted_iota(I32, (height, 128), 0) + start).astype(F32).astype(BF)


def paint_sources(rows, together, acc_ref, where_ref, recv_ref, out_ref, val_ref):
    ybase = where_ref[0].astype(F32)
    grid = counting(16)
    ghost = lax.broadcasted_iota(I32, (16, 128), 0)
    ghost_cell = jnp.where(ghost >= 8, 200, jnp.where((ghost & 1) == 0, 0, 129)).astype(F32).astype(BF)
    ghost_row = (ghost >> 1).astype(F32).astype(BF)

    def prepare(i, slot):
        def op(k):
            return recv_ref[i, k * rows : (k + 1) * rows, :]

        dx, dy, dz, m = op(1), op(2), op(3), op(4)
        xp, yp, zp = cells_of(op(0))
        y = yp - 1.0 - ybase
        y1 = y + jnp.where(dy >= 0, 1.0, -1.0)
        ax, ay, az = jnp.abs(dx), jnp.abs(dy), jnp.abs(dz)
        coarse = jnp.floor(az * 256.0) * (1.0 / 256.0)
        fine = az - coarse
        vals = [xp, xp + jnp.where(dx >= 0, 1.0, -1.0), zp - 1.0, zp - 1.0 + jnp.where(dz >= 0, 1.0, -1.0)]
        vals += [1.0 - coarse, coarse, -fine, fine]
        for j in range(2):
            mj = m * (jnp.where(y == j, 1.0 - ay, 0.0) + jnp.where(y1 == j, ay, 0.0))
            for w in (1.0 - ax, ax):
                vals += list(halves(mj * w))
        for n, v in enumerate(vals):
            val_ref[slot, n, 0:rows] = v

    def operands(slot, r):
        def row(n):
            return jnp.broadcast_to(val_ref[slot, n, r : r + 1, :].astype(BF), (16, 128))

        x0, x1, z0, z1 = (row(n) for n in range(4))
        near = [row(8 + 4 * (c // 2) + c % 2) for c in range(4)]
        far = [row(10 + 4 * (c // 2) + c % 2) for c in range(4)]
        a = [[] for _ in range(4)]
        for g in range(8):
            cell = grid + float(16 * g + 1)
            first, second = cell == x0, cell == x1
            for c in range(4):
                a[c].append(spread(first, second, near[c], far[c]))
        w = far[3]
        for c in range(3):
            w = jnp.where(ghost_row == float(c), far[c], w)
        a = a[0] + a[1] + a[2] + a[3] + [jnp.where(ghost_cell == x1, w, jnp.zeros((), BF))]
        zc, zf = [], []
        weights = [row(n) for n in range(4, 8)]
        for g in range(8):
            cell = grid + float(16 * g)
            first, second = cell == z0, cell == z1
            zc.append(spread(first, second, weights[0], weights[1]))
            zf.append(spread(first, second, weights[2], weights[3]))
        return jnp.concatenate(a, axis=0), jnp.concatenate(zc + zf, axis=0)

    def source(i, slot):
        prepare(i, slot)
        o = None
        for t in range((rows + 1) // 2):
            pairs = [operands(slot, r) for r in range(2 * t, min(2 * t + 2, rows))]
            a = jnp.concatenate([pair[0] for pair in pairs], axis=1)
            z = jnp.concatenate([pair[1] for pair in pairs], axis=1)
            d = lax.dot_general(a, z, (((1,), (1,)), ((), ())), preferred_element_type=F32)
            o = d if o is None else o + d
        ends = o[512:520, :128] + o[512:520, 128:]
        ends = ends + pltpu.roll(ends, 6, 0)
        for j in range(2):
            high, low = o[256 * j : 256 * j + 128], o[256 * j + 128 : 256 * j + 256]
            total = high[:, :128] + high[:, 128:] + low[:, :128]
            end = ends if j == 0 else pltpu.roll(ends, 4, 0)
            if acc_ref is not None:
                total = total + acc_ref[i, j, 0:128]
                end = end + acc_ref[i, j, 128:136]
            out_ref[i, j, 0:128] = total
            out_ref[i, j, 128:136] = end

    def step(b, carry):
        for u in range(together):
            source(b * together + u, u)
        return carry

    lax.fori_loop(0, GX // together, step, 0)


def paint_kernel(where_ref, recv_ref, out_ref, val_ref):
    paint_sources(ROWS, 2, None, where_ref, recv_ref, out_ref, val_ref)


def paint_more_kernel(where_ref, recv_ref, acc_ref, out_ref, val_ref):
    paint_sources(ROWS, 1, acc_ref, where_ref, recv_ref, out_ref, val_ref)


def paint_handed_kernel(where_ref, over_ref, recv_ref, acc_ref, out_ref, flag_ref, val_ref):
    flag_ref[0] = over_ref[0]

    @pl.when((where_ref[1] == 0) | (where_ref[1] == GX - 1))
    def _():
        flag_ref[0] = jnp.maximum(over_ref[0], flagged(recv_ref, 5 * FROWS + 6))
        paint_sources(FROWS, 4, acc_ref, where_ref, recv_ref, out_ref, val_ref)


def flagged(ref, row):
    flag = ref[0, row : row + 1, :]
    for i in range(1, GX):
        flag = jnp.maximum(flag, ref[i, row : row + 1, :])
    return jnp.max(jnp.where(lax.broadcasted_iota(I32, (1, 128), 1) >= 64, flag, 0.0)).astype(I32)


def paint_scratch(together):
    return [pltpu.VMEM((together, 16, 24, 128), F32)]


PAINTED = jax.ShapeDtypeStruct((GX, 2, XR, 128), F32)


def paint(where, recv):
    return pl.pallas_call(
        paint_kernel,
        out_shape=PAINTED,
        in_specs=[SM, VM],
        out_specs=VM,
        scratch_shapes=paint_scratch(2),
        name="paint",
        compiler_params=ROOM,
        cost_estimate=pl.CostEstimate(flops=60000000, bytes_accessed=2000000, transcendentals=0),
    )(where, recv)


def paint_more(where, recv, acc):
    return pl.pallas_call(
        paint_more_kernel,
        out_shape=PAINTED,
        in_specs=[SM, VM, VM],
        out_specs=VM,
        scratch_shapes=paint_scratch(1),
        input_output_aliases={2: 0},
        name="paint_more",
        compiler_params=ROOM,
    )(where, recv, acc)


def paint_handed(where, over, recv, acc):
    return pl.pallas_call(
        paint_handed_kernel,
        out_shape=(PAINTED, jax.ShapeDtypeStruct((1,), I32)),
        in_specs=[SM, SM, VM, VM],
        out_specs=(VM, SM),
        scratch_shapes=paint_scratch(4),
        input_output_aliases={3: 0},
        name="paint_handed",
        compiler_params=ROOM,
        cost_estimate=pl.CostEstimate(flops=30000000, bytes_accessed=2000000, transcendentals=0),
    )(where, over, recv, acc)


def face_kernel(count_ref, cell_ref, off_ref, mass_ref, low_ref, high_ref, val_ref):
    slot = lax.broadcasted_iota(I32, (NROW, 128), 0) * 128 + lax.broadcasted_iota(I32, (NROW, 128), 1)
    m = jnp.where(slot < count_ref[0], mass_ref[...], 0.0)
    dx, dy, dz = off_ref[0], off_ref[1], off_ref[2]
    xp, yp, zp = cells_of(cell_ref[...].astype(F32))
    up = (zp == 128.0) & (dz >= 0)
    down = (zp == 1.0) & (dz < 0)
    ax, ay = jnp.abs(dx), jnp.abs(dy)
    w = jnp.where(up | down, m * jnp.abs(dz), 0.0)
    coarse = jnp.floor(ax * 256.0) * (1.0 / 256.0)
    fine = ax - coarse
    y = yp + jnp.where(up, 24.0, 0.0)
    vals = [xp, xp + jnp.where(dx >= 0, 1.0, -1.0), 1.0 - coarse, coarse, -fine, fine]
    vals += [y, y + jnp.where(dy >= 0, 1.0, -1.0)]
    vals += [*halves(w * (1.0 - ay)), *halves(w * ay)]
    for n, v in enumerate(vals):
        val_ref[n] = v
    grid = counting(16)
    ghost = lax.broadcasted_iota(I32, (16, 128), 0)
    ghost_cell = jnp.where(ghost >= 4, 200, jnp.where((ghost & 1) == 0, 0, 129)).astype(F32).astype(BF)
    ghost_fine = (ghost >> 1).astype(F32).astype(BF) == 1.0

    def operands(r):
        def row(n):
            return jnp.broadcast_to(val_ref[n, pl.ds(r, 1), :].astype(BF), (16, 128))

        x0, x1, y0, y1 = row(0), row(1), row(6), row(7)
        weights = [row(n) for n in (2, 3, 4, 5, 8, 10, 9, 11)]
        xc, xf, high, low = [], [], [], []
        for g in range(8):
            cell = grid + float(16 * g + 1)
            first, second = cell == x0, cell == x1
            xc.append(spread(first, second, weights[0], weights[1]))
            xf.append(spread(first, second, weights[2], weights[3]))
        ends = jnp.where(ghost_cell == x1, jnp.where(ghost_fine, weights[3], weights[1]), jnp.zeros((), BF))
        for g in range(3):
            cell = grid + float(16 * g)
            first, second = cell == y0, cell == y1
            high.append(spread(first, second, weights[4], weights[5]))
            low.append(spread(first, second, weights[6], weights[7]))
        gap = [jnp.zeros((16, 128), BF)]
        return jnp.concatenate(xc + xf + [ends], axis=0), jnp.concatenate(high + gap + low + gap, axis=0)

    def step(b, total):
        for t in range(8):
            pairs = [operands(16 * b + 2 * t + u) for u in range(2)]
            x = jnp.concatenate([pair[0] for pair in pairs], axis=1)
            v = jnp.concatenate([pair[1] for pair in pairs], axis=1)
            total = total + lax.dot_general(x, v, (((1,), (1,)), ((), ())), preferred_element_type=F32)
        return total

    o = lax.fori_loop(0, NROW // 16, step, jnp.zeros((272, 128), F32))
    o = o + pltpu.roll(o, 64, 1)
    t = (o[0:128] + o[128:256]).T
    ends = o[256:264] + pltpu.roll(o[256:264], 6, 0)
    low_ref[0:24] = t[0:24]
    high_ref[0:24] = t[24:48]
    low_ref[24:32] = ends
    high_ref[24:32] = ends


def faces(count, cell, off, mass):
    shape = jax.ShapeDtypeStruct((32, 128), F32)
    return pl.pallas_call(
        face_kernel,
        out_shape=(shape, shape),
        in_specs=[SM, VM, VM, VM],
        out_specs=(VM, VM),
        scratch_shapes=[pltpu.VMEM((12, NROW, 128), F32)],
        name="faces",
        compiler_params=ROOM,
        cost_estimate=pl.CostEstimate(flops=8000000, bytes_accessed=200000, transcendentals=0),
    )(count, cell, off, mass)


def forward_kernel(where_ref, recv_ref, table_ref, out_ref, over_ref):
    first = jnp.where(where_ref[1] == GX - 1, ROWS - FROWS, 0)
    for i in range(GX):
        for o in range(5):
            out_ref[i, o * FROWS : (o + 1) * FROWS, :] = recv_ref[i, pl.ds(o * ROWS + first, FROWS), :]
        out_ref[i, 5 * FROWS : 5 * FROWS + 8, :] = recv_ref[i, FACE : FACE + 8, :]
    over_ref[0] = flagged(recv_ref, FACE + 6)


def forward_pack(where, recv, table):
    return pl.pallas_call(
        forward_kernel,
        out_shape=(jax.ShapeDtypeStruct((GX, 5 * FROWS + 8, 128), F32), jax.ShapeDtypeStruct((1,), I32)),
        in_specs=[SM, VM, pl.BlockSpec(memory_space=pl.ANY)],
        out_specs=(VM, SM),
        name="forward_pack",
        compiler_params=ROOM,
        cost_estimate=pl.CostEstimate(flops=500000, bytes_accessed=600000, transcendentals=0),
    )(where, recv, table)


def table_kernel(high_ref, low_ref):
    scale = 1.0 / 32.0
    j = lax.broadcasted_iota(I32, (64, 128), 1)
    k8 = 8 * lax.broadcasted_iota(I32, (64, 128), 0)
    none = jnp.zeros((64, 128), F32)

    def turns(m):
        angle = (((k8 + m) * j) & 1023).astype(F32) * (2.0 * math.pi / 1024.0)
        return jnp.cos(angle) * scale, jnp.sin(angle) * scale

    for g, (m, w) in enumerate(((1, 7), (3, 5), (2, 6), (0, 4))):
        (c, s), (e, t) = turns(m), turns(w)
        if g < 3:
            parts = ((c, s), (-s, c), (e, -t), (-t, -e))
        else:
            parts = ((c, none), (-s, none), (none, e), (none, -t))
        for n, pair in enumerate(parts):
            for h, value in enumerate(pair):
                high = value.astype(BF)
                high_ref[g, 64 * n : 64 * n + 64, 128 * h : 128 * h + 128] = high
                low_ref[g, 64 * n : 64 * n + 64, 128 * h : 128 * h + 128] = (value - high.astype(F32)).astype(BF)


def tables():
    shape = jax.ShapeDtypeStruct((4, 256, 256), BF)
    return pl.pallas_call(
        table_kernel,
        out_shape=(shape, shape),
        out_specs=(VM, VM),
        name="tables",
        compiler_params=ROOM,
        cost_estimate=pl.CostEstimate(flops=8000000, bytes_accessed=1000000, transcendentals=0),
    )()


def final_kernel(where_ref, acc_ref, face_ref, in_ref, th_ref, tl_ref, dens_ref, spec_ref, x_ref):
    p = where_ref[1]
    first, last = p == 0, p == GX - 1
    lane1 = lax.broadcasted_iota(I32, (1, 128), 1)
    lane2 = lax.broadcasted_iota(I32, (2, 128), 1)

    def face_row(i, side, j):
        v = face_ref[i, FACE + 3 * side + j : FACE + 3 * side + j + 1, :]
        u = in_ref[i, 5 * FROWS + 3 * side + 2 : 5 * FROWS + 3 * side + 3, :]
        return v + jnp.where(first if j == 0 else last, u, 0.0)

    def ghosts(i):
        got = {}
        v, u = face_ref[i, FACE + 6 : FACE + 8, :], in_ref[i, 5 * FROWS + 6 : 5 * FROWS + 8, :]
        for side in range(2):
            base = 24 if side == 0 else 0
            for j in range(2):
                mine = jnp.where(lane2 == base + 2 * p + 1 + j, v, 0.0)
                handed = jnp.where((lane2 == base + (17 if j == 0 else 0)) & (first if j == 0 else last), u, 0.0)
                got[side, j] = jnp.sum(mine + handed, axis=1, keepdims=True)
        return got

    past = [ghosts(i) for i in range(GX)]
    wide = lax.broadcasted_iota(I32, (128, 128), 1)
    for i in range(GX):
        before, after = (i - 1) % GX, (i + 1) % GX
        rows = {}
        for side in range(2):
            for j in range(2):
                v = face_row(i, side, j)
                v = v + jnp.where(lane1 == 127, past[after][side, j][0:1], 0.0)
                rows[side, j] = v + jnp.where(lane1 == 0, past[before][side, j][1:2], 0.0)
        gap = jnp.zeros((4, 128), F32)
        cols = jnp.concatenate(
            [rows[0, 0], rows[0, 1], gap[:2], jnp.zeros((120, 128), F32), gap[:2], rows[1, 0], rows[1, 1]], axis=0
        ).T
        for j in range(2):
            shifted = pltpu.roll(cols, 1 if j == 0 else 127, 1)
            v = acc_ref[i, j, 0:128, :]
            if j == 0:
                v = v + jnp.where(wide == 0, cols, jnp.where(wide == 127, shifted, 0.0))
            else:
                v = v + jnp.where(wide == 127, cols, jnp.where(wide == 0, shifted, 0.0))
            x_ref[i, :, j * 128 : (j + 1) * 128] = v
            x_ref[i, 127:128, j * 128 : (j + 1) * 128] = v[127:128] + acc_ref[after, j, 128:129, :]
            x_ref[i, 0:1, j * 128 : (j + 1) * 128] = v[0:1] + acc_ref[before, j, 129:130, :]
            dens_ref[pl.ds(i * 256 + j, 128, stride=2), :] = x_ref[i, :, j * 128 : (j + 1) * 128]

    def even(b):
        return x_ref[b] + x_ref[b + 4]

    def odd(b):
        return x_ref[b] - x_ref[b + 4]

    root = math.sqrt(0.5)
    for g, (m, w) in enumerate(((1, 7), (3, 5), (2, 6), (0, 4))):
        if g < 2:
            d1, d3 = odd(1), odd(3)
            s, t = (d1 - d3) * root, (d1 + d3) * root
            pair = (odd(0) + s, -odd(2) - t) if g == 0 else (odd(0) - s, odd(2) - t)
        elif g == 2:
            pair = (even(0) - even(2), even(3) - even(1))
        else:
            s, t = even(0) + even(2), even(1) + even(3)
            pair = (s + t, s - t)
        value = jnp.concatenate(pair, axis=0)
        high = value.astype(BF)
        low = (value - high.astype(F32)).astype(BF)
        o = jnp.dot(th_ref[g], high, preferred_element_type=F32)
        o = o + jnp.dot(tl_ref[g], high, preferred_element_type=F32)
        o = o + jnp.dot(th_ref[g], low, preferred_element_type=F32)
        for n, (k, part) in enumerate(((m, 0), (m, 1), (w, 0), (w, 1))):
            for j in range(2):
                spec_ref[pl.ds(part * 1024 + 2 * k + j, 64, stride=16), :] = o[64 * n : 64 * n + 64, j * 128 : (j + 1) * 128]


def finish(where, acc, face, received, th, tl):
    shape = jax.ShapeDtypeStruct((2048, 128), F32)
    return pl.pallas_call(
        final_kernel,
        out_shape=(shape, shape),
        in_specs=[SM] + [VM] * 5,
        out_specs=(VM, VM),
        scratch_shapes=[pltpu.VMEM((GX, 128, 256), F32)],
        name="finish",
        compiler_params=ROOM,
        cost_estimate=pl.CostEstimate(flops=400000000, bytes_accessed=4000000, transcendentals=0),
    )(where, acc, face, received, th, tl)


def y_pairs(blocks):
    pairs = []
    for q in range(blocks):
        pairs.append(((GX - 1) * blocks + q, (q + 1) % blocks))
        pairs.append((q, (GX - 1) * blocks + (q - 1) % blocks))
    return pairs


def exchange(x):
    return lax.all_to_all(x, "gx", split_axis=0, concat_axis=0, tiled=False)


def hand_on(x):
    return lax.ppermute(x, ("gx", "gy"), y_pairs(lax.axis_size("gy")))


def later_window(ordered, count, turn):
    xp, yp, zp = cells_of(ordered[0])
    live = ordered[4] != 0.0
    key = jnp.where(live, jnp.where(ordered[2] >= 0, yp, yp - 1.0), 20.0)
    space = jnp.zeros((5, NROW + 3 * ROWS, 128), F32)
    padded = jnp.concatenate([space, ordered, space], axis=1)
    base = NROW + 3 * ROWS
    blocks = []
    for p in range(GX):
        if p < GX - 1:
            begin = jnp.sum(jnp.where(key < 2 * p, 1, 0))
            w = jnp.minimum(begin // 128, NROW - ROWS) + turn * ROWS
        else:
            w = jnp.clip((count + 127) // 128 - ROWS, 0, NROW - ROWS) - turn * ROWS
        part = lax.dynamic_slice_in_dim(padded, base + w, ROWS, axis=1).reshape(5 * ROWS, 128)
        blocks.append(jnp.concatenate([part, jnp.zeros((PAYROWS - 5 * ROWS, 128), F32)], axis=0))
    return jnp.stack(blocks)


def body(cell_index, offsets, mass, counts):
    p = lax.axis_index("gx")
    blocks = lax.axis_size("gz")
    cell, off, m, count = cell_index.reshape(NROW, 128), offsets.reshape(3, NROW, 128), mass.reshape(NROW, 128), counts.reshape(1)
    here = jnp.stack([2 * p, p]).astype(I32)
    there = jnp.stack([jnp.where(p == 0, 16, -2), p]).astype(I32)

    low, high = faces(count, cell, off, m)
    from_below = lax.ppermute(high, "gz", [(i, (i + 1) % blocks) for i in range(blocks)])
    from_above = lax.ppermute(low, "gz", [((i + 1) % blocks, i) for i in range(blocks)])
    ordered, start = sort_particles(count, cell, off, m)
    recv = exchange(pack(start, ordered, from_below, from_above))
    th, tl = tables()

    packed, mine = forward_pack(here, recv, th)
    passed = hand_on(packed)
    acc = paint(here, recv)
    acc, over = paint_handed(there, mine, passed, acc)

    def slow(acc):
        later = lax.cond(
            mine[0] > 0,
            lambda: jnp.stack([exchange(later_window(ordered, count[0], t)) for t in (1, 2, 3)]),
            lambda: jnp.zeros((3,) + recv.shape, F32),
        )
        first = jnp.where(p == GX - 1, ROWS - FROWS, 0)
        row = lax.broadcasted_iota(I32, (PAYROWS, 128), 0) - 4 * ROWS
        sent = (row >= first) & (row < first + FROWS)
        rest = jnp.where(sent, 0.0, recv)
        for t in range(3):
            acc = paint_more(here, later[t], acc)
        for x in [rest] + [later[t] for t in range(3)]:
            acc = paint_more(there, hand_on(x), acc)
        return acc

    acc = lax.cond(over[0] > 0, slow, lambda a: a, acc)
    density, spectrum = finish(here, acc, recv, passed, th, tl)
    return density.reshape(1024, 1, 2, 128), spectrum.reshape(2, 512, 1, 2, 128)


def solution(mesh):
    placed = (
        P("gx", "gy", "gz", None),
        P("gx", "gy", "gz", None, None),
        P("gx", "gy", "gz", None),
        P("gx", "gy", "gz"),
    )
    return jax.shard_map(
        body,
        mesh=mesh,
        in_specs=placed,
        out_specs=(P(None, "gx", "gy", "gz"), P(None, None, "gx", "gy", "gz")),
        check_vma=False,
    )
```

time: 106 us -> 77.9 us (0.73)
  Pallas kernels: 40.8 us -> 23.4 us
  starting transfers between devices: 42.2 us -> 32.8 us
    pallas_call x5, Pallas kernels: 25.4 us -> 17.2 us  [the longest x1 6.73 us: paint(): pl.pallas_call(paint_kernel, out_shape=PAINTED, in_specs=[SM, VM], out_sp...]
    ppermute x1, starting transfers between devices: 20.4 us -> 15.3 us  [hand_on(): return lax.ppermute(x, ('gx', 'gy'), y_pairs(lax.axis_size('gy')))]
    all_to_all x2 -> x1, starting transfers between devices: 7.65 us -> 3.45 us  [exchange(): return lax.all_to_all(x, 'gx', split_axis=0, concat_axis=0, tiled=False)]
    pallas_call x1, Pallas kernels: 6.69 us -> 2.97 us  [finish(): pl.pallas_call(final_kernel, out_shape=(shape, shape), in_specs=[SM] + [V...]
    pallas_call x1, Pallas kernels: 4.01 us -> 1.13 us  [tables(): pl.pallas_call(table_kernel, out_shape=(shape, shape), out_specs=(VM, VM)...]
    pallas_call x1, Pallas kernels: 4.75 us -> 2.16 us  [faces(): pl.pallas_call(face_kernel, out_shape=(shape, shape), in_specs=[SM, VM, V...]
    unnamed x8 -> x6, local copies, waits for them, and re-layouts: 1.05 us -> 2.4 us
    slice x2 -> x0, local copies, waits for them, and re-layouts: 1.23 us -> none  [the longest x1 0.68 us: body(): acc = paint(there, passed[:, :40], acc, rows=FROWS, skip=True)]
  transfers between devices with their start and end apart: 5 -> 4, of which waited for: 4 -> 1; matrix products, arithmetic and copies ran while one was open for 1% -> 0% of each run, Pallas kernels for 19% -> 14%
where the time goes in v2:
time: 77.9 us; the launch traced here: 77.3 us
  starting transfers between devices  32.8 us (42%)
  Pallas kernels  23.4 us (30%)
  waiting for transfers between devices  16.2 us (21%)
  local copies, waits for them, and re-layouts  2.4 us (3%)
  between operations  2.03 us (3%)
    all_to_all x1, waiting for transfers between devices, exchange(): return lax.all_to_all(x, 'gx', split_axis=0, concat_axis=0, tiled=False)  16.2 us
    ppermute x1, starting transfers between devices, hand_on(): return lax.ppermute(x, ('gx', 'gy'), y_pairs(lax.axis_size('gy')))  15.3 us
    ppermute x1, starting transfers between devices, body(): lax.ppermute(low, 'gz', [((i + 1) % blocks, i) for i in range(blocks)])  11.5 us
    pallas_call x1, Pallas kernels, paint(): pl.pallas_call(paint_kernel, out_shape=PAINTED, in_specs=[SM, VM], out_sp...  6.73 us
    pallas_call x1, Pallas kernels, paint_handed(): pl.pallas_call(paint_handed_kernel, out_shape=(PAINTED, jax.ShapeDtypeStr...  4.74 us
    all_to_all x1, starting transfers between devices, exchange(): return lax.all_to_all(x, 'gx', split_axis=0, concat_axis=0, tiled=False)  3.45 us
    pallas_call x1, Pallas kernels, sort_particles(): pl.pallas_call(sort_kernel, out_shape=(jax.ShapeDtypeStruct((5, NROW, 128...  3.19 us
    pallas_call x1, Pallas kernels, finish(): pl.pallas_call(final_kernel, out_shape=(shape, shape), in_specs=[SM] + [V...  2.97 us
  transfers between devices with their start and end apart: 4, of which 1 were waited for; matrix products, arithmetic and copies ran while one was open for 0% of the time, Pallas kernels for 14%

profile of v2, /device:TPU:1, one launch (start us, length us, event | category | flops | bytes accessed | tf_op | source)
XLA Modules:
  0.0 77.3 jit_solution(14520410378454905421)
XLA Ops:
  1.3 0.0 copy-start
  1.3 0.9 %copy-done = f32[1,1,1,3,8192]{4,2,3,1,0:T(1,128)S(1)} copy-done((f32[1,1,1,3,8192]{4,2,3,1,0:T(1,128)S(1)}, f32[1,1,1,3,8192]{4,2,3,1,0:T(1,128)}, u32[]{:S(2)}) %copy-start) | copy-done | bytes 98328
  2.2 0.0 copy-start.1
  2.2 0.8 copy-done.1
  2.9 0.0 copy-start.2
  2.9 0.8 copy-done.2
  3.7 2.2 %faces.1 = (f32[32,128]{1,0:T(8,128)S(1)}, f32[32,128]{1,0:T(8,128)S(1)}) custom-call(s32[1]{0:T(128)} %bitcast.89.count_ref, s32[64,128]{1,0:T(8,128)S(1)} %bitcast.92, f32[3,64,128]{2,1,0:T(8,128)S(1)} %bitcast.90, f32[64,128]{1,0:T(8,128)S(1)} %bitcast.94), custom_call_target="tpu_custom_call" | custom-call | flops 8000000 | bytes 200000 | tf_op jit(solution)/shard_map/faces/pallas_call | solution.py:396
  5.8 2.6 %collective-permute-start.4 = (f32[32,128]{1,0:T(8,128)S(1)}, f32[32,128]{1,0:T(8,128)S(1)}, u32[]{:S(2)}, u32[]{:S(2)}) collective-permute-start(f32[32,128]{1,0:T(8,128)S(1)} %get-tuple-element.60), channel_id=1, source_target_pairs={{0,1},{1,2},{2,3},{3,4},{4,5},{5,6},{6,7},{7,0},{8,9},{9,10},{10,1... | collective-permute-start | bytes 49160 | tf_op jit(solution)/shard_map/ppermute | solution.py:597
  8.4 11.5 %collective-permute-start.5 = (f32[32,128]{1,0:T(8,128)S(1)}, f32[32,128]{1,0:T(8,128)S(1)}, u32[]{:S(2)}, u32[]{:S(2)}) collective-permute-start(f32[32,128]{1,0:T(8,128)S(1)} %get-tuple-element.61), channel_id=1, source_target_pairs={{1,0},{2,1},{3,2},{4,3},{5,4},{6,5},{7,6},{0,7},{9,8},{10,9},{11,1... | collective-permute-start | bytes 49160 | tf_op jit(solution)/shard_map/ppermute | solution.py:598
  20.0 3.2 %sort_particles.1 = (f32[5,64,128]{2,1,0:T(8,128)S(1)}, s32[9]{0:T(128)S(1)}) custom-call(s32[1]{0:T(128)} %bitcast.88.count_ref, s32[64,128]{1,0:T(8,128)S(1)} %bitcast.93, f32[3,64,128]{2,1,0:T(8,128)S(1)} %bitcast.91, f32[64,128]{1,0:T(8,128)S(1)} %bitcast.95), custom_call_target="tpu_custom_call" | custom-call | flops 30000000 | bytes 800000 | tf_op jit(solution)/shard_map/sort_particles/pallas_call | solution.py:135
  23.2 0.0 collective-permute-done.4.below_ref
  23.2 0.0 collective-permute-done.5.above_ref
  23.2 1.3 %pack.1 = f32[8,96,128]{2,1,0:T(8,128)} custom-call(s32[9]{0:T(128)S(1)} %get-tuple-element.58.start_ref, f32[5,64,128]{2,1,0:T(8,128)S(1)} %get-tuple-element.59.part_ref, f32[32,128]{1,0:T(8,128)S(1)} %collective-permute-done.4.below_ref, f32[32,128]{1,0:T(8,128)S(1)} %collective-permute-done.5.above_ref), custom_call_target="tpu_custom_call" | custom-call | flops 3000000 | bytes 600000 | tf_op jit(solution)/shard_map/pack/pallas_call | solution.py:161
  24.5 3.5 %all-to-all-start.3 = ((f32[8,96,128]{2,1,0:T(8,128)}), f32[8,96,128]{2,1,0:T(8,128)S(1)}, u32[]{:S(2)}, u32[]{:S(2)}) async-start(f32[8,96,128]{2,1,0:T(8,128)} %pack.1), calls=%async_computation.3 | async-start | bytes 786432 | tf_op jit(solution)/shard_map/all_to_all | solution.py:563
  28.0 1.1 %tables.1 = (bf16[4,256,256]{2,1,0:T(8,128)(2,1)S(1)}, bf16[4,256,256]{2,1,0:T(8,128)(2,1)S(1)}) custom-call(), custom_call_target="tpu_custom_call" | custom-call | flops 8000000 | bytes 1000000 | tf_op jit(solution)/shard_map/tables/pallas_call | solution.py:454
  29.1 0.1 pad_add_fusion.where_ref
  29.2 16.2 %all-to-all-done.3.recv_ref.face_ref = f32[8,96,128]{2,1,0:T(8,128)S(1)} async-done(((f32[8,96,128]{2,1,0:T(8,128)}), f32[8,96,128]{2,1,0:T(8,128)S(1)}, u32[]{:S(2)}, u32[]{:S(2)}) %all-to-all-start.3) | async-done | bytes 393248 | tf_op jit(solution)/shard_map/all_to_all | solution.py:563
  45.4 1.2 %forward_pack.1 = (f32[8,48,128]{2,1,0:T(8,128)S(1)}, s32[1]{0:T(128)}) custom-call(s32[2]{0:T(128)S(1)} %pad_add_fusion.where_ref, f32[8,96,128]{2,1,0:T(8,128)S(1)} %all-to-all-done.3.recv_ref.face_ref, bf16[4,256,256]{2,1,0:T(8,128)(2,1)S(1)} %get-tuple-element.62.table_ref.th_ref), custom_call_target="tpu_custom_call" | custom-call | flops 500000 | bytes 600000 | tf_op jit(solution)/shard_map/forward_pack/pallas_call | solution.py:418
  46.6 15.3 %collective-permute-start.6 = (f32[8,48,128]{2,1,0:T(8,128)S(1)}, f32[8,48,128]{2,1,0:T(8,128)S(1)}, u32[]{:S(2)}, u32[]{:S(2)}) collective-permute-start(f32[8,48,128]{2,1,0:T(8,128)S(1)} %get-tuple-element.64), channel_id=1, source_target_pairs={{896,8},{0,1016},{904,16},{8,896},{912,24},{16,904},{920,32},{24,9... | collective-permute-start | bytes 589832 | tf_op jit(solution)/shard_map/ppermute | solution.py:567
  61.9 0.1 pad_add_fusion.1.where_ref
  62.0 6.7 %paint.1.acc_ref = f32[8,2,136,128]{3,2,1,0:T(8,128)S(1)} custom-call(s32[2]{0:T(128)S(1)} %pad_add_fusion.where_ref, f32[8,96,128]{2,1,0:T(8,128)S(1)} %all-to-all-done.3.recv_ref.face_ref), custom_call_target="tpu_custom_call" | custom-call | flops 60000000 | bytes 2000000 | tf_op jit(solution)/shard_map/paint/pallas_call | solution.py:294
  68.7 0.0 collective-permute-done.6.recv_ref.in_ref
  68.7 4.7 %paint_handed.1 = (f32[8,2,136,128]{3,2,1,0:T(8,128)S(1)}, s32[1]{0:T(128)}) custom-call(s32[2]{0:T(128)S(1)} %pad_add_fusion.1.where_ref, s32[1]{0:T(128)} %get-tuple-element.63.over_ref, f32[8,48,128]{2,1,0:T(8,128)S(1)} %collective-permute-done.6.recv_ref.in_ref, f32[8,2,136,128]{3,2,1,0:T(8,128)S(1)} %paint.1.acc_ref), custom_call_target="tpu_custom_call", output_to_operand_aliasing={{0}: (3, {})} | custom-call | flops 30000000 | bytes 2000000 | tf_op jit(solution)/shard_map/paint_handed/pallas_call | solution.py:320
  74.1 0.2 conditional.2
  74.3 3.0 %finish.1 = (f32[2048,128]{1,0:T(8,128)}, f32[2048,128]{1,0:T(8,128)}) custom-call(s32[2]{0:T(128)S(1)} %pad_add_fusion.where_ref, f32[8,2,136,128]{3,2,1,0:T(8,128)S(1)} %get-tuple-element.117.acc_ref, f32[8,96,128]{2,1,0:T(8,128)S(1)} %all-to-all-done.3.recv_ref.face_ref, f32[8,48,128]{2,1,0:T(8,128)S(1)} %collective-permute-done.6.recv_ref.in_ref, ...), custom_call_target="tpu_custom_call" | custom-call | flops 400000000 | bytes 4000000 | tf_op jit(solution)/shard_map/finish/pallas_call | solution.py:542
Async XLA Ops:
  1.3 0.9 %copy-start = (f32[1,1,1,3,8192]{4,2,3,1,0:T(1,128)S(1)}, f32[1,1,1,3,8192]{4,2,3,1,0:T(1,128)}, u32[]{:S(2)}) copy-start(f32[1,1,1,3,8192]{4,2,3,1,0:T(1,128)} %param.9) | copy-start | bytes 294916
  2.2 0.8 copy-start.1
  2.9 0.8 copy-start.2
  5.8 17.3 %collective-permute-start.4 = (f32[32,128]{1,0:T(8,128)S(1)}, f32[32,128]{1,0:T(8,128)S(1)}, u32[]{:S(2)}, u32[]{:S(2)}) collective-permute-start(f32[32,128]{1,0:T(8,128)S(1)} %get-tuple-element.60), channel_id=1, source_target_pairs={{0,1},{1,2},{2,3},{3,4},{4,5},{5,6},{6,7},{7,0},{8,9},{9,10},{10,1... | collective-permute-start | bytes 49160 | tf_op jit(solution)/shard_map/ppermute | solution.py:597
  8.4 14.7 %collective-permute-start.5 = (f32[32,128]{1,0:T(8,128)S(1)}, f32[32,128]{1,0:T(8,128)S(1)}, u32[]{:S(2)}, u32[]{:S(2)}) collective-permute-start(f32[32,128]{1,0:T(8,128)S(1)} %get-tuple-element.61), channel_id=1, source_target_pairs={{1,0},{2,1},{3,2},{4,3},{5,4},{6,5},{7,6},{0,7},{9,8},{10,9},{11,1... | collective-permute-start | bytes 49160 | tf_op jit(solution)/shard_map/ppermute | solution.py:598
  24.5 20.9 %all-to-all-start.3 = ((f32[8,96,128]{2,1,0:T(8,128)}), f32[8,96,128]{2,1,0:T(8,128)S(1)}, u32[]{:S(2)}, u32[]{:S(2)}) async-start(f32[8,96,128]{2,1,0:T(8,128)} %pack.1), calls=%async_computation.3 | async-start | bytes 786432 | tf_op jit(solution)/shard_map/all_to_all | solution.py:563
  46.6 22.1 %collective-permute-start.6 = (f32[8,48,128]{2,1,0:T(8,128)S(1)}, f32[8,48,128]{2,1,0:T(8,128)S(1)}, u32[]{:S(2)}, u32[]{:S(2)}) collective-permute-start(f32[8,48,128]{2,1,0:T(8,128)S(1)} %get-tuple-element.64), channel_id=1, source_target_pairs={{896,8},{0,1016},{904,16},{8,896},{912,24},{16,904},{920,32},{24,9... | collective-permute-start | bytes 589832 | tf_op jit(solution)/shard_map/ppermute | solution.py:567

commit v3 on v2

v3 whole, which is shorter than its diff:
```python
import functools
import math

import jax
import jax.numpy as jnp
from jax import lax
from jax.experimental import pallas as pl
from jax.experimental.pallas import tpu as pltpu
from jax.sharding import PartitionSpec as P

F32, I32, BF = jnp.float32, jnp.int32, jnp.bfloat16
GX = 8
ROWS = 17
FROWS = 8
NROW = 64
PAYROWS = 96
FACE = 5 * ROWS
XR = 136
LANE = {6: 64, 7: 1, 8: 2, 9: 4, 10: 8, 11: 16, 12: 32}
SUB = {3: 1, 4: 2, 5: 4}
CELL = (1 << 19) - 1
FULL = pltpu.CompilerParams(vmem_limit_bytes=60 * 1024 * 1024)
ROOM = pltpu.CompilerParams(vmem_limit_bytes=12 * 1024 * 1024)
VM = pl.BlockSpec(memory_space=pltpu.VMEM)
SM = pl.BlockSpec(memory_space=pltpu.SMEM)
ANY = pl.BlockSpec(memory_space=pl.ANY)


def cells_of(flat):
    row = jnp.floor((flat + 0.5) * (1.0 / 130.0))
    xp = jnp.floor((row + 0.5) * (1.0 / 18.0))
    return xp, row - 18.0 * xp, flat - 130.0 * row


def halves(value):
    high = value.astype(BF).astype(F32)
    return high, value - high


def index_bit(bit, lane, sub, reg):
    if bit < 3:
        return bool((reg >> bit) & 1)
    if bit in SUB:
        return (sub & SUB[bit]) != 0
    return (lane & LANE[bit]) != 0


def sort_network(ops, lane, sub):
    for size in range(1, 14):
        for bit in range(size - 1, -1, -1):
            new = [[None] * 8 for _ in ops]
            if bit < 3:
                for v in range(8):
                    w = v | (1 << bit)
                    if v == w:
                        continue
                    down = False if size == 13 else index_bit(size, lane, sub, v)
                    a, c = ops[0][v], ops[0][w]
                    if down is True:
                        move = a < c
                    elif down is False:
                        move = a > c
                    else:
                        move = ((a > c) ^ down) & (a != c)
                    for o in range(len(ops)):
                        a, c = ops[o][v], ops[o][w]
                        new[o][v] = jnp.where(move, c, a)
                        new[o][w] = jnp.where(move, a, c)
            else:
                axis, step, index = (0, SUB[bit], sub) if bit in SUB else (1, LANE[bit], lane)
                upper = (index & step) != 0
                other = index ^ step

                def partner(x):
                    if 2 * step == x.shape[axis]:
                        return pltpu.roll(x, step, axis)
                    if axis == 0:
                        return jnp.where(upper, pltpu.roll(x, step, 0), pltpu.roll(x, 8 - step, 0))
                    return jnp.take_along_axis(x, other, axis=axis)

                for v in range(8):
                    down = False if size == 13 else index_bit(size, lane, sub, v)
                    mine, theirs = ops[0][v], partner(ops[0][v])
                    if down is True:
                        big = ~upper
                    elif down is False:
                        big = upper
                    else:
                        big = upper ^ down
                    move = ((theirs > mine) & big) | ((theirs < mine) & ~big)
                    new[0][v] = jnp.where(move, theirs, mine)
                    for o in range(1, len(ops)):
                        new[o][v] = jnp.where(move, partner(ops[o][v]), ops[o][v])
            ops = new
    return ops


def sort_and_pack(count, cell_ref, off_ref, mass_ref, low, high, ghosts, sorted_ref, pay_ref):
    lane = lax.broadcasted_iota(I32, (8, 128), 1)
    sub = lax.broadcasted_iota(I32, (8, 128), 0)
    below = [jnp.zeros((8, 128), F32) for _ in range(18)]
    ops = [[] for _ in range(5)]
    for v in range(8):
        s = slice(8 * v, 8 * v + 8)
        cell, dy = cell_ref[s, :], off_ref[1, s, :]
        live = v * 1024 + sub * 128 + lane < count
        _, yp, _ = cells_of(cell.astype(F32))
        row = jnp.where(live, jnp.where(dy >= 0, yp, yp - 1.0), 20.0)
        for t in range(1, 18):
            below[t] = below[t] + jnp.where(row < t, 1.0, 0.0)
        ops[0].append((row.astype(I32) << 19) | cell)
        for o in range(3):
            ops[o + 1].append(off_ref[o, s, :])
        ops[4].append(jnp.where(live, mass_ref[s, :], 0.0))
    below = [None] + [jnp.sum(b).astype(I32) for b in below[1:]]
    ops = sort_network(ops, lane, sub)
    ops[0] = [(k & CELL).astype(F32) for k in ops[0]]
    for o in range(5):
        t = jnp.concatenate(ops[o], axis=0).T
        sorted_ref[o] = jnp.concatenate([t[:64], t[64:]], axis=1)
    over = below[1] > FROWS * 128
    starts = []
    for p in range(GX):
        if p < GX - 1:
            begin = below[2 * p] if p else jnp.int32(0)
            w = jnp.minimum(begin >> 7, NROW - ROWS)
            over = over | (below[2 * p + 3] > 128 * (w + ROWS))
        else:
            w = jnp.clip(((below[17] + 127) >> 7) - ROWS, 0, NROW - ROWS)
            over = over | (below[2 * p] < 128 * w) | (below[2 * p + 2] < 128 * (w + ROWS - FROWS))
        starts.append(w)
    ghosts = jnp.where(lax.broadcasted_iota(I32, (2, 128), 1) < 64, ghosts, jnp.where(over, 1.0, 0.0))
    for p in range(GX):
        for o in range(5):
            pay_ref[p, o * ROWS : (o + 1) * ROWS, :] = sorted_ref[o, pl.ds(starts[p], ROWS), :]
        past = 17 if p == GX - 1 else 0
        rows = []
        for v in (low, high):
            rows += [v[2 * p + 1 : 2 * p + 3], v[past : past + 1]]
        pay_ref[p, FACE : FACE + 8, :] = jnp.concatenate(rows + [ghosts], axis=0)
        pay_ref[p, FACE + 8 : PAYROWS, :] = jnp.zeros((PAYROWS - FACE - 8, 128), F32)


def spread(first, second, one, two):
    return jnp.where(first, one, jnp.where(second, two, jnp.zeros((), BF)))


def counting(height, start=0):
    return (lax.broadcasted_iota(I32, (height, 128), 0) + start).astype(F32).astype(BF)


def paint_sources(rows, together, handed, acc_ref, recv_ref, out_ref, val_ref, begin=0, end=GX):
    p = lax.axis_index("gx")
    count = 1 if handed else 2
    grid = counting(16)
    ghost = lax.broadcasted_iota(I32, (16, 128), 0)
    ghost_cell = jnp.where(ghost >= 4 * count, 200, jnp.where((ghost & 1) == 0, 0, 129)).astype(F32).astype(BF)
    ghost_row = (ghost >> 1).astype(F32).astype(BF)

    def prepare(i, slot):
        def op(k):
            return recv_ref[i, k * rows : (k + 1) * rows, :]

        xp, yp, zp = cells_of(op(0))
        if handed:
            dx, dz, weights = op(1), op(2), [op(3)]
        else:
            dx, dy, dz, m = op(1), op(2), op(3), op(4)
            y = yp - (2 * p + 1).astype(F32)
            y1 = y + jnp.where(dy >= 0, 1.0, -1.0)
            ay = jnp.abs(dy)
            weights = [m * (jnp.where(y == j, 1.0 - ay, 0.0) + jnp.where(y1 == j, ay, 0.0)) for j in range(2)]
        ax, az = jnp.abs(dx), jnp.abs(dz)
        coarse = jnp.floor(az * 256.0) * (1.0 / 256.0)
        fine = az - coarse
        vals = [xp, xp + jnp.where(dx >= 0, 1.0, -1.0), zp - 1.0, zp - 1.0 + jnp.where(dz >= 0, 1.0, -1.0)]
        vals += [1.0 - coarse, coarse, -fine, fine]
        for mj in weights:
            for w in (1.0 - ax, ax):
                vals += list(halves(mj * w))
        for n, v in enumerate(vals):
            val_ref[slot, n, 0:rows] = v

    def operands(slot, r):
        def row(n):
            return jnp.broadcast_to(val_ref[slot, n, r : r + 1, :].astype(BF), (16, 128))

        x0, x1, z0, z1 = (row(n) for n in range(4))
        near = [row(8 + 4 * (c // 2) + c % 2) for c in range(2 * count)]
        far = [row(10 + 4 * (c // 2) + c % 2) for c in range(2 * count)]
        a = [[] for _ in range(2 * count)]
        for g in range(8):
            cell = grid + float(16 * g + 1)
            first, second = cell == x0, cell == x1
            for c in range(2 * count):
                a[c].append(spread(first, second, near[c], far[c]))
        w = far[-1]
        for c in range(2 * count - 1):
            w = jnp.where(ghost_row == float(c), far[c], w)
        a = sum(a, []) + [jnp.where(ghost_cell == x1, w, jnp.zeros((), BF))]
        zc, zf = [], []
        weights = [row(n) for n in range(4, 8)]
        for g in range(8):
            cell = grid + float(16 * g)
            first, second = cell == z0, cell == z1
            zc.append(spread(first, second, weights[0], weights[1]))
            zf.append(spread(first, second, weights[2], weights[3]))
        return jnp.concatenate(a, axis=0), jnp.concatenate(zc + zf, axis=0)

    def source(i, slot):
        prepare(i, slot)
        o = None
        for t in range((rows + 1) // 2):
            pairs = [operands(slot, r) for r in range(2 * t, min(2 * t + 2, rows))]
            a = jnp.concatenate([pair[0] for pair in pairs], axis=1)
            z = jnp.concatenate([pair[1] for pair in pairs], axis=1)
            d = lax.dot_general(a, z, (((1,), (1,)), ((), ())), preferred_element_type=F32)
            o = d if o is None else o + d
        ends = o[256 * count : 256 * count + 8, :128] + o[256 * count : 256 * count + 8, 128:]
        ends = ends + pltpu.roll(ends, 6, 0)
        for j in range(count):
            at = jnp.where(p == 0, 0, 1) if handed else j
            high, low = o[256 * j : 256 * j + 128], o[256 * j + 128 : 256 * j + 256]
            total = high[:, :128] + high[:, 128:] + low[:, :128]
            end = ends if j == 0 else pltpu.roll(ends, 4, 0)
            if acc_ref is not None:
                total = total + acc_ref[i, at, 0:128]
                end = end + acc_ref[i, at, 128:136]
            out_ref[i, at, 0:128] = total
            out_ref[i, at, 128:136] = end

    def step(b, carry):
        for u in range(together):
            source(b * together + u, u)
        return carry

    lax.fori_loop(begin // together, end // together, step, 0)


def waits_long():
    p = lax.axis_index("gx")
    return ((p == 0) | (p == GX - 1)) & (lax.axis_index("gy") % 4 == 0)


def paint_early_kernel(recv_ref, out_ref, val_ref):
    @pl.when(waits_long())
    def _():
        paint_sources(ROWS, 2, False, None, recv_ref, out_ref, val_ref, 0, EARLY)


def paint_late_kernel(recv_ref, after_ref, acc_ref, out_ref, val_ref):
    begin = jnp.where(waits_long(), EARLY, 0)
    paint_sources(ROWS, 2, False, None, recv_ref, out_ref, val_ref, begin)


def paint_more_kernel(handed, recv_ref, acc_ref, out_ref, val_ref):
    if handed:
        out_ref[...] = acc_ref[...]

        @pl.when((lax.axis_index("gx") == 0) | (lax.axis_index("gx") == GX - 1))
        def _():
            paint_sources(ROWS, 1, handed, acc_ref, recv_ref, out_ref, val_ref)
    else:
        paint_sources(ROWS, 1, handed, acc_ref, recv_ref, out_ref, val_ref)


def flagged(ref, row):
    flag = ref[0, row : row + 1, :]
    for i in range(1, GX):
        flag = jnp.maximum(flag, ref[i, row : row + 1, :])
    return jnp.max(jnp.where(lax.broadcasted_iota(I32, (1, 128), 1) >= 64, flag, 0.0)).astype(I32)


def paint_scratch(together):
    return [pltpu.VMEM((together, 16, 24, 128), F32)]


EARLY = 8
PAINTED = jax.ShapeDtypeStruct((GX, 2, XR, 128), F32)
PAINT_COST = pl.CostEstimate(flops=60000000, bytes_accessed=2000000, transcendentals=0)


def paint_early(recv):
    return pl.pallas_call(
        paint_early_kernel,
        out_shape=PAINTED,
        in_specs=[VM],
        out_specs=VM,
        scratch_shapes=paint_scratch(2),
        name="paint_early",
        compiler_params=ROOM,
        cost_estimate=PAINT_COST,
    )(recv)


def paint_late(recv, after, acc):
    return pl.pallas_call(
        paint_late_kernel,
        out_shape=PAINTED,
        in_specs=[VM, ANY, VM],
        out_specs=VM,
        scratch_shapes=paint_scratch(2),
        input_output_aliases={2: 0},
        name="paint_late",
        compiler_params=ROOM,
        cost_estimate=PAINT_COST,
    )(recv, after, acc)


def paint_more(recv, acc, handed=False):
    return pl.pallas_call(
        functools.partial(paint_more_kernel, handed),
        out_shape=PAINTED,
        in_specs=[VM, VM],
        out_specs=VM,
        scratch_shapes=paint_scratch(1),
        input_output_aliases={1: 0},
        name="paint_more",
        compiler_params=ROOM,
    )(recv, acc)


def paint_faces(count, cell_ref, off_ref, mass_ref, val_ref):
    slot = lax.broadcasted_iota(I32, (NROW, 128), 0) * 128 + lax.broadcasted_iota(I32, (NROW, 128), 1)
    m = jnp.where(slot < count, mass_ref[...], 0.0)
    dx, dy, dz = off_ref[0], off_ref[1], off_ref[2]
    xp, yp, zp = cells_of(cell_ref[...].astype(F32))
    up = (zp == 128.0) & (dz >= 0)
    down = (zp == 1.0) & (dz < 0)
    ax, ay = jnp.abs(dx), jnp.abs(dy)
    w = jnp.where(up | down, m * jnp.abs(dz), 0.0)
    coarse = jnp.floor(ax * 256.0) * (1.0 / 256.0)
    fine = ax - coarse
    y = yp + jnp.where(up, 24.0, 0.0)
    vals = [xp, xp + jnp.where(dx >= 0, 1.0, -1.0), 1.0 - coarse, coarse, -fine, fine]
    vals += [y, y + jnp.where(dy >= 0, 1.0, -1.0)]
    vals += [*halves(w * (1.0 - ay)), *halves(w * ay)]
    for n, v in enumerate(vals):
        val_ref[n] = v
    grid = counting(16)
    ghost = lax.broadcasted_iota(I32, (16, 128), 0)
    ghost_cell = jnp.where(ghost >= 4, 200, jnp.where((ghost & 1) == 0, 0, 129)).astype(F32).astype(BF)
    ghost_fine = (ghost >> 1).astype(F32).astype(BF) == 1.0

    def operands(r):
        def row(n):
            return jnp.broadcast_to(val_ref[n, pl.ds(r, 1), :].astype(BF), (16, 128))

        x0, x1, y0, y1 = row(0), row(1), row(6), row(7)
        weights = [row(n) for n in (2, 3, 4, 5, 8, 10, 9, 11)]
        xc, xf, high, low = [], [], [], []
        for g in range(8):
            cell = grid + float(16 * g + 1)
            first, second = cell == x0, cell == x1
            xc.append(spread(first, second, weights[0], weights[1]))
            xf.append(spread(first, second, weights[2], weights[3]))
        ends = jnp.where(ghost_cell == x1, jnp.where(ghost_fine, weights[3], weights[1]), jnp.zeros((), BF))
        for g in range(3):
            cell = grid + float(16 * g)
            first, second = cell == y0, cell == y1
            high.append(spread(first, second, weights[4], weights[5]))
            low.append(spread(first, second, weights[6], weights[7]))
        gap = [jnp.zeros((16, 128), BF)]
        return jnp.concatenate(xc + xf + [ends], axis=0), jnp.concatenate(high + gap + low + gap, axis=0)

    def step(b, total):
        for t in range(8):
            pairs = [operands(16 * b + 2 * t + u) for u in range(2)]
            x = jnp.concatenate([pair[0] for pair in pairs], axis=1)
            v = jnp.concatenate([pair[1] for pair in pairs], axis=1)
            total = total + lax.dot_general(x, v, (((1,), (1,)), ((), ())), preferred_element_type=F32)
        return total

    o = lax.fori_loop(0, NROW // 16, step, jnp.zeros((272, 128), F32))
    o = o + pltpu.roll(o, 64, 1)
    t = (o[0:128] + o[128:256]).T
    ends = o[256:264] + pltpu.roll(o[256:264], 6, 0)
    return t[0:24], t[24:48], ends[0:2]


def front_kernel(count_ref, cell_ref, off_ref, mass_ref, sorted_ref, pay_ref, val_ref):
    count = count_ref[0, 0, 0]
    low, high, ghosts = paint_faces(count, cell_ref, off_ref, mass_ref, val_ref)
    sort_and_pack(count, cell_ref, off_ref, mass_ref, low, high, ghosts, sorted_ref, pay_ref)


def front(count, cell, off, mass):
    return pl.pallas_call(
        front_kernel,
        out_shape=(jax.ShapeDtypeStruct((5, NROW, 128), F32), jax.ShapeDtypeStruct((GX, PAYROWS, 128), F32)),
        in_specs=[SM, VM, VM, VM],
        out_specs=(VM, VM),
        scratch_shapes=[pltpu.VMEM((12, NROW, 128), F32)],
        name="front",
        compiler_params=FULL,
        cost_estimate=pl.CostEstimate(flops=40000000, bytes_accessed=1000000, transcendentals=0),
    )(count, cell, off, mass)


def forward_kernel(recv_ref, table_ref, acc_ref, out_ref):
    last = lax.axis_index("gx") == GX - 1
    first = jnp.where(last, ROWS - FROWS, 0)
    row = jnp.where(last, 17.0, 0.0)
    for i in range(GX):
        cell, dx, dy, dz, m = (recv_ref[i, pl.ds(o * ROWS + first, FROWS), :] for o in range(5))
        _, yp, _ = cells_of(cell)
        ay = jnp.abs(dy)
        near = jnp.where(yp == row, 1.0 - ay, 0.0)
        weight = m * (near + jnp.where(yp + jnp.where(dy >= 0, 1.0, -1.0) == row, ay, 0.0))
        for o, v in enumerate((cell, dx, dz, weight)):
            out_ref[i, o * FROWS : (o + 1) * FROWS, :] = v
        out_ref[i, 4 * FROWS : 4 * FROWS + 8, :] = recv_ref[i, FACE : FACE + 8, :]


def forward_pack(recv, table, acc):
    return pl.pallas_call(
        forward_kernel,
        out_shape=jax.ShapeDtypeStruct((GX, 4 * FROWS + 8, 128), F32),
        in_specs=[VM, ANY, ANY],
        out_specs=VM,
        name="forward_pack",
        compiler_params=ROOM,
        cost_estimate=pl.CostEstimate(flops=500000, bytes_accessed=600000, transcendentals=0),
    )(recv, table, acc)


def table_kernel(high_ref, low_ref):
    scale = 1.0 / 32.0
    j = lax.broadcasted_iota(I32, (64, 128), 1)
    k8 = 8 * lax.broadcasted_iota(I32, (64, 128), 0)
    none = jnp.zeros((64, 128), F32)

    def turns(m):
        angle = (((k8 + m) * j) & 1023).astype(F32) * (2.0 * math.pi / 1024.0)
        return jnp.cos(angle) * scale, jnp.sin(angle) * scale

    for g, (m, w) in enumerate(((1, 7), (3, 5), (2, 6), (0, 4))):
        (c, s), (e, t) = turns(m), turns(w)
        if g < 3:
            parts = ((c, s), (-s, c), (e, -t), (-t, -e))
        else:
            parts = ((c, none), (-s, none), (none, e), (none, -t))
        for n, pair in enumerate(parts):
            for h, value in enumerate(pair):
                high = value.astype(BF)
                high_ref[g, 64 * n : 64 * n + 64, 128 * h : 128 * h + 128] = high
                low_ref[g, 64 * n : 64 * n + 64, 128 * h : 128 * h + 128] = (value - high.astype(F32)).astype(BF)


def tables():
    shape = jax.ShapeDtypeStruct((4, 256, 256), BF)
    return pl.pallas_call(
        table_kernel,
        out_shape=(shape, shape),
        out_specs=(VM, VM),
        name="tables",
        compiler_params=ROOM,
        cost_estimate=pl.CostEstimate(flops=8000000, bytes_accessed=1000000, transcendentals=0),
    )()


GROUPS = ((1, 7), (3, 5), (2, 6), (0, 4))


def transform(field, th_ref, tl_ref, put):
    root = math.sqrt(0.5)

    def even(b):
        return field(b) + field(b + 4)

    def odd(b):
        return field(b) - field(b + 4)

    for g in range(4):
        if g < 2:
            d1, d3 = odd(1), odd(3)
            s, t = (d1 - d3) * root, (d1 + d3) * root
            pair = (odd(0) + s, -odd(2) - t) if g == 0 else (odd(0) - s, odd(2) - t)
        elif g == 2:
            pair = (even(0) - even(2), even(3) - even(1))
        else:
            s, t = even(0) + even(2), even(1) + even(3)
            pair = (s + t, s - t)
        value = jnp.concatenate(pair, axis=0)
        high = value.astype(BF)
        low = (value - high.astype(F32)).astype(BF)
        o = jnp.dot(th_ref[g], high, preferred_element_type=F32)
        o = o + jnp.dot(tl_ref[g], high, preferred_element_type=F32)
        put(g, o + jnp.dot(th_ref[g], low, preferred_element_type=F32))


def face_columns(i, rows, ghosts):
    before, after = (i - 1) % GX, (i + 1) % GX
    lane = lax.broadcasted_iota(I32, (1, 128), 1)
    out = []
    for side in range(2):
        v = rows[i][side] + jnp.where(lane == 127, ghosts[after][side][0:1], 0.0)
        out.append(v + jnp.where(lane == 0, ghosts[before][side][1:2], 0.0))
    return out


def pick(v, lane):
    return jnp.sum(jnp.where(lax.broadcasted_iota(I32, (2, 128), 1) == lane, v, 0.0), axis=1, keepdims=True)


def along_z_kernel(face_ref, in_ref, down_ref, up_ref):
    p = lax.axis_index("gx")
    for j in range(2):
        on = p == (0 if j == 0 else GX - 1)
        rows, ghosts = [], []
        for i in range(GX):
            own, handed = face_ref[i, FACE : FACE + 8, :], in_ref[i, 4 * FROWS : 4 * FROWS + 8, :]
            rows.append([own[3 * n + j : 3 * n + j + 1] + jnp.where(on, handed[3 * n + 2 : 3 * n + 3], 0.0) for n in range(2)])
            past = [pick(own[6:8], base + 2 * p + 1 + j) for base in (0, 24)]
            more = [pick(handed[6:8], base + (17 if j == 0 else 0)) for base in (0, 24)]
            ghosts.append([a + jnp.where(on, b, 0.0) for a, b in zip(past, more)])
        for i in range(GX):
            down, up = face_columns(i, rows, ghosts)
            down_ref[2 * i + j : 2 * i + j + 1] = down
            up_ref[2 * i + j : 2 * i + j + 1] = up


def along_z(recv, passed):
    shape = jax.ShapeDtypeStruct((2 * GX, 128), F32)
    return pl.pallas_call(
        along_z_kernel,
        out_shape=(shape, shape),
        in_specs=[VM, VM],
        out_specs=(VM, VM),
        name="along_z",
        compiler_params=ROOM,
        cost_estimate=pl.CostEstimate(flops=500000, bytes_accessed=100000, transcendentals=0),
    )(recv, passed)


def handed_kernel(in_ref, acc_ref, out_ref, val_ref):
    p = lax.axis_index("gx")

    @pl.when((p == 0) | (p == GX - 1))
    def _():
        paint_sources(FROWS, 4, True, acc_ref, in_ref, out_ref, val_ref)


def paint_handed(passed, acc):
    return pl.pallas_call(
        handed_kernel,
        out_shape=PAINTED,
        in_specs=[VM, VM],
        out_specs=VM,
        scratch_shapes=paint_scratch(4),
        input_output_aliases={1: 0},
        name="paint_handed",
        compiler_params=ROOM,
        cost_estimate=PAINT_COST,
    )(passed, acc)


def finish_kernel(acc_ref, face_ref, in_ref, below_ref, above_ref, th_ref, tl_ref, dens_ref, spec_ref, flag_ref, x_ref):
    p = lax.axis_index("gx")
    flag_ref[0] = flagged(face_ref, FACE + 6)

    @pl.when((p == 0) | (p == GX - 1))
    def _():
        flag_ref[0] = jnp.maximum(flag_ref[0], flagged(in_ref, 4 * FROWS + 6))

    wide = lax.broadcasted_iota(I32, (128, 128), 1)
    for i in range(GX):
        before, after = (i - 1) % GX, (i + 1) % GX
        gap = jnp.zeros((124, 128), F32)
        t = jnp.concatenate([below_ref[2 * i : 2 * i + 2], gap, above_ref[2 * i : 2 * i + 2]], axis=0).T
        for j in range(2):
            shifted = pltpu.roll(t, 1 if j == 0 else 127, 1)
            low, high = (t, shifted) if j == 0 else (shifted, t)
            v = acc_ref[i, j, 0:128, :] + jnp.where(wide == 0, low, jnp.where(wide == 127, high, 0.0))
            cols = slice(j * 128, (j + 1) * 128)
            x_ref[i, :, cols] = v
            x_ref[i, 127:128, cols] = v[127:128] + acc_ref[after, j, 128:129, :]
            x_ref[i, 0:1, cols] = v[0:1] + acc_ref[before, j, 129:130, :]
            dens_ref[pl.ds(i * 256 + j, 128, stride=2), :] = x_ref[i, :, cols]

    def put(g, o):
        m, w = GROUPS[g]
        for n, (k, part) in enumerate(((m, 0), (m, 1), (w, 0), (w, 1))):
            for j in range(2):
                spec_ref[pl.ds(part * 1024 + 2 * k + j, 64, stride=16), :] = o[64 * n : 64 * n + 64, j * 128 : (j + 1) * 128]

    transform(lambda b: x_ref[b], th_ref, tl_ref, put)


def finish(acc, recv, passed, below, above, th, tl):
    shape = jax.ShapeDtypeStruct((2048, 128), F32)
    return pl.pallas_call(
        finish_kernel,
        out_shape=(shape, shape, jax.ShapeDtypeStruct((1,), I32)),
        in_specs=[VM] * 7,
        out_specs=(VM, VM, SM),
        scratch_shapes=[pltpu.VMEM((GX, 128, 256), F32)],
        name="finish",
        compiler_params=ROOM,
        cost_estimate=pl.CostEstimate(flops=400000000, bytes_accessed=4000000, transcendentals=0),
    )(acc, recv, passed, below, above, th, tl)


def y_pairs(blocks):
    pairs = []
    for q in range(blocks):
        pairs.append(((GX - 1) * blocks + q, (q + 1) % blocks))
        pairs.append((q, (GX - 1) * blocks + (q - 1) % blocks))
    return pairs


def exchange(x):
    return lax.all_to_all(x, "gx", split_axis=0, concat_axis=0, tiled=False)


def hand_on(x):
    return lax.ppermute(x, ("gx", "gy"), y_pairs(lax.axis_size("gy")))


def weighted(block):
    cell, dx, dy, dz, m = (block[:, o * ROWS : (o + 1) * ROWS] for o in range(5))
    row = jnp.where(lax.axis_index("gx") == GX - 1, 17.0, 0.0)
    _, yp, _ = cells_of(cell)
    ay = jnp.abs(dy)
    far = yp + jnp.where(dy >= 0, 1.0, -1.0)
    weight = m * (jnp.where(yp == row, 1.0 - ay, 0.0) + jnp.where(far == row, ay, 0.0))
    return jnp.concatenate([cell, dx, dz, weight, jnp.zeros((GX, PAYROWS - 4 * ROWS, 128), F32)], axis=1)


def later_window(ordered, turn):
    xp, yp, zp = cells_of(ordered[0])
    live = ordered[4] != 0.0
    key = jnp.where(live, jnp.where(ordered[2] >= 0, yp, yp - 1.0), 20.0)
    space = jnp.zeros((5, NROW + 3 * ROWS, 128), F32)
    padded = jnp.concatenate([space, ordered, space], axis=1)
    base = NROW + 3 * ROWS
    blocks = []
    for p in range(GX):
        if p < GX - 1:
            begin = jnp.sum(jnp.where(key < 2 * p, 1, 0))
            w = jnp.minimum(begin // 128, NROW - ROWS) + turn * ROWS
        else:
            w = jnp.clip((jnp.sum(jnp.where(live, 1, 0)) + 127) // 128 - ROWS, 0, NROW - ROWS) - turn * ROWS
        part = lax.dynamic_slice_in_dim(padded, base + w, ROWS, axis=1).reshape(5 * ROWS, 128)
        blocks.append(jnp.concatenate([part, jnp.zeros((PAYROWS - 5 * ROWS, 128), F32)], axis=0))
    return jnp.stack(blocks)


def body(cell_index, offsets, mass, counts):
    p = lax.axis_index("gx")
    blocks = lax.axis_size("gz")
    ordered, pay = front(counts, cell_index.reshape(NROW, 128), offsets.reshape(3, NROW, 128), mass.reshape(NROW, 128))
    recv = exchange(pay)
    th, tl = tables()

    acc = paint_early(recv)
    packed = forward_pack(recv, th, acc)
    passed = hand_on(packed)
    acc = paint_late(recv, packed, acc)
    down, up = along_z(recv, passed)
    below = lax.ppermute(up, "gz", [(i, (i + 1) % blocks) for i in range(blocks)])
    above = lax.ppermute(down, "gz", [((i + 1) % blocks, i) for i in range(blocks)])
    acc = paint_handed(passed, acc)
    density, spectrum, over = finish(acc, recv, passed, below, above, th, tl)

    def slow(outputs):
        mine = jnp.max(recv[:, FACE + 6, 64:]) > 0
        later = lax.cond(
            mine,
            lambda: tuple(exchange(later_window(ordered, t)) for t in (1, 2, 3)),
            lambda: (jnp.zeros(recv.shape, F32),) * 3,
        )
        first = jnp.where(p == GX - 1, ROWS - FROWS, 0)
        row = lax.broadcasted_iota(I32, (PAYROWS, 128), 0) - 4 * ROWS
        sent = (row >= first) & (row < first + FROWS)
        rest = jnp.where(sent, 0.0, recv)
        acc = jnp.zeros(PAINTED.shape, F32)
        for x in (recv, *later):
            acc = paint_more(x, acc)
        for x in (rest, *later):
            acc = paint_more(hand_on(weighted(x)), acc, handed=True)
        acc = paint_handed(passed, acc)
        density, spectrum, _ = finish(acc, recv, passed, below, above, th, tl)
        return density, spectrum

    density, spectrum = lax.cond(over[0] > 0, slow, lambda outputs: outputs, (density, spectrum))
    return density.reshape(1024, 1, 2, 128), spectrum.reshape(2, 512, 1, 2, 128)


def solution(mesh):
    placed = (
        P("gx", "gy", "gz", None),
        P("gx", "gy", "gz", None, None),
        P("gx", "gy", "gz", None),
        P("gx", "gy", "gz"),
    )
    return jax.shard_map(
        body,
        mesh=mesh,
        in_specs=placed,
        out_specs=(P(None, "gx", "gy", "gz"), P(None, None, "gx", "gy", "gz")),
        check_vma=False,
    )
```

time: 77.9 us -> 70.3 us (0.902)
  Pallas kernels: 23.4 us -> 18.8 us
  local copies, waits for them, and re-layouts: 2.4 us -> 0 us
  starting transfers between devices: 32.8 us -> 31.9 us
    ppermute x2, starting transfers between devices: 14.1 us -> 3.8 us  [the longest x1 3.8 us: body(): lax.ppermute(up, 'gz', [(i, (i + 1) % blocks) for i in range(blocks)])]
    all_to_all x1, starting transfers between devices: 3.45 us -> 13.1 us  [exchange(): return lax.all_to_all(x, 'gx', split_axis=0, concat_axis=0, tiled=False)]
    pallas_call x7, Pallas kernels: 22.3 us -> 17.7 us  [the longest x1 6.88 us: front(): pl.pallas_call(front_kernel, out_shape=(jax.ShapeDtypeStruct((5, NROW, 12...]
    all_to_all x1, waiting for transfers between devices: 16.2 us -> 13.1 us  [exchange(): return lax.all_to_all(x, 'gx', split_axis=0, concat_axis=0, tiled=False)]
    ppermute x1, waiting for transfers between devices: 0.01 us -> 2.69 us  [hand_on(): return lax.ppermute(x, ('gx', 'gy'), y_pairs(lax.axis_size('gy')))]
    unnamed x6 -> x0, local copies, waits for them, and re-layouts: 2.4 us -> none
    ppermute x2, waiting for transfers between devices: 0.01 us -> 1.11 us  [the longest x1 1.11 us: body(): lax.ppermute(down, 'gz', [((i + 1) % blocks, i) for i in range(blocks)])]
  transfers between devices with their start and end apart: 4 -> 4, of which waited for: 1 -> 3; matrix products, arithmetic and copies ran while one was open for 0% -> 0% of each run, Pallas kernels for 14% -> 4%
where the time goes in v3:
time: 70.3 us; the launch traced here: 70 us
  starting transfers between devices  31.9 us (45%)
  Pallas kernels  18.8 us (27%)
  waiting for transfers between devices  16.9 us (24%)
  between operations  2.2 us (3%)
    ppermute x1, starting transfers between devices, hand_on(): return lax.ppermute(x, ('gx', 'gy'), y_pairs(lax.axis_size('gy')))  15 us
    all_to_all x1, waiting for transfers between devices, exchange(): return lax.all_to_all(x, 'gx', split_axis=0, concat_axis=0, tiled=False)  13.1 us
    all_to_all x1, starting transfers between devices, exchange(): return lax.all_to_all(x, 'gx', split_axis=0, concat_axis=0, tiled=False)  13.1 us
    pallas_call x1, Pallas kernels, front(): pl.pallas_call(front_kernel, out_shape=(jax.ShapeDtypeStruct((5, NROW, 12...  6.88 us
    pallas_call x1, Pallas kernels, paint_early(): pl.pallas_call(paint_early_kernel, out_shape=PAINTED, in_specs=[VM], out_...  6.2 us
    ppermute x1, starting transfers between devices, body(): lax.ppermute(up, 'gz', [(i, (i + 1) % blocks) for i in range(blocks)])  3.8 us
    ppermute x1, waiting for transfers between devices, hand_on(): return lax.ppermute(x, ('gx', 'gy'), y_pairs(lax.axis_size('gy')))  2.69 us
    pallas_call x1, Pallas kernels, finish(): pl.pallas_call(finish_kernel, out_shape=(shape, shape, jax.ShapeDtypeStru...  2.48 us
  transfers between devices with their start and end apart: 4, of which 3 were waited for; matrix products, arithmetic and copies ran while one was open for 0% of the time, Pallas kernels for 4%

profile of v3, /device:TPU:1, one launch (start us, length us, event | category | flops | bytes accessed | tf_op | source)
XLA Modules:
  0.0 70.0 jit_solution(1123556945973790218)
XLA Ops:
  1.3 6.9 %front.1 = (f32[5,64,128]{2,1,0:T(8,128)S(1)}, f32[8,96,128]{2,1,0:T(8,128)}) custom-call(s32[1,1,1]{2,1,0:T(1,128)S(6)} %copy.61.count_ref, s32[64,128]{1,0:T(8,128)} %bitcast.77, f32[3,64,128]{2,1,0:T(8,128)} %bitcast.76, f32[64,128]{1,0:T(8,128)} %bitcast.78), custom_call_target="tpu_custom_call" | custom-call | flops 40000000 | bytes 1000000 | tf_op jit(solution)/shard_map/front/pallas_call | solution.py:388
  8.2 13.1 %all-to-all-start.3 = ((f32[8,96,128]{2,1,0:T(8,128)}), f32[8,96,128]{2,1,0:T(8,128)S(1)}, u32[]{:S(2)}, u32[]{:S(2)}) async-start(f32[8,96,128]{2,1,0:T(8,128)} %get-tuple-element.51), calls=%async_computation.3 | async-start | bytes 786432 | tf_op jit(solution)/shard_map/all_to_all | solution.py:613
  21.2 1.1 %tables.1 = (bf16[4,256,256]{2,1,0:T(8,128)(2,1)S(1)}, bf16[4,256,256]{2,1,0:T(8,128)(2,1)S(1)}) custom-call(), custom_call_target="tpu_custom_call" | custom-call | flops 8000000 | bytes 1000000 | tf_op jit(solution)/shard_map/tables/pallas_call | solution.py:452
  22.4 13.1 %all-to-all-done.3.recv_ref.face_ref = f32[8,96,128]{2,1,0:T(8,128)S(1)} async-done(((f32[8,96,128]{2,1,0:T(8,128)}), f32[8,96,128]{2,1,0:T(8,128)S(1)}, u32[]{:S(2)}, u32[]{:S(2)}) %all-to-all-start.3) | async-done | bytes 393248 | tf_op jit(solution)/shard_map/all_to_all | solution.py:613
  35.4 6.2 %paint_early.1.acc_ref = f32[8,2,136,128]{3,2,1,0:T(8,128)S(1)} custom-call(f32[8,96,128]{2,1,0:T(8,128)S(1)} %all-to-all-done.3.recv_ref.face_ref), custom_call_target="tpu_custom_call" | custom-call | flops 60000000 | bytes 2000000 | tf_op jit(solution)/shard_map/paint_early/pallas_call | solution.py:284
  41.7 15.0 %collective-permute-start.4 = (f32[8,40,128]{2,1,0:T(8,128)S(1)}, f32[8,40,128]{2,1,0:T(8,128)S(1)}, u32[]{:S(2)}, u32[]{:S(2)}) collective-permute-start(f32[8,40,128]{2,1,0:T(8,128)S(1)} %forward_pack.1.after_ref), channel_id=1, source_target_pairs={{896,8},{0,1016},{904,16},{8,896},{912,24},{16,904},{920,32},{24,9... | collective-permute-start | bytes 491528 | tf_op jit(solution)/shard_map/ppermute | solution.py:617
  56.7 2.7 %collective-permute-done.4.in_ref = f32[8,40,128]{2,1,0:T(8,128)S(1)} collective-permute-done((f32[8,40,128]{2,1,0:T(8,128)S(1)}, f32[8,40,128]{2,1,0:T(8,128)S(1)}, u32[]{:S(2)}, u32[]{:S(2)}) %collective-permute-start.4) | collective-permute-done | bytes 163872 | tf_op jit(solution)/shard_map/ppermute | solution.py:617
  59.4 0.2 along_z.1
  59.6 3.8 %collective-permute-start.5 = (f32[16,128]{1,0:T(8,128)S(1)}, f32[16,128]{1,0:T(8,128)S(1)}, u32[]{:S(2)}, u32[]{:S(2)}) collective-permute-start(f32[16,128]{1,0:T(8,128)S(1)} %get-tuple-element.53), channel_id=1, source_target_pairs={{0,1},{1,2},{2,3},{3,4},{4,5},{5,6},{6,7},{7,0},{8,9},{9,10},{10,1... | collective-permute-start | bytes 24584 | tf_op jit(solution)/shard_map/ppermute | solution.py:661
  63.4 0.0 collective-permute-start.6
  63.4 1.9 %paint_handed.3.acc_ref = f32[8,2,136,128]{3,2,1,0:T(8,128)S(1)} custom-call(f32[8,40,128]{2,1,0:T(8,128)S(1)} %collective-permute-done.4.in_ref, f32[8,2,136,128]{3,2,1,0:T(8,128)S(1)} %paint_late.1.acc_ref), custom_call_target="tpu_custom_call", output_to_operand_aliasing={{}: (1, {})} | custom-call | flops 60000000 | bytes 2000000 | tf_op jit(solution)/shard_map/paint_handed/pallas_call | solution.py:545
  65.3 0.0 collective-permute-done.5.below_ref
  65.3 1.1 %collective-permute-done.6.above_ref = f32[16,128]{1,0:T(8,128)S(1)} collective-permute-done((f32[16,128]{1,0:T(8,128)S(1)}, f32[16,128]{1,0:T(8,128)S(1)}, u32[]{:S(2)}, u32[]{:S(2)}) %collective-permute-start.6) | collective-permute-done | bytes 8224 | tf_op jit(solution)/shard_map/ppermute | solution.py:662
  66.4 2.5 %finish.3 = (f32[2048,128]{1,0:T(8,128)}, f32[2048,128]{1,0:T(8,128)}, s32[1]{0:T(128)}) custom-call(f32[8,2,136,128]{3,2,1,0:T(8,128)S(1)} %paint_handed.3.acc_ref, f32[8,96,128]{2,1,0:T(8,128)S(1)} %all-to-all-done.3.recv_ref.face_ref, f32[8,40,128]{2,1,0:T(8,128)S(1)} %collective-permute-done.4.in_ref, f32[16,128]{1,0:T(8,128)S(1)} %collective-permute-done.5.below_ref, ...), custom_call_target="tpu_custom_call" | custom-call | flops 400000000 | bytes 4000000 | tf_op jit(solution)/shard_map/finish/pallas_call | solution.py:592
  69.6 0.2 conditional.2
  (2 shorter events, 0.1 us)
Async XLA Ops:
  8.2 27.3 %all-to-all-start.3 = ((f32[8,96,128]{2,1,0:T(8,128)}), f32[8,96,128]{2,1,0:T(8,128)S(1)}, u32[]{:S(2)}, u32[]{:S(2)}) async-start(f32[8,96,128]{2,1,0:T(8,128)} %get-tuple-element.51), calls=%async_computation.3 | async-start | bytes 786432 | tf_op jit(solution)/shard_map/all_to_all | solution.py:613
  41.7 17.7 %collective-permute-start.4 = (f32[8,40,128]{2,1,0:T(8,128)S(1)}, f32[8,40,128]{2,1,0:T(8,128)S(1)}, u32[]{:S(2)}, u32[]{:S(2)}) collective-permute-start(f32[8,40,128]{2,1,0:T(8,128)S(1)} %forward_pack.1.after_ref), channel_id=1, source_target_pairs={{896,8},{0,1016},{904,16},{8,896},{912,24},{16,904},{920,32},{24,9... | collective-permute-start | bytes 491528 | tf_op jit(solution)/shard_map/ppermute | solution.py:617
  59.6 5.8 %collective-permute-start.5 = (f32[16,128]{1,0:T(8,128)S(1)}, f32[16,128]{1,0:T(8,128)S(1)}, u32[]{:S(2)}, u32[]{:S(2)}) collective-permute-start(f32[16,128]{1,0:T(8,128)S(1)} %get-tuple-element.53), channel_id=1, source_target_pairs={{0,1},{1,2},{2,3},{3,4},{4,5},{5,6},{6,7},{7,0},{8,9},{9,10},{10,1... | collective-permute-start | bytes 24584 | tf_op jit(solution)/shard_map/ppermute | solution.py:661
  63.4 3.1 %collective-permute-start.6 = (f32[16,128]{1,0:T(8,128)S(1)}, f32[16,128]{1,0:T(8,128)S(1)}, u32[]{:S(2)}, u32[]{:S(2)}) collective-permute-start(f32[16,128]{1,0:T(8,128)S(1)} %get-tuple-element.54), channel_id=1, source_target_pairs={{1,0},{2,1},{3,2},{4,3},{5,4},{6,5},{7,6},{0,7},{9,8},{10,9},{11,1... | collective-permute-start | bytes 24584 | tf_op jit(solution)/shard_map/ppermute | solution.py:662

commit v4 on v3

--- a/solution.py
+++ b/solution.py
@@ -11,8 +11,9 @@
 F32, I32, BF = jnp.float32, jnp.int32, jnp.bfloat16
 GX = 8
 ROWS = 17
-FROWS = 8
+FROWS = 7
 NROW = 64
+HANDED = 4 * FROWS + 4
 PAYROWS = 96
 FACE = 5 * ROWS
 XR = 136
@@ -61,7 +62,7 @@
                     elif down is False:
                         move = a > c
                     else:
-                        move = ((a > c) ^ down) & (a != c)
+                        move = jnp.where(down, c, a) > jnp.where(down, a, c)
                     for o in range(len(ops)):
                         a, c = ops[o][v], ops[o][w]
                         new[o][v] = jnp.where(move, c, a)
@@ -87,7 +88,7 @@
                         big = upper
                     else:
                         big = upper ^ down
-                    move = ((theirs > mine) & big) | ((theirs < mine) & ~big)
+                    move = jnp.where(big, theirs, mine) > jnp.where(big, mine, theirs)
                     new[0][v] = jnp.where(move, theirs, mine)
                     for o in range(1, len(ops)):
                         new[o][v] = jnp.where(move, partner(ops[o][v]), ops[o][v])
@@ -344,7 +345,7 @@
 
     def operands(r):
         def row(n):
-            return jnp.broadcast_to(val_ref[n, pl.ds(r, 1), :].astype(BF), (16, 128))
+            return jnp.broadcast_to(val_ref[n, r : r + 1, :].astype(BF), (16, 128))
 
         x0, x1, y0, y1 = row(0), row(1), row(6), row(7)
         weights = [row(n) for n in (2, 3, 4, 5, 8, 10, 9, 11)]
@@ -371,7 +372,9 @@
             total = total + lax.dot_general(x, v, (((1,), (1,)), ((), ())), preferred_element_type=F32)
         return total
 
-    o = lax.fori_loop(0, NROW // 16, step, jnp.zeros((272, 128), F32))
+    o = jnp.zeros((272, 128), F32)
+    for b in range(NROW // 16):
+        o = step(b, o)
     o = o + pltpu.roll(o, 64, 1)
     t = (o[0:128] + o[128:256]).T
     ends = o[256:264] + pltpu.roll(o[256:264], 6, 0)
@@ -409,13 +412,14 @@
         weight = m * (near + jnp.where(yp + jnp.where(dy >= 0, 1.0, -1.0) == row, ay, 0.0))
         for o, v in enumerate((cell, dx, dz, weight)):
             out_ref[i, o * FROWS : (o + 1) * FROWS, :] = v
-        out_ref[i, 4 * FROWS : 4 * FROWS + 8, :] = recv_ref[i, FACE : FACE + 8, :]
+        for n, r in enumerate((2, 5, 6, 7)):
+            out_ref[i, 4 * FROWS + n : 4 * FROWS + n + 1, :] = recv_ref[i, FACE + r : FACE + r + 1, :]
 
 
 def forward_pack(recv, table, acc):
     return pl.pallas_call(
         forward_kernel,
-        out_shape=jax.ShapeDtypeStruct((GX, 4 * FROWS + 8, 128), F32),
+        out_shape=jax.ShapeDtypeStruct((GX, HANDED, 128), F32),
         in_specs=[VM, ANY, ANY],
         out_specs=VM,
         name="forward_pack",
@@ -503,16 +507,16 @@
     return jnp.sum(jnp.where(lax.broadcasted_iota(I32, (2, 128), 1) == lane, v, 0.0), axis=1, keepdims=True)
 
 
-def along_z_kernel(face_ref, in_ref, down_ref, up_ref):
+def along_z_kernel(face_ref, in_ref, after_ref, down_ref, up_ref):
     p = lax.axis_index("gx")
     for j in range(2):
         on = p == (0 if j == 0 else GX - 1)
         rows, ghosts = [], []
         for i in range(GX):
-            own, handed = face_ref[i, FACE : FACE + 8, :], in_ref[i, 4 * FROWS : 4 * FROWS + 8, :]
-            rows.append([own[3 * n + j : 3 * n + j + 1] + jnp.where(on, handed[3 * n + 2 : 3 * n + 3], 0.0) for n in range(2)])
+            own, handed = face_ref[i, FACE : FACE + 8, :], in_ref[i, 4 * FROWS : HANDED, :]
+            rows.append([own[3 * n + j : 3 * n + j + 1] + jnp.where(on, handed[n : n + 1], 0.0) for n in range(2)])
             past = [pick(own[6:8], base + 2 * p + 1 + j) for base in (0, 24)]
-            more = [pick(handed[6:8], base + (17 if j == 0 else 0)) for base in (0, 24)]
+            more = [pick(handed[2:4], base + (17 if j == 0 else 0)) for base in (0, 24)]
             ghosts.append([a + jnp.where(on, b, 0.0) for a, b in zip(past, more)])
         for i in range(GX):
             down, up = face_columns(i, rows, ghosts)
@@ -520,49 +524,44 @@
             up_ref[2 * i + j : 2 * i + j + 1] = up
 
 
-def along_z(recv, passed):
+def along_z(recv, passed, after):
     shape = jax.ShapeDtypeStruct((2 * GX, 128), F32)
     return pl.pallas_call(
         along_z_kernel,
         out_shape=(shape, shape),
-        in_specs=[VM, VM],
+        in_specs=[VM, VM, ANY],
         out_specs=(VM, VM),
         name="along_z",
         compiler_params=ROOM,
         cost_estimate=pl.CostEstimate(flops=500000, bytes_accessed=100000, transcendentals=0),
-    )(recv, passed)
-
-
-def handed_kernel(in_ref, acc_ref, out_ref, val_ref):
+    )(recv, passed, after)
+
+
+def handed_kernel(in_ref, face_ref, acc_ref, out_ref, flag_ref, val_ref):
     p = lax.axis_index("gx")
+    flag_ref[0] = flagged(face_ref, FACE + 6)
 
     @pl.when((p == 0) | (p == GX - 1))
     def _():
+        flag_ref[0] = jnp.maximum(flag_ref[0], flagged(in_ref, 4 * FROWS + 2))
         paint_sources(FROWS, 4, True, acc_ref, in_ref, out_ref, val_ref)
 
 
-def paint_handed(passed, acc):
+def paint_handed(passed, recv, acc):
     return pl.pallas_call(
         handed_kernel,
-        out_shape=PAINTED,
-        in_specs=[VM, VM],
-        out_specs=VM,
+        out_shape=(PAINTED, pltpu.SMEM((1,), I32)),
+        in_specs=[VM, VM, VM],
+        out_specs=(VM, SM),
         scratch_shapes=paint_scratch(4),
-        input_output_aliases={1: 0},
+        input_output_aliases={2: 0},
         name="paint_handed",
         compiler_params=ROOM,
         cost_estimate=PAINT_COST,
-    )(passed, acc)
-
-
-def finish_kernel(acc_ref, face_ref, in_ref, below_ref, above_ref, th_ref, tl_ref, dens_ref, spec_ref, flag_ref, x_ref):
-    p = lax.axis_index("gx")
-    flag_ref[0] = flagged(face_ref, FACE + 6)
-
-    @pl.when((p == 0) | (p == GX - 1))
-    def _():
-        flag_ref[0] = jnp.maximum(flag_ref[0], flagged(in_ref, 4 * FROWS + 6))
-
+    )(passed, recv, acc)
+
+
+def finish_kernel(acc_ref, below_ref, above_ref, th_ref, tl_ref, dens_ref, spec_ref, x_ref):
     wide = lax.broadcasted_iota(I32, (128, 128), 1)
     for i in range(GX):
         before, after = (i - 1) % GX, (i + 1) % GX
@@ -587,18 +586,18 @@
     transform(lambda b: x_ref[b], th_ref, tl_ref, put)
 
 
-def finish(acc, recv, passed, below, above, th, tl):
+def finish(acc, below, above, th, tl):
     shape = jax.ShapeDtypeStruct((2048, 128), F32)
     return pl.pallas_call(
         finish_kernel,
-        out_shape=(shape, shape, jax.ShapeDtypeStruct((1,), I32)),
-        in_specs=[VM] * 7,
-        out_specs=(VM, VM, SM),
+        out_shape=(shape, shape),
+        in_specs=[VM] * 5,
+        out_specs=(VM, VM),
         scratch_shapes=[pltpu.VMEM((GX, 128, 256), F32)],
         name="finish",
         compiler_params=ROOM,
         cost_estimate=pl.CostEstimate(flops=400000000, bytes_accessed=4000000, transcendentals=0),
-    )(acc, recv, passed, below, above, th, tl)
+    )(acc, below, above, th, tl)
 
 
 def y_pairs(blocks):
@@ -657,11 +656,11 @@
     packed = forward_pack(recv, th, acc)
     passed = hand_on(packed)
     acc = paint_late(recv, packed, acc)
-    down, up = along_z(recv, passed)
+    down, up = along_z(recv, passed, acc)
     below = lax.ppermute(up, "gz", [(i, (i + 1) % blocks) for i in range(blocks)])
     above = lax.ppermute(down, "gz", [((i + 1) % blocks, i) for i in range(blocks)])
-    acc = paint_handed(passed, acc)
-    density, spectrum, over = finish(acc, recv, passed, below, above, th, tl)
+    acc, over = paint_handed(passed, recv, acc)
+    density, spectrum = finish(acc, below, above, th, tl)
 
     def slow(outputs):
         mine = jnp.max(recv[:, FACE + 6, 64:]) > 0
@@ -679,9 +678,8 @@
             acc = paint_more(x, acc)
         for x in (rest, *later):
             acc = paint_more(hand_on(weighted(x)), acc, handed=True)
-        acc = paint_handed(passed, acc)
-        density, spectrum, _ = finish(acc, recv, passed, below, above, th, tl)
-        return density, spectrum
+        acc, _ = paint_handed(passed, recv, acc)
+        return finish(acc, below, above, th, tl)
 
     density, spectrum = lax.cond(over[0] > 0, slow, lambda outputs: outputs, (density, spectrum))
     return density.reshape(1024, 1, 2, 128), spectrum.reshape(2, 512, 1, 2, 128)

time: 70.3 us -> 67.4 us (0.959)
  Pallas kernels: 18.8 us -> 17.5 us
  between operations: 2.2 us -> 1.34 us
    pallas_call x1, Pallas kernels: 6.88 us -> 5.47 us  [front(): pl.pallas_call(front_kernel, out_shape=(jax.ShapeDtypeStruct((5, NROW, 12...]
  transfers between devices with their start and end apart: 4 -> 4, of which waited for: 3 -> 3; matrix products, arithmetic and copies ran while one was open for 0% -> 0% of each run, Pallas kernels for 4% -> 5%
where the time goes in v4:
time: 67.4 us; the launch traced here: 67.1 us
  starting transfers between devices  31.9 us (47%)
  Pallas kernels  17.5 us (26%)
  waiting for transfers between devices  16.5 us (24%)
  between operations  1.34 us (2%)
    ppermute x1, starting transfers between devices, hand_on(): return lax.ppermute(x, ('gx', 'gy'), y_pairs(lax.axis_size('gy')))  15 us
    all_to_all x1, waiting for transfers between devices, exchange(): return lax.all_to_all(x, 'gx', split_axis=0, concat_axis=0, tiled=False)  13.1 us
    all_to_all x1, starting transfers between devices, exchange(): return lax.all_to_all(x, 'gx', split_axis=0, concat_axis=0, tiled=False)  13.1 us
    pallas_call x1, Pallas kernels, paint_early(): pl.pallas_call(paint_early_kernel, out_shape=PAINTED, in_specs=[VM], out_...  6.2 us
    pallas_call x1, Pallas kernels, front(): pl.pallas_call(front_kernel, out_shape=(jax.ShapeDtypeStruct((5, NROW, 12...  5.47 us
    ppermute x1, starting transfers between devices, body(): lax.ppermute(up, 'gz', [(i, (i + 1) % blocks) for i in range(blocks)])  3.8 us
    pallas_call x1, Pallas kernels, finish(): pl.pallas_call(finish_kernel, out_shape=(shape, shape), in_specs=[VM] * 5...  2.34 us
    ppermute x1, waiting for transfers between devices, hand_on(): return lax.ppermute(x, ('gx', 'gy'), y_pairs(lax.axis_size('gy')))  2.31 us
  transfers between devices with their start and end apart: 4, of which 3 were waited for; matrix products, arithmetic and copies ran while one was open for 0% of the time, Pallas kernels for 5%

profile of v4, /device:TPU:1, one launch (start us, length us, event | category | flops | bytes accessed | tf_op | source)
XLA Modules:
  0.0 67.1 jit_solution(7643094026722033452)
XLA Ops:
  1.3 5.5 %front.1 = (f32[5,64,128]{2,1,0:T(8,128)S(1)}, f32[8,96,128]{2,1,0:T(8,128)}) custom-call(s32[1,1,1]{2,1,0:T(1,128)S(6)} %copy.61.count_ref, s32[64,128]{1,0:T(8,128)} %bitcast.77, f32[3,64,128]{2,1,0:T(8,128)} %bitcast.76, f32[64,128]{1,0:T(8,128)} %bitcast.78), custom_call_target="tpu_custom_call" | custom-call | flops 40000000 | bytes 1000000 | tf_op jit(solution)/shard_map/front/pallas_call | solution.py:391
  6.7 13.1 %all-to-all-start.3 = ((f32[8,96,128]{2,1,0:T(8,128)}), f32[8,96,128]{2,1,0:T(8,128)S(1)}, u32[]{:S(2)}, u32[]{:S(2)}) async-start(f32[8,96,128]{2,1,0:T(8,128)} %get-tuple-element.53), calls=%async_computation.3 | async-start | bytes 786432 | tf_op jit(solution)/shard_map/all_to_all | solution.py:612
  19.8 1.1 %tables.1 = (bf16[4,256,256]{2,1,0:T(8,128)(2,1)S(1)}, bf16[4,256,256]{2,1,0:T(8,128)(2,1)S(1)}) custom-call(), custom_call_target="tpu_custom_call" | custom-call | flops 8000000 | bytes 1000000 | tf_op jit(solution)/shard_map/tables/pallas_call | solution.py:456
  20.9 13.1 %all-to-all-done.3.recv_ref.face_ref = f32[8,96,128]{2,1,0:T(8,128)S(1)} async-done(((f32[8,96,128]{2,1,0:T(8,128)}), f32[8,96,128]{2,1,0:T(8,128)S(1)}, u32[]{:S(2)}, u32[]{:S(2)}) %all-to-all-start.3) | async-done | bytes 393248 | tf_op jit(solution)/shard_map/all_to_all | solution.py:612
  34.0 6.2 %paint_early.1.acc_ref = f32[8,2,136,128]{3,2,1,0:T(8,128)S(1)} custom-call(f32[8,96,128]{2,1,0:T(8,128)S(1)} %all-to-all-done.3.recv_ref.face_ref), custom_call_target="tpu_custom_call" | custom-call | flops 60000000 | bytes 2000000 | tf_op jit(solution)/shard_map/paint_early/pallas_call | solution.py:285
  40.3 15.0 %collective-permute-start.4 = (f32[8,32,128]{2,1,0:T(8,128)S(1)}, f32[8,32,128]{2,1,0:T(8,128)S(1)}, u32[]{:S(2)}, u32[]{:S(2)}) collective-permute-start(f32[8,32,128]{2,1,0:T(8,128)S(1)} %forward_pack.1.after_ref), channel_id=1, source_target_pairs={{896,8},{0,1016},{904,16},{8,896},{912,24},{16,904},{920,32},{24,9... | collective-permute-start | bytes 393224 | tf_op jit(solution)/shard_map/ppermute | solution.py:616
  55.3 2.3 %collective-permute-done.4.in_ref = f32[8,32,128]{2,1,0:T(8,128)S(1)} collective-permute-done((f32[8,32,128]{2,1,0:T(8,128)S(1)}, f32[8,32,128]{2,1,0:T(8,128)S(1)}, u32[]{:S(2)}, u32[]{:S(2)}) %collective-permute-start.4) | collective-permute-done | bytes 131104 | tf_op jit(solution)/shard_map/ppermute | solution.py:616
  57.6 0.3 along_z.1
  57.9 3.8 %collective-permute-start.5 = (f32[16,128]{1,0:T(8,128)S(1)}, f32[16,128]{1,0:T(8,128)S(1)}, u32[]{:S(2)}, u32[]{:S(2)}) collective-permute-start(f32[16,128]{1,0:T(8,128)S(1)} %get-tuple-element.57), channel_id=1, source_target_pairs={{0,1},{1,2},{2,3},{3,4},{4,5},{5,6},{6,7},{7,0},{8,9},{9,10},{10,1... | collective-permute-start | bytes 24584 | tf_op jit(solution)/shard_map/ppermute | solution.py:660
  61.7 0.0 collective-permute-start.6
  61.7 2.0 %paint_handed.3 = (f32[8,2,136,128]{3,2,1,0:T(8,128)S(1)}, s32[1]{0:T(128)S(4)}) custom-call(f32[8,32,128]{2,1,0:T(8,128)S(1)} %collective-permute-done.4.in_ref, f32[8,96,128]{2,1,0:T(8,128)S(1)} %all-to-all-done.3.recv_ref.face_ref, f32[8,2,136,128]{3,2,1,0:T(8,128)S(1)} %paint_late.1.acc_ref.after_ref), custom_call_target="tpu_custom_call", output_to_operand_aliasing={{0}: (2, {})} | custom-call | flops 60000000 | bytes 2000000 | tf_op jit(solution)/shard_map/paint_handed/pallas_call | solution.py:551
  63.7 0.0 collective-permute-done.5.below_ref
  63.7 1.1 %collective-permute-done.6.above_ref = f32[16,128]{1,0:T(8,128)S(1)} collective-permute-done((f32[16,128]{1,0:T(8,128)S(1)}, f32[16,128]{1,0:T(8,128)S(1)}, u32[]{:S(2)}, u32[]{:S(2)}) %collective-permute-start.6) | collective-permute-done | bytes 8224 | tf_op jit(solution)/shard_map/ppermute | solution.py:661
  64.8 2.3 %finish.3 = (f32[2048,128]{1,0:T(8,128)}, f32[2048,128]{1,0:T(8,128)}) custom-call(f32[8,2,136,128]{3,2,1,0:T(8,128)S(1)} %get-tuple-element.56.acc_ref, f32[16,128]{1,0:T(8,128)S(1)} %collective-permute-done.5.below_ref, f32[16,128]{1,0:T(8,128)S(1)} %collective-permute-done.6.above_ref, bf16[4,256,256]{2,1,0:T(8,128)(2,1)S(1)} %get-tuple-element.54.table_ref.th_ref, ...), custom_call_target="tpu_custom_call" | custom-call | flops 400000000 | bytes 4000000 | tf_op jit(solution)/shard_map/finish/pallas_call | solution.py:591
  (3 shorter events, 0.1 us)
Async XLA Ops:
  6.7 27.3 %all-to-all-start.3 = ((f32[8,96,128]{2,1,0:T(8,128)}), f32[8,96,128]{2,1,0:T(8,128)S(1)}, u32[]{:S(2)}, u32[]{:S(2)}) async-start(f32[8,96,128]{2,1,0:T(8,128)} %get-tuple-element.53), calls=%async_computation.3 | async-start | bytes 786432 | tf_op jit(solution)/shard_map/all_to_all | solution.py:612
  40.3 17.3 %collective-permute-start.4 = (f32[8,32,128]{2,1,0:T(8,128)S(1)}, f32[8,32,128]{2,1,0:T(8,128)S(1)}, u32[]{:S(2)}, u32[]{:S(2)}) collective-permute-start(f32[8,32,128]{2,1,0:T(8,128)S(1)} %forward_pack.1.after_ref), channel_id=1, source_target_pairs={{896,8},{0,1016},{904,16},{8,896},{912,24},{16,904},{920,32},{24,9... | collective-permute-start | bytes 393224 | tf_op jit(solution)/shard_map/ppermute | solution.py:616
  57.9 5.8 %collective-permute-start.5 = (f32[16,128]{1,0:T(8,128)S(1)}, f32[16,128]{1,0:T(8,128)S(1)}, u32[]{:S(2)}, u32[]{:S(2)}) collective-permute-start(f32[16,128]{1,0:T(8,128)S(1)} %get-tuple-element.57), channel_id=1, source_target_pairs={{0,1},{1,2},{2,3},{3,4},{4,5},{5,6},{6,7},{7,0},{8,9},{9,10},{10,1... | collective-permute-start | bytes 24584 | tf_op jit(solution)/shard_map/ppermute | solution.py:660
  61.7 3.1 %collective-permute-start.6 = (f32[16,128]{1,0:T(8,128)S(1)}, f32[16,128]{1,0:T(8,128)S(1)}, u32[]{:S(2)}, u32[]{:S(2)}) collective-permute-start(f32[16,128]{1,0:T(8,128)S(1)} %get-tuple-element.58), channel_id=1, source_target_pairs={{1,0},{2,1},{3,2},{4,3},{5,4},{6,5},{7,6},{0,7},{9,8},{10,9},{11,1... | collective-permute-start | bytes 24584 | tf_op jit(solution)/shard_map/ppermute | solution.py:661

commit v5 on v4

--- a/solution.py
+++ b/solution.py
@@ -8,8 +8,10 @@
 from jax.experimental.pallas import tpu as pltpu
 from jax.sharding import PartitionSpec as P
 
+
 F32, I32, BF = jnp.float32, jnp.int32, jnp.bfloat16
 GX = 8
+RING = 4
 ROWS = 17
 FROWS = 7
 NROW = 64
@@ -75,8 +77,6 @@
                 def partner(x):
                     if 2 * step == x.shape[axis]:
                         return pltpu.roll(x, step, axis)
-                    if axis == 0:
-                        return jnp.where(upper, pltpu.roll(x, step, 0), pltpu.roll(x, 8 - step, 0))
                     return jnp.take_along_axis(x, other, axis=axis)
 
                 for v in range(8):
@@ -96,7 +96,7 @@
     return ops
 
 
-def sort_and_pack(count, cell_ref, off_ref, mass_ref, low, high, ghosts, sorted_ref, pay_ref):
+def sort_and_pack(count, cell_ref, off_ref, mass_ref, low, high, ghosts, sorted_ref, pay_ref, hand_ref):
     lane = lax.broadcasted_iota(I32, (8, 128), 1)
     sub = lax.broadcasted_iota(I32, (8, 128), 0)
     below = [jnp.zeros((8, 128), F32) for _ in range(18)]
@@ -140,6 +140,21 @@
             rows += [v[2 * p + 1 : 2 * p + 3], v[past : past + 1]]
         pay_ref[p, FACE : FACE + 8, :] = jnp.concatenate(rows + [ghosts], axis=0)
         pay_ref[p, FACE + 8 : PAYROWS, :] = jnp.zeros((PAYROWS - FACE - 8, 128), F32)
+    last = lax.axis_index("gy") % RING == RING - 1
+    first = jnp.where(last, starts[GX - 1] + ROWS - FROWS, 0)
+    row = jnp.where(last, 17.0, 0.0)
+    parts = [sorted_ref[o, pl.ds(first, FROWS), :] for o in range(5)]
+    for o, v in enumerate(one_row(*parts, row)):
+        hand_ref[o * FROWS : (o + 1) * FROWS, :] = v
+    ends = [jnp.where(last, v[17:18], v[0:1]) for v in (low, high)]
+    hand_ref[4 * FROWS : HANDED, :] = jnp.concatenate(ends + [ghosts], axis=0)
+
+
+def one_row(cell, dx, dy, dz, m, row):
+    _, yp, _ = cells_of(cell)
+    ay = jnp.abs(dy)
+    far = yp + jnp.where(dy >= 0, 1.0, -1.0)
+    return cell, dx, dz, m * (jnp.where(yp == row, 1.0 - ay, 0.0) + jnp.where(far == row, ay, 0.0))
 
 
 def spread(first, second, one, two):
@@ -238,20 +253,21 @@
     lax.fori_loop(begin // together, end // together, step, 0)
 
 
-def waits_long():
-    p = lax.axis_index("gx")
-    return ((p == 0) | (p == GX - 1)) & (lax.axis_index("gy") % 4 == 0)
+SOME = 0
+
+
+def painted_early():
+    p, q = lax.axis_index("gx"), lax.axis_index("gy") % RING
+    every = ((q == 0) & (p == 0)) | ((q == RING - 1) & (p == GX - 1))
+    return jnp.where(every, GX, jnp.where((q == 0) & (p == GX - 1), SOME, 0))
 
 
 def paint_early_kernel(recv_ref, out_ref, val_ref):
-    @pl.when(waits_long())
-    def _():
-        paint_sources(ROWS, 2, False, None, recv_ref, out_ref, val_ref, 0, EARLY)
+    paint_sources(ROWS, 2, False, None, recv_ref, out_ref, val_ref, 0, painted_early())
 
 
 def paint_late_kernel(recv_ref, after_ref, acc_ref, out_ref, val_ref):
-    begin = jnp.where(waits_long(), EARLY, 0)
-    paint_sources(ROWS, 2, False, None, recv_ref, out_ref, val_ref, begin)
+    paint_sources(ROWS, 2, False, None, recv_ref, out_ref, val_ref, painted_early())
 
 
 def paint_more_kernel(handed, recv_ref, acc_ref, out_ref, val_ref):
@@ -276,7 +292,6 @@
     return [pltpu.VMEM((together, 16, 24, 128), F32)]
 
 
-EARLY = 8
 PAINTED = jax.ShapeDtypeStruct((GX, 2, XR, 128), F32)
 PAINT_COST = pl.CostEstimate(flops=60000000, bytes_accessed=2000000, transcendentals=0)
 
@@ -381,18 +396,22 @@
     return t[0:24], t[24:48], ends[0:2]
 
 
-def front_kernel(count_ref, cell_ref, off_ref, mass_ref, sorted_ref, pay_ref, val_ref):
+def front_kernel(count_ref, cell_ref, off_ref, mass_ref, sorted_ref, pay_ref, hand_ref, val_ref):
     count = count_ref[0, 0, 0]
     low, high, ghosts = paint_faces(count, cell_ref, off_ref, mass_ref, val_ref)
-    sort_and_pack(count, cell_ref, off_ref, mass_ref, low, high, ghosts, sorted_ref, pay_ref)
+    sort_and_pack(count, cell_ref, off_ref, mass_ref, low, high, ghosts, sorted_ref, pay_ref, hand_ref)
 
 
 def front(count, cell, off, mass):
     return pl.pallas_call(
         front_kernel,
-        out_shape=(jax.ShapeDtypeStruct((5, NROW, 128), F32), jax.ShapeDtypeStruct((GX, PAYROWS, 128), F32)),
+        out_shape=(
+            jax.ShapeDtypeStruct((5, NROW, 128), F32),
+            jax.ShapeDtypeStruct((GX, PAYROWS, 128), F32),
+            pltpu.VMEM((HANDED, 128), F32),
+        ),
         in_specs=[SM, VM, VM, VM],
-        out_specs=(VM, VM),
+        out_specs=(VM, VM, VM),
         scratch_shapes=[pltpu.VMEM((12, NROW, 128), F32)],
         name="front",
         compiler_params=FULL,
@@ -400,32 +419,59 @@
     )(count, cell, off, mass)
 
 
-def forward_kernel(recv_ref, table_ref, acc_ref, out_ref):
+def forward_kernel(recv_ref, acc_ref, out_ref):
     last = lax.axis_index("gx") == GX - 1
     first = jnp.where(last, ROWS - FROWS, 0)
     row = jnp.where(last, 17.0, 0.0)
     for i in range(GX):
-        cell, dx, dy, dz, m = (recv_ref[i, pl.ds(o * ROWS + first, FROWS), :] for o in range(5))
-        _, yp, _ = cells_of(cell)
-        ay = jnp.abs(dy)
-        near = jnp.where(yp == row, 1.0 - ay, 0.0)
-        weight = m * (near + jnp.where(yp + jnp.where(dy >= 0, 1.0, -1.0) == row, ay, 0.0))
-        for o, v in enumerate((cell, dx, dz, weight)):
+        parts = [recv_ref[i, pl.ds(o * ROWS + first, FROWS), :] for o in range(5)]
+        for o, v in enumerate(one_row(*parts, row)):
             out_ref[i, o * FROWS : (o + 1) * FROWS, :] = v
         for n, r in enumerate((2, 5, 6, 7)):
             out_ref[i, 4 * FROWS + n : 4 * FROWS + n + 1, :] = recv_ref[i, FACE + r : FACE + r + 1, :]
 
 
-def forward_pack(recv, table, acc):
+def forward_pack(recv, acc):
     return pl.pallas_call(
         forward_kernel,
         out_shape=jax.ShapeDtypeStruct((GX, HANDED, 128), F32),
-        in_specs=[VM, ANY, ANY],
+        in_specs=[VM, ANY],
         out_specs=VM,
         name="forward_pack",
         compiler_params=ROOM,
         cost_estimate=pl.CostEstimate(flops=500000, bytes_accessed=600000, transcendentals=0),
-    )(recv, table, acc)
+    )(recv, acc)
+
+
+def join_kernel(one_ref, two_ref, out_ref):
+    out_ref[0] = one_ref[...]
+    out_ref[1] = two_ref[...]
+
+
+def join(one, two):
+    return pl.pallas_call(
+        join_kernel,
+        out_shape=jax.ShapeDtypeStruct((2, HANDED, 128), F32),
+        in_specs=[VM, VM],
+        out_specs=VM,
+        name="join",
+        compiler_params=ROOM,
+    )(one, two)
+
+
+def either_kernel(one_ref, two_ref, out_ref):
+    out_ref[...] = one_ref[...] + two_ref[...]
+
+
+def either(one, two):
+    return pl.pallas_call(
+        either_kernel,
+        out_shape=jax.ShapeDtypeStruct((2, HANDED, 128), F32),
+        in_specs=[VM, VM],
+        out_specs=VM,
+        name="either",
+        compiler_params=ROOM,
+    )(one, two)
 
 
 def table_kernel(high_ref, low_ref):
@@ -507,13 +553,19 @@
     return jnp.sum(jnp.where(lax.broadcasted_iota(I32, (2, 128), 1) == lane, v, 0.0), axis=1, keepdims=True)
 
 
-def along_z_kernel(face_ref, in_ref, after_ref, down_ref, up_ref):
-    p = lax.axis_index("gx")
+def along_z_kernel(face_ref, in_ref, *refs):
+    gathered, (after_ref, down_ref, up_ref, all_ref) = refs[: GX // 2], refs[GX // 2 :]
+    p, q = lax.axis_index("gx"), lax.axis_index("gy") % RING
+    across = ((p == 0) & (q == 0)) | ((p == GX - 1) & (q == RING - 1))
+    for i in range(GX):
+        n = GX - 1 - i
+        mine = jnp.where(p == 0, gathered[i // 2][i % 2], gathered[n // 2][n % 2])
+        all_ref[i] = jnp.where(across, mine, in_ref[i])
     for j in range(2):
         on = p == (0 if j == 0 else GX - 1)
         rows, ghosts = [], []
         for i in range(GX):
-            own, handed = face_ref[i, FACE : FACE + 8, :], in_ref[i, 4 * FROWS : HANDED, :]
+            own, handed = face_ref[i, FACE : FACE + 8, :], all_ref[i, 4 * FROWS : HANDED, :]
             rows.append([own[3 * n + j : 3 * n + j + 1] + jnp.where(on, handed[n : n + 1], 0.0) for n in range(2)])
             past = [pick(own[6:8], base + 2 * p + 1 + j) for base in (0, 24)]
             more = [pick(handed[2:4], base + (17 if j == 0 else 0)) for base in (0, 24)]
@@ -524,17 +576,17 @@
             up_ref[2 * i + j : 2 * i + j + 1] = up
 
 
-def along_z(recv, passed, after):
+def along_z(recv, passed, gathered, after):
     shape = jax.ShapeDtypeStruct((2 * GX, 128), F32)
     return pl.pallas_call(
         along_z_kernel,
-        out_shape=(shape, shape),
-        in_specs=[VM, VM, ANY],
-        out_specs=(VM, VM),
+        out_shape=(shape, shape, jax.ShapeDtypeStruct((GX, HANDED, 128), F32)),
+        in_specs=[VM] * (2 + GX // 2) + [ANY],
+        out_specs=(VM, VM, VM),
         name="along_z",
         compiler_params=ROOM,
         cost_estimate=pl.CostEstimate(flops=500000, bytes_accessed=100000, transcendentals=0),
-    )(recv, passed, after)
+    )(recv, passed, *gathered, after)
 
 
 def handed_kernel(in_ref, face_ref, acc_ref, out_ref, flag_ref, val_ref):
@@ -600,11 +652,12 @@
     )(acc, below, above, th, tl)
 
 
-def y_pairs(blocks):
+def y_pairs(blocks, across):
     pairs = []
     for q in range(blocks):
-        pairs.append(((GX - 1) * blocks + q, (q + 1) % blocks))
-        pairs.append((q, (GX - 1) * blocks + (q - 1) % blocks))
+        n, top = (q + 1) % blocks, (GX - 1) * blocks
+        if across or q % RING != RING - 1:
+            pairs += [(top + q, n), (n, top + q)]
     return pairs
 
 
@@ -612,22 +665,45 @@
     return lax.all_to_all(x, "gx", split_axis=0, concat_axis=0, tiled=False)
 
 
-def hand_on(x):
-    return lax.ppermute(x, ("gx", "gy"), y_pairs(lax.axis_size("gy")))
+def hand_on(x, across=False):
+    return lax.ppermute(x, ("gx", "gy"), y_pairs(lax.axis_size("gy"), across))
+
+
+def beside(x, up):
+    blocks, pairs = lax.axis_size("gy"), []
+    for q in range(RING - 1 if up else 0, blocks, RING):
+        for p in range(0, GX, 2):
+            pairs.append(((p + 1) * blocks + q, p * blocks + q) if up else (p * blocks + q, (p + 1) * blocks + q))
+    return lax.ppermute(x, ("gx", "gy"), pairs)
+
+
+def cross(x, up):
+    blocks, pairs = lax.axis_size("gy"), []
+    for q in range(RING - 1, blocks, RING):
+        n = (q + 1) % blocks
+        for p in range(0 if up else 1, GX, 2):
+            pairs.append((p * blocks + q, p * blocks + n) if up else (p * blocks + n, p * blocks + q))
+    return lax.ppermute(x, ("gx", "gy"), pairs)
+
+
+def gather(x, n):
+    blocks, pairs = lax.axis_size("gy"), []
+    for q in range(blocks):
+        if q % RING == 0:
+            pairs.append((n * blocks + q, q))
+        elif q % RING == RING - 1:
+            pairs.append(((GX - 1 - n) * blocks + q, (GX - 1) * blocks + q))
+    return lax.ppermute(x, ("gx", "gy"), pairs)
 
 
 def weighted(block):
-    cell, dx, dy, dz, m = (block[:, o * ROWS : (o + 1) * ROWS] for o in range(5))
     row = jnp.where(lax.axis_index("gx") == GX - 1, 17.0, 0.0)
-    _, yp, _ = cells_of(cell)
-    ay = jnp.abs(dy)
-    far = yp + jnp.where(dy >= 0, 1.0, -1.0)
-    weight = m * (jnp.where(yp == row, 1.0 - ay, 0.0) + jnp.where(far == row, ay, 0.0))
-    return jnp.concatenate([cell, dx, dz, weight, jnp.zeros((GX, PAYROWS - 4 * ROWS, 128), F32)], axis=1)
+    parts = one_row(*(block[:, o * ROWS : (o + 1) * ROWS] for o in range(5)), row)
+    return jnp.concatenate([*parts, jnp.zeros((GX, PAYROWS - 4 * ROWS, 128), F32)], axis=1)
 
 
 def later_window(ordered, turn):
-    xp, yp, zp = cells_of(ordered[0])
+    _, yp, _ = cells_of(ordered[0])
     live = ordered[4] != 0.0
     key = jnp.where(live, jnp.where(ordered[2] >= 0, yp, yp - 1.0), 20.0)
     space = jnp.zeros((5, NROW + 3 * ROWS, 128), F32)
@@ -648,15 +724,24 @@
 def body(cell_index, offsets, mass, counts):
     p = lax.axis_index("gx")
     blocks = lax.axis_size("gz")
-    ordered, pay = front(counts, cell_index.reshape(NROW, 128), offsets.reshape(3, NROW, 128), mass.reshape(NROW, 128))
+    ordered, pay, hand = front(
+        counts, cell_index.reshape(NROW, 128), offsets.reshape(3, NROW, 128), mass.reshape(NROW, 128)
+    )
+    next_to = beside(hand, True)
+    came_up = cross(join(hand, next_to), True)
     recv = exchange(pay)
+    next_to = beside(hand, False)
+    came_down = cross(join(hand, next_to), False)
     th, tl = tables()
-
+    held = either(came_up, came_down)
+    gathered = [held]
+    for n in range(2, GX, 2):
+        gathered.append(gather(held, n))
     acc = paint_early(recv)
-    packed = forward_pack(recv, th, acc)
+    packed = forward_pack(recv, acc)
     passed = hand_on(packed)
     acc = paint_late(recv, packed, acc)
-    down, up = along_z(recv, passed, acc)
+    down, up, passed = along_z(recv, passed, gathered, acc)
     below = lax.ppermute(up, "gz", [(i, (i + 1) % blocks) for i in range(blocks)])
     above = lax.ppermute(down, "gz", [((i + 1) % blocks, i) for i in range(blocks)])
     acc, over = paint_handed(passed, recv, acc)
@@ -677,7 +762,7 @@
         for x in (recv, *later):
             acc = paint_more(x, acc)
         for x in (rest, *later):
-            acc = paint_more(hand_on(weighted(x)), acc, handed=True)
+            acc = paint_more(hand_on(weighted(x), across=True), acc, handed=True)
         acc, _ = paint_handed(passed, recv, acc)
         return finish(acc, below, above, th, tl)
 

time: 67.4 us -> 90.7 us (1.35)
  blocking collectives: 0 us -> 32.1 us
  starting transfers between devices: 31.9 us -> 13.8 us
  waiting for transfers between devices: 16.5 us -> 25.8 us
    all_to_all x0 -> x1, blocking collectives: none -> 32.1 us  [exchange(): return lax.all_to_all(x, 'gx', split_axis=0, concat_axis=0, tiled=False)]
    ppermute x1 -> x8, waiting for transfers between devices: 2.31 us -> 25.8 us  [the longest x2 19.3 us: cross(): return lax.ppermute(x, ('gx', 'gy'), pairs)]
    all_to_all x1 -> x0, waiting for transfers between devices: 13.1 us -> none  [exchange(): return lax.all_to_all(x, 'gx', split_axis=0, concat_axis=0, tiled=False)]
    all_to_all x1 -> x0, starting transfers between devices: 13.1 us -> none  [exchange(): return lax.all_to_all(x, 'gx', split_axis=0, concat_axis=0, tiled=False)]
    ppermute x1 -> x8, starting transfers between devices: 15 us -> 8.45 us  [the longest x3 3.88 us: gather(): return lax.ppermute(x, ('gx', 'gy'), pairs)]
    ppermute x1, starting transfers between devices: 3.8 us -> 5.3 us  [body(): lax.ppermute(up, 'gz', [(i, (i + 1) % blocks) for i in range(blocks)])]
    ppermute x1, waiting for transfers between devices: 1.07 us -> 0.01 us  [body(): lax.ppermute(down, 'gz', [((i + 1) % blocks, i) for i in range(blocks)])]
  transfers between devices with their start and end apart: 4 -> 10, of which waited for: 3 -> 2; matrix products, arithmetic and copies ran while one was open for 0% -> 0% of each run, Pallas kernels for 5% -> 3%
where the time goes in v5:
time: 90.7 us; the launch traced here: 90.3 us
  blocking collectives  32.1 us (35%)
  waiting for transfers between devices  25.8 us (28%)
  Pallas kernels  17.2 us (19%)
  starting transfers between devices  13.8 us (15%)
  between operations  1.44 us (2%)
    all_to_all x1, blocking collectives, exchange(): return lax.all_to_all(x, 'gx', split_axis=0, concat_axis=0, tiled=False)  32.1 us
    ppermute x2, waiting for transfers between devices, cross(): return lax.ppermute(x, ('gx', 'gy'), pairs)  19.3 us
    ppermute x3, waiting for transfers between devices, gather(): return lax.ppermute(x, ('gx', 'gy'), pairs)  6.43 us
    pallas_call x1, Pallas kernels, paint_early(): pl.pallas_call(paint_early_kernel, out_shape=PAINTED, in_specs=[VM], out_...  6.2 us
    ppermute x1, starting transfers between devices, body(): lax.ppermute(up, 'gz', [(i, (i + 1) % blocks) for i in range(blocks)])  5.3 us
    pallas_call x1, Pallas kernels, front(): pl.pallas_call(front_kernel, out_shape=(jax.ShapeDtypeStruct((5, NROW, 12...  5.23 us
    ppermute x3, starting transfers between devices, gather(): return lax.ppermute(x, ('gx', 'gy'), pairs)  3.88 us
    pallas_call x1, Pallas kernels, finish(): pl.pallas_call(finish_kernel, out_shape=(shape, shape), in_specs=[VM] * 5...  2.34 us
  transfers between devices with their start and end apart: 10, of which 2 were waited for; matrix products, arithmetic and copies ran while one was open for 0% of the time, Pallas kernels for 3%

profile of v5, /device:TPU:1, one launch (start us, length us, event | category | flops | bytes accessed | tf_op | source)
XLA Modules:
  0.0 90.3 jit_solution(7697298780740234473)
XLA Ops:
  1.3 5.2 %front.1 = (f32[5,64,128]{2,1,0:T(8,128)S(1)}, f32[8,96,128]{2,1,0:T(8,128)}, f32[32,128]{1,0:T(8,128)S(1)}) custom-call(s32[1,1,1]{2,1,0:T(1,128)S(6)} %copy.61.count_ref, s32[64,128]{1,0:T(8,128)} %bitcast.77, f32[3,64,128]{2,1,0:T(8,128)} %bitcast.76, f32[64,128]{1,0:T(8,128)} %bitcast.78), custom_call_target="tpu_custom_call" | custom-call | flops 40000000 | bytes 1000000 | tf_op jit(solution)/shard_map/front/pallas_call | solution.py:406
  6.5 32.1 %all_to_all.18.recv_ref.face_ref = f32[8,96,128]{2,1,0:T(8,128)S(1)} all-to-all(f32[8,96,128]{2,1,0:T(8,128)} %get-tuple-element.55), channel_id=1, replica_groups=mesh['gx'=8,'gy'=16,'gz'=8] {'gx'}, dimensions={0} | all-to-all | bytes 786432 | tf_op jit(solution)/shard_map/all_to_all | solution.py:665
  38.6 6.2 %paint_early.1.acc_ref = f32[8,2,136,128]{3,2,1,0:T(8,128)S(1)} custom-call(f32[8,96,128]{2,1,0:T(8,128)S(1)} %all_to_all.18.recv_ref.face_ref), custom_call_target="tpu_custom_call" | custom-call | flops 60000000 | bytes 2000000 | tf_op jit(solution)/shard_map/paint_early/pallas_call | solution.py:300
  44.8 0.7 collective-permute-start.4
  45.5 0.7 collective-permute-start.5
  46.2 1.3 %collective-permute-start.7 = (f32[32,128]{1,0:T(8,128)S(1)}, f32[32,128]{1,0:T(8,128)S(1)}, u32[]{:S(2)}, u32[]{:S(2)}) collective-permute-start(f32[32,128]{1,0:T(8,128)S(1)} %get-tuple-element.56.one_ref), channel_id=1, source_target_pairs={{0,128},{256,384},{512,640},{768,896},{32,160},{288,416},{544,672}... | collective-permute-start | bytes 49160 | tf_op jit(solution)/shard_map/ppermute | solution.py:677
  47.5 0.0 collective-permute-done.5.two_ref
  47.5 1.3 %collective-permute-start.6 = (f32[2,32,128]{2,1,0:T(8,128)S(1)}, f32[2,32,128]{2,1,0:T(8,128)S(1)}, u32[]{:S(2)}, u32[]{:S(2)}) collective-permute-start(f32[2,32,128]{2,1,0:T(8,128)S(1)} %join.2), channel_id=1, source_target_pairs={{24,32},{280,288},{536,544},{792,800},{56,64},{312,320},{568,576},... | collective-permute-start | bytes 98312 | tf_op jit(solution)/shard_map/ppermute | solution.py:686
  48.8 0.0 collective-permute-done.7.two_ref
  48.8 0.7 collective-permute-start.8
  49.5 19.3 %collective-permute-done.6.one_ref = f32[2,32,128]{2,1,0:T(8,128)S(1)} collective-permute-done((f32[2,32,128]{2,1,0:T(8,128)S(1)}, f32[2,32,128]{2,1,0:T(8,128)S(1)}, u32[]{:S(2)}, u32[]{:S(2)}) %collective-permute-start.6) | collective-permute-done | bytes 32800 | tf_op jit(solution)/shard_map/ppermute | solution.py:686
  68.8 0.0 collective-permute-done.8.two_ref
  68.9 1.3 %collective-permute-start.11 = (f32[2,32,128]{2,1,0:T(8,128)S(1)}, f32[2,32,128]{2,1,0:T(8,128)S(1)}, u32[]{:S(2)}, u32[]{:S(2)}) collective-permute-start(f32[2,32,128]{2,1,0:T(8,128)S(1)} %either.1.refs_0_), channel_id=1, source_target_pairs={{768,0},{152,920},{800,32},{184,952},{832,64},{216,984},{864,96},{... | collective-permute-start | bytes 98312 | tf_op jit(solution)/shard_map/ppermute | solution.py:696
  70.2 1.3 %collective-permute-start.10 = (f32[2,32,128]{2,1,0:T(8,128)S(1)}, f32[2,32,128]{2,1,0:T(8,128)S(1)}, u32[]{:S(2)}, u32[]{:S(2)}) collective-permute-start(f32[2,32,128]{2,1,0:T(8,128)S(1)} %either.1.refs_0_), channel_id=1, source_target_pairs={{512,0},{408,920},{544,32},{440,952},{576,64},{472,984},{608,96},{... | collective-permute-start | bytes 98312 | tf_op jit(solution)/shard_map/ppermute | solution.py:696
  71.5 1.3 %collective-permute-start.9 = (f32[2,32,128]{2,1,0:T(8,128)S(1)}, f32[2,32,128]{2,1,0:T(8,128)S(1)}, u32[]{:S(2)}, u32[]{:S(2)}) collective-permute-start(f32[2,32,128]{2,1,0:T(8,128)S(1)} %either.1.refs_0_), channel_id=1, source_target_pairs={{256,0},{664,920},{288,32},{696,952},{320,64},{728,984},{352,96},{... | collective-permute-start | bytes 98312 | tf_op jit(solution)/shard_map/ppermute | solution.py:696
  72.8 6.4 %collective-permute-done.11.refs_3_ = f32[2,32,128]{2,1,0:T(8,128)S(1)} collective-permute-done((f32[2,32,128]{2,1,0:T(8,128)S(1)}, f32[2,32,128]{2,1,0:T(8,128)S(1)}, u32[]{:S(2)}, u32[]{:S(2)}) %collective-permute-start.11) | collective-permute-done | bytes 32800 | tf_op jit(solution)/shard_map/ppermute | solution.py:696
  79.2 0.0 collective-permute-done.10.refs_2_
  79.2 0.0 collective-permute-done.9.refs_1_
  79.2 0.0 collective-permute-done.4.in_ref
  79.2 0.3 along_z.1
  79.5 5.3 %collective-permute-start.12 = (f32[16,128]{1,0:T(8,128)S(1)}, f32[16,128]{1,0:T(8,128)S(1)}, u32[]{:S(2)}, u32[]{:S(2)}) collective-permute-start(f32[16,128]{1,0:T(8,128)S(1)} %get-tuple-element.60), channel_id=1, source_target_pairs={{0,1},{1,2},{2,3},{3,4},{4,5},{5,6},{6,7},{7,0},{8,9},{9,10},{10,1... | collective-permute-start | bytes 24584 | tf_op jit(solution)/shard_map/ppermute | solution.py:745
  84.8 0.0 collective-permute-start.13
  84.8 1.1 %tables.1 = (bf16[4,256,256]{2,1,0:T(8,128)(2,1)S(1)}, bf16[4,256,256]{2,1,0:T(8,128)(2,1)S(1)}) custom-call(), custom_call_target="tpu_custom_call" | custom-call | flops 8000000 | bytes 1000000 | tf_op jit(solution)/shard_map/tables/pallas_call | solution.py:502
  85.9 2.0 %paint_handed.3 = (f32[8,2,136,128]{3,2,1,0:T(8,128)S(1)}, s32[1]{0:T(128)S(4)}) custom-call(f32[8,32,128]{2,1,0:T(8,128)S(1)} %get-tuple-element.57.in_ref, f32[8,96,128]{2,1,0:T(8,128)S(1)} %all_to_all.18.recv_ref.face_ref, f32[8,2,136,128]{3,2,1,0:T(8,128)S(1)} %paint_late.1.refs_4_.acc_ref), custom_call_target="tpu_custom_call", output_to_operand_aliasing={{0}: (2, {})} | custom-call | flops 60000000 | bytes 2000000 | tf_op jit(solution)/shard_map/paint_handed/pallas_call | solution.py:603
  87.9 0.0 collective-permute-done.12.below_ref
  88.0 0.0 collective-permute-done.13.above_ref
  88.0 2.3 %finish.3 = (f32[2048,128]{1,0:T(8,128)}, f32[2048,128]{1,0:T(8,128)}) custom-call(f32[8,2,136,128]{3,2,1,0:T(8,128)S(1)} %get-tuple-element.59.acc_ref, f32[16,128]{1,0:T(8,128)S(1)} %collective-permute-done.12.below_ref, f32[16,128]{1,0:T(8,128)S(1)} %collective-permute-done.13.above_ref, bf16[4,256,256]{2,1,0:T(8,128)(2,1)S(1)} %get-tuple-element.62.th_ref, ...), custom_call_target="tpu_custom_call" | custom-call | flops 400000000 | bytes 4000000 | tf_op jit(solution)/shard_map/finish/pallas_call | solution.py:643
  (6 shorter events, 0.1 us)
Async XLA Ops:
  44.8 34.4 %collective-permute-start.4 = (f32[8,32,128]{2,1,0:T(8,128)S(1)}, f32[8,32,128]{2,1,0:T(8,128)S(1)}, u32[]{:S(2)}, u32[]{:S(2)}) collective-permute-start(f32[8,32,128]{2,1,0:T(8,128)S(1)} %forward_pack.1.after_ref), channel_id=1, source_target_pairs={{896,8},{8,896},{904,16},{16,904},{912,24},{24,912},{928,40},{40,9... | collective-permute-start | bytes 393224 | tf_op jit(solution)/shard_map/ppermute | solution.py:669
  45.5 2.0 %collective-permute-start.5 = (f32[32,128]{1,0:T(8,128)S(1)}, f32[32,128]{1,0:T(8,128)S(1)}, u32[]{:S(2)}, u32[]{:S(2)}) collective-permute-start(f32[32,128]{1,0:T(8,128)S(1)} %get-tuple-element.56.one_ref), channel_id=1, source_target_pairs={{152,24},{408,280},{664,536},{920,792},{184,56},{440,312},{696,568... | collective-permute-start | bytes 49160 | tf_op jit(solution)/shard_map/ppermute | solution.py:677
  46.2 2.6 %collective-permute-start.7 = (f32[32,128]{1,0:T(8,128)S(1)}, f32[32,128]{1,0:T(8,128)S(1)}, u32[]{:S(2)}, u32[]{:S(2)}) collective-permute-start(f32[32,128]{1,0:T(8,128)S(1)} %get-tuple-element.56.one_ref), channel_id=1, source_target_pairs={{0,128},{256,384},{512,640},{768,896},{32,160},{288,416},{544,672}... | collective-permute-start | bytes 49160 | tf_op jit(solution)/shard_map/ppermute | solution.py:677
  47.5 21.3 %collective-permute-start.6 = (f32[2,32,128]{2,1,0:T(8,128)S(1)}, f32[2,32,128]{2,1,0:T(8,128)S(1)}, u32[]{:S(2)}, u32[]{:S(2)}) collective-permute-start(f32[2,32,128]{2,1,0:T(8,128)S(1)} %join.2), channel_id=1, source_target_pairs={{24,32},{280,288},{536,544},{792,800},{56,64},{312,320},{568,576},... | collective-permute-start | bytes 98312 | tf_op jit(solution)/shard_map/ppermute | solution.py:686
  48.8 20.0 %collective-permute-start.8 = (f32[2,32,128]{2,1,0:T(8,128)S(1)}, f32[2,32,128]{2,1,0:T(8,128)S(1)}, u32[]{:S(2)}, u32[]{:S(2)}) collective-permute-start(f32[2,32,128]{2,1,0:T(8,128)S(1)} %join.3), channel_id=1, source_target_pairs={{160,152},{416,408},{672,664},{928,920},{192,184},{448,440},{704,6... | collective-permute-start | bytes 98312 | tf_op jit(solution)/shard_map/ppermute | solution.py:686
  68.9 10.4 %collective-permute-start.11 = (f32[2,32,128]{2,1,0:T(8,128)S(1)}, f32[2,32,128]{2,1,0:T(8,128)S(1)}, u32[]{:S(2)}, u32[]{:S(2)}) collective-permute-start(f32[2,32,128]{2,1,0:T(8,128)S(1)} %either.1.refs_0_), channel_id=1, source_target_pairs={{768,0},{152,920},{800,32},{184,952},{832,64},{216,984},{864,96},{... | collective-permute-start | bytes 98312 | tf_op jit(solution)/shard_map/ppermute | solution.py:696
  70.2 9.1 %collective-permute-start.10 = (f32[2,32,128]{2,1,0:T(8,128)S(1)}, f32[2,32,128]{2,1,0:T(8,128)S(1)}, u32[]{:S(2)}, u32[]{:S(2)}) collective-permute-start(f32[2,32,128]{2,1,0:T(8,128)S(1)} %either.1.refs_0_), channel_id=1, source_target_pairs={{512,0},{408,920},{544,32},{440,952},{576,64},{472,984},{608,96},{... | collective-permute-start | bytes 98312 | tf_op jit(solution)/shard_map/ppermute | solution.py:696
  71.5 7.8 %collective-permute-start.9 = (f32[2,32,128]{2,1,0:T(8,128)S(1)}, f32[2,32,128]{2,1,0:T(8,128)S(1)}, u32[]{:S(2)}, u32[]{:S(2)}) collective-permute-start(f32[2,32,128]{2,1,0:T(8,128)S(1)} %either.1.refs_0_), channel_id=1, source_target_pairs={{256,0},{664,920},{288,32},{696,952},{320,64},{728,984},{352,96},{... | collective-permute-start | bytes 98312 | tf_op jit(solution)/shard_map/ppermute | solution.py:696
  79.5 8.4 %collective-permute-start.12 = (f32[16,128]{1,0:T(8,128)S(1)}, f32[16,128]{1,0:T(8,128)S(1)}, u32[]{:S(2)}, u32[]{:S(2)}) collective-permute-start(f32[16,128]{1,0:T(8,128)S(1)} %get-tuple-element.60), channel_id=1, source_target_pairs={{0,1},{1,2},{2,3},{3,4},{4,5},{5,6},{6,7},{7,0},{8,9},{9,10},{10,1... | collective-permute-start | bytes 24584 | tf_op jit(solution)/shard_map/ppermute | solution.py:745
  84.8 3.1 %collective-permute-start.13 = (f32[16,128]{1,0:T(8,128)S(1)}, f32[16,128]{1,0:T(8,128)S(1)}, u32[]{:S(2)}, u32[]{:S(2)}) collective-permute-start(f32[16,128]{1,0:T(8,128)S(1)} %get-tuple-element.61), channel_id=1, source_target_pairs={{1,0},{2,1},{3,2},{4,3},{5,4},{6,5},{7,6},{0,7},{9,8},{10,9},{11,1... | collective-permute-start | bytes 24584 | tf_op jit(solution)/shard_map/ppermute | solution.py:746

commit v6 on v5

--- a/solution.py
+++ b/solution.py
@@ -253,13 +253,14 @@
     lax.fori_loop(begin // together, end // together, step, 0)
 
 
-SOME = 0
+SOME = 2
 
 
 def painted_early():
-    p, q = lax.axis_index("gx"), lax.axis_index("gy") % RING
+    p, block = lax.axis_index("gx"), lax.axis_index("gy")
+    q = block % RING
     every = ((q == 0) & (p == 0)) | ((q == RING - 1) & (p == GX - 1))
-    return jnp.where(every, GX, jnp.where((q == 0) & (p == GX - 1), SOME, 0))
+    return jnp.where(every, GX, jnp.where((q == 0) & (p == GX - 1) & (block > 0), SOME, 0))
 
 
 def paint_early_kernel(recv_ref, out_ref, val_ref):
@@ -267,7 +268,13 @@
 
 
 def paint_late_kernel(recv_ref, after_ref, acc_ref, out_ref, val_ref):
-    paint_sources(ROWS, 2, False, None, recv_ref, out_ref, val_ref, painted_early())
+    @pl.when(painted_early() == 0)
+    def _():
+        paint_sources(ROWS, 4, False, None, recv_ref, out_ref, val_ref)
+
+    @pl.when(painted_early() == SOME)
+    def _():
+        paint_sources(ROWS, 2, False, None, recv_ref, out_ref, val_ref, SOME)
 
 
 def paint_more_kernel(handed, recv_ref, acc_ref, out_ref, val_ref):
@@ -315,7 +322,7 @@
         out_shape=PAINTED,
         in_specs=[VM, ANY, VM],
         out_specs=VM,
-        scratch_shapes=paint_scratch(2),
+        scratch_shapes=paint_scratch(4),
         input_output_aliases={2: 0},
         name="paint_late",
         compiler_params=ROOM,

time: 90.7 us -> 90.7 us (level)
  transfers between devices with their start and end apart: 10 -> 10, of which waited for: 2 -> 2; matrix products, arithmetic and copies ran while one was open for 0% -> 0% of each run, Pallas kernels for 3% -> 4%
where the time goes in v6:
time: 90.7 us; the launch traced here: 90.4 us
  blocking collectives  32.1 us (35%)
  waiting for transfers between devices  25.8 us (28%)
  Pallas kernels  17.3 us (19%)
  starting transfers between devices  13.8 us (15%)
  between operations  1.44 us (2%)
    all_to_all x1, blocking collectives, exchange(): return lax.all_to_all(x, 'gx', split_axis=0, concat_axis=0, tiled=False)  32.1 us
    ppermute x2, waiting for transfers between devices, cross(): return lax.ppermute(x, ('gx', 'gy'), pairs)  19.3 us
    ppermute x3, waiting for transfers between devices, gather(): return lax.ppermute(x, ('gx', 'gy'), pairs)  6.43 us
    pallas_call x1, Pallas kernels, paint_early(): pl.pallas_call(paint_early_kernel, out_shape=PAINTED, in_specs=[VM], out_...  6.2 us
    ppermute x1, starting transfers between devices, body(): lax.ppermute(up, 'gz', [(i, (i + 1) % blocks) for i in range(blocks)])  5.3 us
    pallas_call x1, Pallas kernels, front(): pl.pallas_call(front_kernel, out_shape=(jax.ShapeDtypeStruct((5, NROW, 12...  5.23 us
    ppermute x3, starting transfers between devices, gather(): return lax.ppermute(x, ('gx', 'gy'), pairs)  3.88 us
    pallas_call x1, Pallas kernels, finish(): pl.pallas_call(finish_kernel, out_shape=(shape, shape), in_specs=[VM] * 5...  2.34 us
  transfers between devices with their start and end apart: 10, of which 2 were waited for; matrix products, arithmetic and copies ran while one was open for 0% of the time, Pallas kernels for 4%

profile of v6, /device:TPU:1, one launch (start us, length us, event | category | flops | bytes accessed | tf_op | source)
XLA Modules:
  0.0 90.4 jit_solution(11637024993120202677)
XLA Ops:
  1.3 5.2 %front.1 = (f32[5,64,128]{2,1,0:T(8,128)S(1)}, f32[8,96,128]{2,1,0:T(8,128)}, f32[32,128]{1,0:T(8,128)S(1)}) custom-call(s32[1,1,1]{2,1,0:T(1,128)S(6)} %copy.61.count_ref, s32[64,128]{1,0:T(8,128)} %bitcast.77, f32[3,64,128]{2,1,0:T(8,128)} %bitcast.76, f32[64,128]{1,0:T(8,128)} %bitcast.78), custom_call_target="tpu_custom_call" | custom-call | flops 40000000 | bytes 1000000 | tf_op jit(solution)/shard_map/front/pallas_call | solution.py:413
  6.5 32.1 %all_to_all.18.recv_ref.face_ref = f32[8,96,128]{2,1,0:T(8,128)S(1)} all-to-all(f32[8,96,128]{2,1,0:T(8,128)} %get-tuple-element.55), channel_id=1, replica_groups=mesh['gx'=8,'gy'=16,'gz'=8] {'gx'}, dimensions={0} | all-to-all | bytes 786432 | tf_op jit(solution)/shard_map/all_to_all | solution.py:672
  38.6 6.2 %paint_early.1.acc_ref = f32[8,2,136,128]{3,2,1,0:T(8,128)S(1)} custom-call(f32[8,96,128]{2,1,0:T(8,128)S(1)} %all_to_all.18.recv_ref.face_ref), custom_call_target="tpu_custom_call" | custom-call | flops 60000000 | bytes 2000000 | tf_op jit(solution)/shard_map/paint_early/pallas_call | solution.py:307
  44.8 0.7 collective-permute-start.4
  45.5 0.7 collective-permute-start.5
  46.2 1.3 %collective-permute-start.7 = (f32[32,128]{1,0:T(8,128)S(1)}, f32[32,128]{1,0:T(8,128)S(1)}, u32[]{:S(2)}, u32[]{:S(2)}) collective-permute-start(f32[32,128]{1,0:T(8,128)S(1)} %get-tuple-element.56.one_ref), channel_id=1, source_target_pairs={{0,128},{256,384},{512,640},{768,896},{32,160},{288,416},{544,672}... | collective-permute-start | bytes 49160 | tf_op jit(solution)/shard_map/ppermute | solution.py:684
  47.5 0.0 collective-permute-done.5.two_ref
  47.5 1.3 %collective-permute-start.6 = (f32[2,32,128]{2,1,0:T(8,128)S(1)}, f32[2,32,128]{2,1,0:T(8,128)S(1)}, u32[]{:S(2)}, u32[]{:S(2)}) collective-permute-start(f32[2,32,128]{2,1,0:T(8,128)S(1)} %join.2), channel_id=1, source_target_pairs={{24,32},{280,288},{536,544},{792,800},{56,64},{312,320},{568,576},... | collective-permute-start | bytes 98312 | tf_op jit(solution)/shard_map/ppermute | solution.py:693
  48.8 0.0 collective-permute-done.7.two_ref
  48.8 0.7 collective-permute-start.8
  49.5 19.3 %collective-permute-done.6.one_ref = f32[2,32,128]{2,1,0:T(8,128)S(1)} collective-permute-done((f32[2,32,128]{2,1,0:T(8,128)S(1)}, f32[2,32,128]{2,1,0:T(8,128)S(1)}, u32[]{:S(2)}, u32[]{:S(2)}) %collective-permute-start.6) | collective-permute-done | bytes 32800 | tf_op jit(solution)/shard_map/ppermute | solution.py:693
  68.8 0.0 collective-permute-done.8.two_ref
  68.9 1.3 %collective-permute-start.11 = (f32[2,32,128]{2,1,0:T(8,128)S(1)}, f32[2,32,128]{2,1,0:T(8,128)S(1)}, u32[]{:S(2)}, u32[]{:S(2)}) collective-permute-start(f32[2,32,128]{2,1,0:T(8,128)S(1)} %either.1.refs_0_), channel_id=1, source_target_pairs={{768,0},{152,920},{800,32},{184,952},{832,64},{216,984},{864,96},{... | collective-permute-start | bytes 98312 | tf_op jit(solution)/shard_map/ppermute | solution.py:703
  70.2 1.3 %collective-permute-start.10 = (f32[2,32,128]{2,1,0:T(8,128)S(1)}, f32[2,32,128]{2,1,0:T(8,128)S(1)}, u32[]{:S(2)}, u32[]{:S(2)}) collective-permute-start(f32[2,32,128]{2,1,0:T(8,128)S(1)} %either.1.refs_0_), channel_id=1, source_target_pairs={{512,0},{408,920},{544,32},{440,952},{576,64},{472,984},{608,96},{... | collective-permute-start | bytes 98312 | tf_op jit(solution)/shard_map/ppermute | solution.py:703
  71.5 1.3 %collective-permute-start.9 = (f32[2,32,128]{2,1,0:T(8,128)S(1)}, f32[2,32,128]{2,1,0:T(8,128)S(1)}, u32[]{:S(2)}, u32[]{:S(2)}) collective-permute-start(f32[2,32,128]{2,1,0:T(8,128)S(1)} %either.1.refs_0_), channel_id=1, source_target_pairs={{256,0},{664,920},{288,32},{696,952},{320,64},{728,984},{352,96},{... | collective-permute-start | bytes 98312 | tf_op jit(solution)/shard_map/ppermute | solution.py:703
  72.8 6.4 %collective-permute-done.11.refs_3_ = f32[2,32,128]{2,1,0:T(8,128)S(1)} collective-permute-done((f32[2,32,128]{2,1,0:T(8,128)S(1)}, f32[2,32,128]{2,1,0:T(8,128)S(1)}, u32[]{:S(2)}, u32[]{:S(2)}) %collective-permute-start.11) | collective-permute-done | bytes 32800 | tf_op jit(solution)/shard_map/ppermute | solution.py:703
  79.2 0.0 collective-permute-done.10.refs_2_
  79.2 0.0 collective-permute-done.9.refs_1_
  79.2 0.0 collective-permute-done.4.in_ref
  79.2 0.3 along_z.1
  79.5 5.3 %collective-permute-start.12 = (f32[16,128]{1,0:T(8,128)S(1)}, f32[16,128]{1,0:T(8,128)S(1)}, u32[]{:S(2)}, u32[]{:S(2)}) collective-permute-start(f32[16,128]{1,0:T(8,128)S(1)} %get-tuple-element.60), channel_id=1, source_target_pairs={{0,1},{1,2},{2,3},{3,4},{4,5},{5,6},{6,7},{7,0},{8,9},{9,10},{10,1... | collective-permute-start | bytes 24584 | tf_op jit(solution)/shard_map/ppermute | solution.py:752
  84.8 0.0 collective-permute-start.13
  84.8 1.1 %tables.1 = (bf16[4,256,256]{2,1,0:T(8,128)(2,1)S(1)}, bf16[4,256,256]{2,1,0:T(8,128)(2,1)S(1)}) custom-call(), custom_call_target="tpu_custom_call" | custom-call | flops 8000000 | bytes 1000000 | tf_op jit(solution)/shard_map/tables/pallas_call | solution.py:509
  85.9 2.1 %paint_handed.3 = (f32[8,2,136,128]{3,2,1,0:T(8,128)S(1)}, s32[1]{0:T(128)S(4)}) custom-call(f32[8,32,128]{2,1,0:T(8,128)S(1)} %get-tuple-element.57.in_ref, f32[8,96,128]{2,1,0:T(8,128)S(1)} %all_to_all.18.recv_ref.face_ref, f32[8,2,136,128]{3,2,1,0:T(8,128)S(1)} %paint_late.1.refs_4_.acc_ref), custom_call_target="tpu_custom_call", output_to_operand_aliasing={{0}: (2, {})} | custom-call | flops 60000000 | bytes 2000000 | tf_op jit(solution)/shard_map/paint_handed/pallas_call | solution.py:610
  88.0 0.0 collective-permute-done.12.below_ref
  88.0 0.0 collective-permute-done.13.above_ref
  88.0 2.3 %finish.3 = (f32[2048,128]{1,0:T(8,128)}, f32[2048,128]{1,0:T(8,128)}) custom-call(f32[8,2,136,128]{3,2,1,0:T(8,128)S(1)} %get-tuple-element.59.acc_ref, f32[16,128]{1,0:T(8,128)S(1)} %collective-permute-done.12.below_ref, f32[16,128]{1,0:T(8,128)S(1)} %collective-permute-done.13.above_ref, bf16[4,256,256]{2,1,0:T(8,128)(2,1)S(1)} %get-tuple-element.62.th_ref, ...), custom_call_target="tpu_custom_call" | custom-call | flops 400000000 | bytes 4000000 | tf_op jit(solution)/shard_map/finish/pallas_call | solution.py:650
  (6 shorter events, 0.1 us)
Async XLA Ops:
  44.8 34.4 %collective-permute-start.4 = (f32[8,32,128]{2,1,0:T(8,128)S(1)}, f32[8,32,128]{2,1,0:T(8,128)S(1)}, u32[]{:S(2)}, u32[]{:S(2)}) collective-permute-start(f32[8,32,128]{2,1,0:T(8,128)S(1)} %forward_pack.1.after_ref), channel_id=1, source_target_pairs={{896,8},{8,896},{904,16},{16,904},{912,24},{24,912},{928,40},{40,9... | collective-permute-start | bytes 393224 | tf_op jit(solution)/shard_map/ppermute | solution.py:676
  45.5 2.0 %collective-permute-start.5 = (f32[32,128]{1,0:T(8,128)S(1)}, f32[32,128]{1,0:T(8,128)S(1)}, u32[]{:S(2)}, u32[]{:S(2)}) collective-permute-start(f32[32,128]{1,0:T(8,128)S(1)} %get-tuple-element.56.one_ref), channel_id=1, source_target_pairs={{152,24},{408,280},{664,536},{920,792},{184,56},{440,312},{696,568... | collective-permute-start | bytes 49160 | tf_op jit(solution)/shard_map/ppermute | solution.py:684
  46.2 2.6 %collective-permute-start.7 = (f32[32,128]{1,0:T(8,128)S(1)}, f32[32,128]{1,0:T(8,128)S(1)}, u32[]{:S(2)}, u32[]{:S(2)}) collective-permute-start(f32[32,128]{1,0:T(8,128)S(1)} %get-tuple-element.56.one_ref), channel_id=1, source_target_pairs={{0,128},{256,384},{512,640},{768,896},{32,160},{288,416},{544,672}... | collective-permute-start | bytes 49160 | tf_op jit(solution)/shard_map/ppermute | solution.py:684
  47.5 21.3 %collective-permute-start.6 = (f32[2,32,128]{2,1,0:T(8,128)S(1)}, f32[2,32,128]{2,1,0:T(8,128)S(1)}, u32[]{:S(2)}, u32[]{:S(2)}) collective-permute-start(f32[2,32,128]{2,1,0:T(8,128)S(1)} %join.2), channel_id=1, source_target_pairs={{24,32},{280,288},{536,544},{792,800},{56,64},{312,320},{568,576},... | collective-permute-start | bytes 98312 | tf_op jit(solution)/shard_map/ppermute | solution.py:693
  48.8 20.0 %collective-permute-start.8 = (f32[2,32,128]{2,1,0:T(8,128)S(1)}, f32[2,32,128]{2,1,0:T(8,128)S(1)}, u32[]{:S(2)}, u32[]{:S(2)}) collective-permute-start(f32[2,32,128]{2,1,0:T(8,128)S(1)} %join.3), channel_id=1, source_target_pairs={{160,152},{416,408},{672,664},{928,920},{192,184},{448,440},{704,6... | collective-permute-start | bytes 98312 | tf_op jit(solution)/shard_map/ppermute | solution.py:693
  68.9 10.4 %collective-permute-start.11 = (f32[2,32,128]{2,1,0:T(8,128)S(1)}, f32[2,32,128]{2,1,0:T(8,128)S(1)}, u32[]{:S(2)}, u32[]{:S(2)}) collective-permute-start(f32[2,32,128]{2,1,0:T(8,128)S(1)} %either.1.refs_0_), channel_id=1, source_target_pairs={{768,0},{152,920},{800,32},{184,952},{832,64},{216,984},{864,96},{... | collective-permute-start | bytes 98312 | tf_op jit(solution)/shard_map/ppermute | solution.py:703
  70.2 9.1 %collective-permute-start.10 = (f32[2,32,128]{2,1,0:T(8,128)S(1)}, f32[2,32,128]{2,1,0:T(8,128)S(1)}, u32[]{:S(2)}, u32[]{:S(2)}) collective-permute-start(f32[2,32,128]{2,1,0:T(8,128)S(1)} %either.1.refs_0_), channel_id=1, source_target_pairs={{512,0},{408,920},{544,32},{440,952},{576,64},{472,984},{608,96},{... | collective-permute-start | bytes 98312 | tf_op jit(solution)/shard_map/ppermute | solution.py:703
  71.5 7.8 %collective-permute-start.9 = (f32[2,32,128]{2,1,0:T(8,128)S(1)}, f32[2,32,128]{2,1,0:T(8,128)S(1)}, u32[]{:S(2)}, u32[]{:S(2)}) collective-permute-start(f32[2,32,128]{2,1,0:T(8,128)S(1)} %either.1.refs_0_), channel_id=1, source_target_pairs={{256,0},{664,920},{288,32},{696,952},{320,64},{728,984},{352,96},{... | collective-permute-start | bytes 98312 | tf_op jit(solution)/shard_map/ppermute | solution.py:703
  79.5 8.5 %collective-permute-start.12 = (f32[16,128]{1,0:T(8,128)S(1)}, f32[16,128]{1,0:T(8,128)S(1)}, u32[]{:S(2)}, u32[]{:S(2)}) collective-permute-start(f32[16,128]{1,0:T(8,128)S(1)} %get-tuple-element.60), channel_id=1, source_target_pairs={{0,1},{1,2},{2,3},{3,4},{4,5},{5,6},{6,7},{7,0},{8,9},{9,10},{10,1... | collective-permute-start | bytes 24584 | tf_op jit(solution)/shard_map/ppermute | solution.py:752
  84.8 3.2 %collective-permute-start.13 = (f32[16,128]{1,0:T(8,128)S(1)}, f32[16,128]{1,0:T(8,128)S(1)}, u32[]{:S(2)}, u32[]{:S(2)}) collective-permute-start(f32[16,128]{1,0:T(8,128)S(1)} %get-tuple-element.61), channel_id=1, source_target_pairs={{1,0},{2,1},{3,2},{4,3},{5,4},{6,5},{7,6},{0,7},{9,8},{10,9},{11,1... | collective-permute-start | bytes 24584 | tf_op jit(solution)/shard_map/ppermute | solution.py:753

commit v7 on v6

--- a/solution.py
+++ b/solution.py
@@ -483,13 +483,20 @@
 
 def table_kernel(high_ref, low_ref):
     scale = 1.0 / 32.0
-    j = lax.broadcasted_iota(I32, (64, 128), 1)
-    k8 = 8 * lax.broadcasted_iota(I32, (64, 128), 0)
     none = jnp.zeros((64, 128), F32)
 
+    def waves(height, step, size):
+        j = lax.broadcasted_iota(I32, (height, 128), 1)
+        k = lax.broadcasted_iota(I32, (height, 128), 0) * step
+        angle = ((k * j) & 1023).astype(F32) * (2.0 * math.pi / 1024.0)
+        return jnp.cos(angle) * size, jnp.sin(angle) * size
+
+    many_c, many_s = waves(64, 8, scale)
+    few_c, few_s = waves(8, 1, 1.0)
+
     def turns(m):
-        angle = (((k8 + m) * j) & 1023).astype(F32) * (2.0 * math.pi / 1024.0)
-        return jnp.cos(angle) * scale, jnp.sin(angle) * scale
+        c, s = few_c[m : m + 1], few_s[m : m + 1]
+        return many_c * c - many_s * s, many_s * c + many_c * s
 
     for g, (m, w) in enumerate(((1, 7), (3, 5), (2, 6), (0, 4))):
         (c, s), (e, t) = turns(m), turns(w)

time: 90.7 us -> 90.6 us (level)
  transfers between devices with their start and end apart: 10 -> 10, of which waited for: 2 -> 3; matrix products, arithmetic and copies ran while one was open for 0% -> 0% of each run, Pallas kernels for 4% -> 3%
where the time goes in v7:
time: 90.6 us; the launch traced here: 90.2 us
  blocking collectives  32.1 us (35%)
  waiting for transfers between devices  26.3 us (29%)
  Pallas kernels  16.6 us (18%)
  starting transfers between devices  13.8 us (15%)
  between operations  1.44 us (2%)
    all_to_all x1, blocking collectives, exchange(): return lax.all_to_all(x, 'gx', split_axis=0, concat_axis=0, tiled=False)  32.1 us
    ppermute x2, waiting for transfers between devices, cross(): return lax.ppermute(x, ('gx', 'gy'), pairs)  19.3 us
    ppermute x3, waiting for transfers between devices, gather(): return lax.ppermute(x, ('gx', 'gy'), pairs)  6.43 us
    pallas_call x1, Pallas kernels, paint_early(): pl.pallas_call(paint_early_kernel, out_shape=PAINTED, in_specs=[VM], out_...  6.2 us
    ppermute x1, starting transfers between devices, body(): lax.ppermute(up, 'gz', [(i, (i + 1) % blocks) for i in range(blocks)])  5.3 us
    pallas_call x1, Pallas kernels, front(): pl.pallas_call(front_kernel, out_shape=(jax.ShapeDtypeStruct((5, NROW, 12...  5.23 us
    ppermute x3, starting transfers between devices, gather(): return lax.ppermute(x, ('gx', 'gy'), pairs)  3.88 us
    pallas_call x1, Pallas kernels, finish(): pl.pallas_call(finish_kernel, out_shape=(shape, shape), in_specs=[VM] * 5...  2.34 us
  transfers between devices with their start and end apart: 10, of which 3 were waited for; matrix products, arithmetic and copies ran while one was open for 0% of the time, Pallas kernels for 3%

profile of v7, /device:TPU:1, one launch (start us, length us, event | category | flops | bytes accessed | tf_op | source)
XLA Modules:
  0.0 90.2 jit_solution(17483739794592202091)
XLA Ops:
  1.3 5.2 %front.1 = (f32[5,64,128]{2,1,0:T(8,128)S(1)}, f32[8,96,128]{2,1,0:T(8,128)}, f32[32,128]{1,0:T(8,128)S(1)}) custom-call(s32[1,1,1]{2,1,0:T(1,128)S(6)} %copy.61.count_ref, s32[64,128]{1,0:T(8,128)} %bitcast.77, f32[3,64,128]{2,1,0:T(8,128)} %bitcast.76, f32[64,128]{1,0:T(8,128)} %bitcast.78), custom_call_target="tpu_custom_call" | custom-call | flops 40000000 | bytes 1000000 | tf_op jit(solution)/shard_map/front/pallas_call | solution.py:413
  6.5 32.1 %all_to_all.18.recv_ref.face_ref = f32[8,96,128]{2,1,0:T(8,128)S(1)} all-to-all(f32[8,96,128]{2,1,0:T(8,128)} %get-tuple-element.55), channel_id=1, replica_groups=mesh['gx'=8,'gy'=16,'gz'=8] {'gx'}, dimensions={0} | all-to-all | bytes 786432 | tf_op jit(solution)/shard_map/all_to_all | solution.py:679
  38.6 6.2 %paint_early.1.acc_ref = f32[8,2,136,128]{3,2,1,0:T(8,128)S(1)} custom-call(f32[8,96,128]{2,1,0:T(8,128)S(1)} %all_to_all.18.recv_ref.face_ref), custom_call_target="tpu_custom_call" | custom-call | flops 60000000 | bytes 2000000 | tf_op jit(solution)/shard_map/paint_early/pallas_call | solution.py:307
  44.8 0.7 collective-permute-start.4
  45.5 0.7 collective-permute-start.5
  46.2 1.3 %collective-permute-start.7 = (f32[32,128]{1,0:T(8,128)S(1)}, f32[32,128]{1,0:T(8,128)S(1)}, u32[]{:S(2)}, u32[]{:S(2)}) collective-permute-start(f32[32,128]{1,0:T(8,128)S(1)} %get-tuple-element.56.one_ref), channel_id=1, source_target_pairs={{0,128},{256,384},{512,640},{768,896},{32,160},{288,416},{544,672}... | collective-permute-start | bytes 49160 | tf_op jit(solution)/shard_map/ppermute | solution.py:691
  47.5 0.0 collective-permute-done.5.two_ref
  47.5 1.3 %collective-permute-start.6 = (f32[2,32,128]{2,1,0:T(8,128)S(1)}, f32[2,32,128]{2,1,0:T(8,128)S(1)}, u32[]{:S(2)}, u32[]{:S(2)}) collective-permute-start(f32[2,32,128]{2,1,0:T(8,128)S(1)} %join.2), channel_id=1, source_target_pairs={{24,32},{280,288},{536,544},{792,800},{56,64},{312,320},{568,576},... | collective-permute-start | bytes 98312 | tf_op jit(solution)/shard_map/ppermute | solution.py:700
  48.8 0.0 collective-permute-done.7.two_ref
  48.8 0.7 collective-permute-start.8
  49.5 19.3 %collective-permute-done.6.one_ref = f32[2,32,128]{2,1,0:T(8,128)S(1)} collective-permute-done((f32[2,32,128]{2,1,0:T(8,128)S(1)}, f32[2,32,128]{2,1,0:T(8,128)S(1)}, u32[]{:S(2)}, u32[]{:S(2)}) %collective-permute-start.6) | collective-permute-done | bytes 32800 | tf_op jit(solution)/shard_map/ppermute | solution.py:700
  68.8 0.0 collective-permute-done.8.two_ref
  68.9 1.3 %collective-permute-start.11 = (f32[2,32,128]{2,1,0:T(8,128)S(1)}, f32[2,32,128]{2,1,0:T(8,128)S(1)}, u32[]{:S(2)}, u32[]{:S(2)}) collective-permute-start(f32[2,32,128]{2,1,0:T(8,128)S(1)} %either.1.refs_0_), channel_id=1, source_target_pairs={{768,0},{152,920},{800,32},{184,952},{832,64},{216,984},{864,96},{... | collective-permute-start | bytes 98312 | tf_op jit(solution)/shard_map/ppermute | solution.py:710
  70.2 1.3 %collective-permute-start.10 = (f32[2,32,128]{2,1,0:T(8,128)S(1)}, f32[2,32,128]{2,1,0:T(8,128)S(1)}, u32[]{:S(2)}, u32[]{:S(2)}) collective-permute-start(f32[2,32,128]{2,1,0:T(8,128)S(1)} %either.1.refs_0_), channel_id=1, source_target_pairs={{512,0},{408,920},{544,32},{440,952},{576,64},{472,984},{608,96},{... | collective-permute-start | bytes 98312 | tf_op jit(solution)/shard_map/ppermute | solution.py:710
  71.5 1.3 %collective-permute-start.9 = (f32[2,32,128]{2,1,0:T(8,128)S(1)}, f32[2,32,128]{2,1,0:T(8,128)S(1)}, u32[]{:S(2)}, u32[]{:S(2)}) collective-permute-start(f32[2,32,128]{2,1,0:T(8,128)S(1)} %either.1.refs_0_), channel_id=1, source_target_pairs={{256,0},{664,920},{288,32},{696,952},{320,64},{728,984},{352,96},{... | collective-permute-start | bytes 98312 | tf_op jit(solution)/shard_map/ppermute | solution.py:710
  72.8 6.4 %collective-permute-done.11.refs_3_ = f32[2,32,128]{2,1,0:T(8,128)S(1)} collective-permute-done((f32[2,32,128]{2,1,0:T(8,128)S(1)}, f32[2,32,128]{2,1,0:T(8,128)S(1)}, u32[]{:S(2)}, u32[]{:S(2)}) %collective-permute-start.11) | collective-permute-done | bytes 32800 | tf_op jit(solution)/shard_map/ppermute | solution.py:710
  79.2 0.0 collective-permute-done.10.refs_2_
  79.2 0.0 collective-permute-done.9.refs_1_
  79.2 0.0 collective-permute-done.4.in_ref
  79.2 0.3 along_z.1
  79.5 5.3 %collective-permute-start.12 = (f32[16,128]{1,0:T(8,128)S(1)}, f32[16,128]{1,0:T(8,128)S(1)}, u32[]{:S(2)}, u32[]{:S(2)}) collective-permute-start(f32[16,128]{1,0:T(8,128)S(1)} %get-tuple-element.60), channel_id=1, source_target_pairs={{0,1},{1,2},{2,3},{3,4},{4,5},{5,6},{6,7},{7,0},{8,9},{9,10},{10,1... | collective-permute-start | bytes 24584 | tf_op jit(solution)/shard_map/ppermute | solution.py:759
  84.8 0.0 collective-permute-start.13
  84.8 0.3 tables.1
  85.2 2.2 %paint_handed.3 = (f32[8,2,136,128]{3,2,1,0:T(8,128)S(1)}, s32[1]{0:T(128)S(4)}) custom-call(f32[8,32,128]{2,1,0:T(8,128)S(1)} %get-tuple-element.57.in_ref, f32[8,96,128]{2,1,0:T(8,128)S(1)} %all_to_all.18.recv_ref.face_ref, f32[8,2,136,128]{3,2,1,0:T(8,128)S(1)} %paint_late.1.refs_4_.acc_ref), custom_call_target="tpu_custom_call", output_to_operand_aliasing={{0}: (2, {})} | custom-call | flops 60000000 | bytes 2000000 | tf_op jit(solution)/shard_map/paint_handed/pallas_call | solution.py:617
  87.3 0.0 collective-permute-done.12.below_ref
  87.3 0.6 collective-permute-done.13.above_ref
  87.9 2.3 %finish.3 = (f32[2048,128]{1,0:T(8,128)}, f32[2048,128]{1,0:T(8,128)}) custom-call(f32[8,2,136,128]{3,2,1,0:T(8,128)S(1)} %get-tuple-element.59.acc_ref, f32[16,128]{1,0:T(8,128)S(1)} %collective-permute-done.12.below_ref, f32[16,128]{1,0:T(8,128)S(1)} %collective-permute-done.13.above_ref, bf16[4,256,256]{2,1,0:T(8,128)(2,1)S(1)} %get-tuple-element.62.th_ref, ...), custom_call_target="tpu_custom_call" | custom-call | flops 400000000 | bytes 4000000 | tf_op jit(solution)/shard_map/finish/pallas_call | solution.py:657
  (6 shorter events, 0.1 us)
Async XLA Ops:
  44.8 34.4 %collective-permute-start.4 = (f32[8,32,128]{2,1,0:T(8,128)S(1)}, f32[8,32,128]{2,1,0:T(8,128)S(1)}, u32[]{:S(2)}, u32[]{:S(2)}) collective-permute-start(f32[8,32,128]{2,1,0:T(8,128)S(1)} %forward_pack.1.after_ref), channel_id=1, source_target_pairs={{896,8},{8,896},{904,16},{16,904},{912,24},{24,912},{928,40},{40,9... | collective-permute-start | bytes 393224 | tf_op jit(solution)/shard_map/ppermute | solution.py:683
  45.5 2.0 %collective-permute-start.5 = (f32[32,128]{1,0:T(8,128)S(1)}, f32[32,128]{1,0:T(8,128)S(1)}, u32[]{:S(2)}, u32[]{:S(2)}) collective-permute-start(f32[32,128]{1,0:T(8,128)S(1)} %get-tuple-element.56.one_ref), channel_id=1, source_target_pairs={{152,24},{408,280},{664,536},{920,792},{184,56},{440,312},{696,568... | collective-permute-start | bytes 49160 | tf_op jit(solution)/shard_map/ppermute | solution.py:691
  46.2 2.6 %collective-permute-start.7 = (f32[32,128]{1,0:T(8,128)S(1)}, f32[32,128]{1,0:T(8,128)S(1)}, u32[]{:S(2)}, u32[]{:S(2)}) collective-permute-start(f32[32,128]{1,0:T(8,128)S(1)} %get-tuple-element.56.one_ref), channel_id=1, source_target_pairs={{0,128},{256,384},{512,640},{768,896},{32,160},{288,416},{544,672}... | collective-permute-start | bytes 49160 | tf_op jit(solution)/shard_map/ppermute | solution.py:691
  47.5 21.3 %collective-permute-start.6 = (f32[2,32,128]{2,1,0:T(8,128)S(1)}, f32[2,32,128]{2,1,0:T(8,128)S(1)}, u32[]{:S(2)}, u32[]{:S(2)}) collective-permute-start(f32[2,32,128]{2,1,0:T(8,128)S(1)} %join.2), channel_id=1, source_target_pairs={{24,32},{280,288},{536,544},{792,800},{56,64},{312,320},{568,576},... | collective-permute-start | bytes 98312 | tf_op jit(solution)/shard_map/ppermute | solution.py:700
  48.8 20.0 %collective-permute-start.8 = (f32[2,32,128]{2,1,0:T(8,128)S(1)}, f32[2,32,128]{2,1,0:T(8,128)S(1)}, u32[]{:S(2)}, u32[]{:S(2)}) collective-permute-start(f32[2,32,128]{2,1,0:T(8,128)S(1)} %join.3), channel_id=1, source_target_pairs={{160,152},{416,408},{672,664},{928,920},{192,184},{448,440},{704,6... | collective-permute-start | bytes 98312 | tf_op jit(solution)/shard_map/ppermute | solution.py:700
  68.9 10.4 %collective-permute-start.11 = (f32[2,32,128]{2,1,0:T(8,128)S(1)}, f32[2,32,128]{2,1,0:T(8,128)S(1)}, u32[]{:S(2)}, u32[]{:S(2)}) collective-permute-start(f32[2,32,128]{2,1,0:T(8,128)S(1)} %either.1.refs_0_), channel_id=1, source_target_pairs={{768,0},{152,920},{800,32},{184,952},{832,64},{216,984},{864,96},{... | collective-permute-start | bytes 98312 | tf_op jit(solution)/shard_map/ppermute | solution.py:710
  70.2 9.1 %collective-permute-start.10 = (f32[2,32,128]{2,1,0:T(8,128)S(1)}, f32[2,32,128]{2,1,0:T(8,128)S(1)}, u32[]{:S(2)}, u32[]{:S(2)}) collective-permute-start(f32[2,32,128]{2,1,0:T(8,128)S(1)} %either.1.refs_0_), channel_id=1, source_target_pairs={{512,0},{408,920},{544,32},{440,952},{576,64},{472,984},{608,96},{... | collective-permute-start | bytes 98312 | tf_op jit(solution)/shard_map/ppermute | solution.py:710
  71.5 7.8 %collective-permute-start.9 = (f32[2,32,128]{2,1,0:T(8,128)S(1)}, f32[2,32,128]{2,1,0:T(8,128)S(1)}, u32[]{:S(2)}, u32[]{:S(2)}) collective-permute-start(f32[2,32,128]{2,1,0:T(8,128)S(1)} %either.1.refs_0_), channel_id=1, source_target_pairs={{256,0},{664,920},{288,32},{696,952},{320,64},{728,984},{352,96},{... | collective-permute-start | bytes 98312 | tf_op jit(solution)/shard_map/ppermute | solution.py:710
  79.5 7.8 %collective-permute-start.12 = (f32[16,128]{1,0:T(8,128)S(1)}, f32[16,128]{1,0:T(8,128)S(1)}, u32[]{:S(2)}, u32[]{:S(2)}) collective-permute-start(f32[16,128]{1,0:T(8,128)S(1)} %get-tuple-element.60), channel_id=1, source_target_pairs={{0,1},{1,2},{2,3},{3,4},{4,5},{5,6},{6,7},{7,0},{8,9},{9,10},{10,1... | collective-permute-start | bytes 24584 | tf_op jit(solution)/shard_map/ppermute | solution.py:759
  84.8 3.1 %collective-permute-start.13 = (f32[16,128]{1,0:T(8,128)S(1)}, f32[16,128]{1,0:T(8,128)S(1)}, u32[]{:S(2)}, u32[]{:S(2)}) collective-permute-start(f32[16,128]{1,0:T(8,128)S(1)} %get-tuple-element.61), channel_id=1, source_target_pairs={{1,0},{2,1},{3,2},{4,3},{5,4},{6,5},{7,6},{0,7},{9,8},{10,9},{11,1... | collective-permute-start | bytes 24584 | tf_op jit(solution)/shard_map/ppermute | solution.py:760
